TPU v7x, 32 devices: a whole 2x2x4 slice. The times are simulated.
32 devices in a mesh: limb: 4 (over z), coef: 8 (over y, x, core).
Axes of the slice: x: 2, y: 2, z: 4, core: 2. Of those that a mesh axis runs over, the one named last changes fastest.
Arguments:
- residues: float32 [16, 64, 65536], P('limb', None, 'coef'), may hold values from 0 to 65534, as said below
- levels: int32 [64], replicated, may hold values from 1 to 16
- moduli: int32 [24], replicated, may hold values from 32768 to 65535, as said below
- inverse_table: int32 [16, 16], replicated, may hold values from 1 to 65534, as said below
- cross_table: int32 [16, 16, 8], replicated, may hold values from 0 to 65534, as said below
Outputs:
- source_part: float32 [16, 64, 65536], P('limb', 'coef')
- special_part: float32 [8, 64, 65536], P('limb', 'coef')
Inputs may be any that keep to these rules, and one draw needn't show every extreme that they name: `moduli`: distinct primes; the first 16 form the source basis, the last 8 the special basis. `inverse_table`: entry [l, i] lies below the source modulus q_i. `cross_table`: entry [l, i, j] lies below the special modulus p_j. `residues`: whole numbers; entry [i, n, k] lies below the source modulus q_i.
All inputs are finite; a program needn't handle non-finite values.
Results may differ from a plain program's by a relative error of at most 0.0003.
Values may be sent and summed in bfloat16 or wider, within the bound.
No kernel may reach another device: no remote copies, remote signals or barrier semaphores. Data moves between devices by JAX's collectives and lax.ppermute only.
A program may use at most 192 MiB of HBM per device.

v0:
```python
import jax
import jax.numpy as jnp
from jax import lax
from jax.sharding import PartitionSpec as P


def modulo(amount, modulus):
    quotient = jnp.floor(amount / modulus)
    remain = amount - quotient * modulus
    remain = jnp.where(remain < 0, remain + modulus, remain)
    return jnp.where(remain >= modulus, remain - modulus, remain)


def split_bytes(amount):
    high_byte = jnp.floor(amount / 256.0)
    return (amount - 256.0 * high_byte, high_byte)


def level_tables(levels, inverse_table, cross_table):
    limb_total = inverse_table.shape[0]
    positions = jnp.arange(limb_total, dtype=jnp.int32)
    onehot = (levels[:, None] - 1 == positions[None, :]).astype(jnp.float32)
    inverse_rows = jnp.dot(
        onehot, inverse_table.astype(jnp.float32), precision=lax.Precision.HIGHEST
    )
    cross_rows = jnp.einsum(
        "nl,lij->nij", onehot, cross_table.astype(jnp.float32), precision=lax.Precision.HIGHEST
    )
    active = (positions[None, :] < levels[:, None]).astype(jnp.float32)
    return (inverse_rows, cross_rows, active)


def scale_limbs(values, inverse_rows, active, source_mod):
    low_byte, high_byte = split_bytes(inverse_rows)
    modulus = source_mod[:, None, None]
    upper_part = modulo(values * high_byte[:, :, None], modulus)
    lower_part = modulo(values * low_byte[:, :, None], modulus)
    joined = modulo(modulo(256.0 * upper_part, modulus) + lower_part, modulus)
    return joined * active[:, :, None]


def fold_bytes(cross_rows, target_mod):
    modulus = target_mod[None, None, :]
    folded = jnp.stack([modulo(cross_rows, modulus), modulo(256.0 * cross_rows, modulus)], axis=3)
    low_byte, high_byte = split_bytes(folded)
    stacked = jnp.stack([low_byte, high_byte], axis=3)
    return jnp.transpose(stacked, (0, 2, 3, 1, 4)).astype(jnp.bfloat16)


def reduce_targets(digit_sums, modulus_row):
    modulus = modulus_row[:, None, None]
    upper_part = modulo(256.0 * modulo(digit_sums[:, 1], modulus), modulus)
    return modulo(upper_part + modulo(digit_sums[:, 0], modulus), modulus)


def per_device(residues, levels, moduli, inverse_table, cross_table):
    source_count = inverse_table.shape[0]
    local_limbs = residues.shape[0]
    target_count = cross_table.shape[2]
    group_count = lax.axis_size("limb")
    local_targets = target_count // group_count
    group_index = lax.axis_index("limb")
    module = moduli.astype(jnp.float32)
    inverse_rows, cross_rows, active = level_tables(levels, inverse_table, cross_table)
    limb_start = group_index * local_limbs
    target_start = group_index * local_targets
    source_mod = lax.dynamic_slice_in_dim(module, limb_start, local_limbs, 0)
    target_mod = module[source_count:]
    own_mod = lax.dynamic_slice_in_dim(target_mod, target_start, local_targets, 0)
    own_inverse = lax.dynamic_slice_in_dim(inverse_rows, limb_start, local_limbs, 1).T
    own_active = lax.dynamic_slice_in_dim(active, limb_start, local_limbs, 1).T
    normalized = residues * own_active[:, :, None] / source_mod[:, None, None]
    scaled = scale_limbs(residues, own_inverse, own_active, source_mod)
    low_byte, high_byte = split_bytes(scaled)
    digits = jnp.stack([low_byte, high_byte], axis=1).astype(jnp.bfloat16)
    own_cross = lax.dynamic_slice_in_dim(cross_rows, limb_start, local_limbs, 1)
    weights = fold_bytes(own_cross, target_mod)
    digit_sums = jnp.einsum("lank,njbla->jbnk", digits, weights, preferred_element_type=jnp.float32)
    summed = lax.psum_scatter(
        reduce_targets(digit_sums, target_mod), "limb", scatter_dimension=0, tiled=True
    )
    converted = modulo(summed, own_mod[:, None, None])
    result = converted / own_mod[:, None, None]
    source_blocks, target_blocks = (
        lax.all_to_all(normalized, "coef", split_axis=1, concat_axis=2, tiled=True),
        lax.all_to_all(result, "coef", split_axis=1, concat_axis=2, tiled=True),
    )
    return (source_blocks, target_blocks)


def solution(mesh):
    placed = (P("limb", None, "coef"), P(), P(), P(), P())
    return jax.shard_map(
        per_device,
        mesh=mesh,
        in_specs=placed,
        out_specs=(P("limb", "coef", None), P("limb", "coef", None)),
        check_vma=False,
    )
```

profile of v0, /device:TPU:0, one launch (start us, length us, event | category | flops | bytes accessed | tf_op | source)
XLA Modules:
  0.0 464.6 jit_solution(2813836809831612075)
XLA Ops:
  7.2 0.0 reduce-scatter.2.cloned.1.call-start
  7.2 0.7 convert_element_type.19
  7.9 0.1 slice.9
  7.9 0.1 dynamic_slice.16
  8.0 0.7 broadcast_add_fusion
  8.7 0.7 convert_bitcast_fusion
  9.4 0.9 fusion.16
  10.3 0.1 copy.32
  10.4 0.1 copy.34
  10.5 0.8 convert_element_type.20
  11.4 0.2 fusion.11
  11.6 0.1 fusion.14
  11.8 0.3 copy.37
  12.0 33.8 %fusion.9 = (bf16[4,1,64,8192]{3,0,1,2:T(4,128)(2,1)S(1)}, f32[4,64,8192]{2,0,1:T(4,128)S(1)}, f32[4,64,8192]{2,0,1:T(4,128)}) fusion(f32[4,64]{0,1:T(8,128)S(1)} %convert_bitcast_fusion, f32[4,64]{0,1:T(8,128)S(1)} %copy.34, f32[4]{0:T(128)S(1)} %dynamic_slice.16, f32[4,64]{0,1:T(8,128)S(1)} %copy.32, f32[4,64,8192]{2,1,0:T(8,128)} %param.5), kind=kLoop, calls=%fused_computation.34 | loop fusion | flops 109051904 | bytes 29363216 | tf_op jit(solution)/shard_map/stack | solution.py:75
  45.9 4.3 fusion.8
  50.2 14.6 %convolution_bitcast_fusion = f32[8,2,64,8192]{3,0,1,2:T(8,128)} fusion(bf16[64,8,2,4,2]{1,3,4,2,0:T(4,128)(2,1)S(1)} %copy.37, bf16[4,1,64,8192]{3,0,1,2:T(4,128)(2,1)} %fusion.8, bf16[4,1,64,8192]{3,0,1,2:T(4,128)(2,1)S(1)} %get-tuple-element.2), kind=kOutput, calls=%fused_computation.16 | convolution fusion | flops 150994944 | bytes 41959424 | tf_op jit(solution)/shard_map/lank,njbla->jbnk/dot_general | solution.py:78
  64.8 25.8 %compare_select_fusion = f32[8,64,8192]{2,0,1:T(8,128)S(1)} fusion(f32[8,2,64,8192]{3,0,1,2:T(8,128)} %convolution_bitcast_fusion, f32[8]{0:T(128)S(1)} %slice.9), kind=kLoop, calls=%fused_computation | loop fusion | flops 176160768 | bytes 50331680 | tf_op jit(solution)/shard_map/jit(_where)/select_n | solution.py:11
  90.6 15.0 %copy.39 = f32[8,64,8192]{2,1,0:T(8,128)} copy(f32[8,64,8192]{2,0,1:T(8,128)S(1)} %compare_select_fusion) | data formatting | bytes 33554432 | tf_op jit(solution)/shard_map/jit(_where)/select_n | solution.py:11
  105.6 0.0 reduce-scatter.2.cloned.1.call-update
  105.7 5.2 %all-to-all-start = ((f32[4,64,8192]{2,0,1:T(4,128)}), f32[4,64,8192]{2,0,1:T(4,128)}, u32[]{:S(2)}, u32[]{:S(2)}) async-start(f32[4,64,8192]{2,0,1:T(4,128)} %get-tuple-element.4), calls=%async_computation | async-start | bytes 16777216 | tf_op jit(solution)/shard_map/all_to_all | solution.py:85
  110.9 0.1 dynamic_slice.19
  110.9 278.0 %reduce-scatter.2.cloned.1.call-done = f32[2,64,8192]{2,1,0:T(8,128)} async-done(((f32[8,64,8192]{2,1,0:T(8,128)}), f32[2,64,8192]{2,1,0:T(8,128)}) %reduce-scatter.2.cloned.1.call-update) | async-done | bytes 4194320 | tf_op jit(solution)/shard_map/reduce_scatter | solution.py:79
  389.0 3.3 fusion.10
  392.2 5.2 %copy.40 = f32[2,64,8192]{2,0,1:T(2,128)} copy(f32[2,64,8192]{2,1,0:T(8,128)S(1)} %fusion.10) | data formatting | bytes 8388608 | tf_op jit(solution)/shard_map/div | solution.py:83
  397.5 0.0 all-to-all-done
  397.5 4.6 all-to-all-start.1
  402.1 11.6 %copy.30 = f32[4,8,8,8192]{3,1,2,0:T(8,128)} copy(f32[4,8,8,8192]{3,0,1,2:T(4,128)} %bitcast.2) | data formatting | bytes 16777216 | tf_op jit(solution)/shard_map/all_to_all | solution.py:85
  413.7 37.5 %all-to-all-done.1 = f32[2,64,8192]{2,0,1:T(2,128)} async-done(((f32[2,64,8192]{2,0,1:T(2,128)}), f32[2,64,8192]{2,0,1:T(2,128)}, u32[]{:S(2)}, u32[]{:S(2)}) %all-to-all-start.1) | async-done | bytes 4194336 | tf_op jit(solution)/shard_map/all_to_all | solution.py:86
  451.2 6.6 %copy.41 = f32[2,8,8,8192]{3,1,2,0:T(8,128)} copy(f32[2,8,8,8192]{3,0,1,2:T(2,128)} %bitcast.21) | data formatting | bytes 8388608 | tf_op jit(solution)/shard_map/all_to_all | solution.py:86
  (3 shorter events, 0.1 us)
Async XLA Ops:
  7.2 381.8 %reduce-scatter.2.cloned.1.call-start = ((), (), s32[]{:S(2)}) async-start(), calls=%async_computation.3 | async-start | bytes 20971520 | tf_op jit(solution)/shard_map/reduce_scatter | solution.py:79
  105.7 291.8 %all-to-all-start = ((f32[4,64,8192]{2,0,1:T(4,128)}), f32[4,64,8192]{2,0,1:T(4,128)}, u32[]{:S(2)}, u32[]{:S(2)}) async-start(f32[4,64,8192]{2,0,1:T(4,128)} %get-tuple-element.4), calls=%async_computation | async-start | bytes 16777216 | tf_op jit(solution)/shard_map/all_to_all | solution.py:85
  397.5 53.7 %all-to-all-start.1 = ((f32[2,64,8192]{2,0,1:T(2,128)}), f32[2,64,8192]{2,0,1:T(2,128)}, u32[]{:S(2)}, u32[]{:S(2)}) async-start(f32[2,64,8192]{2,0,1:T(2,128)} %copy.40), calls=%async_computation.2 | async-start | bytes 8388608 | tf_op jit(solution)/shard_map/all_to_all | solution.py:86
Sparse Core Ops, SparseCore 0:
  105.8 283.1 reduce-scatter.1
where the time goes:
time: 465 us
  waiting for transfers between devices  316 us (68%)
  other arithmetic  70.2 us (15%)
  local copies, waits for them, and re-layouts  39.2 us (8%)
  matrix products  15.8 us (3%)
  between operations  14.1 us (3%)
  starting transfers between devices  9.81 us (2%)
    reduce_scatter x1, waiting for transfers between devices, per_device(): lax.psum_scatter(reduce_targets(digit_sums, target_mod), 'limb', scatter_...  278 us
    another operation x2, other arithmetic, per_device(): digits = jnp.stack([low_byte, high_byte], axis=1).astype(jnp.bfloat16)  38.1 us
    all_to_all x1, waiting for transfers between devices, per_device(): lax.all_to_all(result, 'coef', split_axis=1, concat_axis=2, tiled=True)  37.5 us
    select_n x1, other arithmetic, modulo(): return jnp.where(remain >= modulus, remain - modulus, remain)  25.8 us
    select_n x1, local copies, waits for them, and re-layouts, modulo(): return jnp.where(remain >= modulus, remain - modulus, remain)  15 us
    dot_general x1, matrix products, per_device(): jnp.einsum('lank,njbla->jbnk', digits, weights, preferred_element_type=jn...  14.6 us
    all_to_all x1, local copies, waits for them, and re-layouts, per_device(): lax.all_to_all(normalized, 'coef', split_axis=1, concat_axis=2, tiled=True)  11.6 us
  transfers between devices with their start and end apart: 3, of which 2 were waited for; matrix products, arithmetic and copies ran while one was open for 4% of the time, Pallas kernels for 0%

commit v1 on v0

v1 whole, which is shorter than its diff:
```python
import functools

import jax
import jax.numpy as jnp
from jax import lax
from jax.experimental import pallas as pl
from jax.experimental.pallas import tpu as pltpu
from jax.sharding import PartitionSpec as P

LANES = 128
MIB = 1024 * 1024
HERE = pl.BlockSpec(memory_space=pltpu.VMEM)
FAR = pl.BlockSpec(memory_space=pl.ANY)
SCALARS = pl.BlockSpec(memory_space=pltpu.SMEM)


def log2(number):
    assert number & (number - 1) == 0
    return number.bit_length() - 1


def pack_pair(first, second):
    return first | lax.shift_left(second, 16)


def halves(word):
    return word & 0xFFFF, lax.shift_right_logical(word, 16)


def centred(amount, modulus, inverse):
    return amount - jnp.round(amount * inverse) * modulus


def residue(amount, modulus, inverse):
    remain = centred(amount, modulus, inverse)
    return jnp.where(remain < 0, remain + modulus, remain)


def join_residues(first, second, modulus):
    total = first + second
    less = total - modulus
    return jnp.where(less < 0, total, less)


def spread(column, width):
    return jnp.concatenate([column] * (width // LANES), axis=1)


def params(limit):
    return pltpu.CompilerParams(vmem_limit_bytes=limit * MIB)


def cost(elements, ops, moved):
    return pl.CostEstimate(flops=elements * ops, bytes_accessed=moved, transcendentals=0)


def loop(count, body):
    lax.fori_loop(0, count, lambda step, carry: (body(step), carry)[1], 0)


def span_of(step, tile):
    return pl.ds(pl.multiple_of(step * tile, tile), tile)


def constants(limit):
    return lambda number: jnp.full(limit, number, jnp.int32).astype(jnp.float32)


def build_tables(place, levels, moduli, inverse, cross, columns, targets, weights):
    group, home = place[0], place[1]
    limbs, block = columns.shape[1], columns.shape[2]
    source_count = inverse.shape[0]
    total = targets.shape[1]
    quarter = total // 4
    shape = (block, LANES)
    fill = constants(shape)
    row = lax.broadcasted_iota(jnp.int32, shape, 0)
    own_levels = [levels[home * block + n] for n in range(block)]
    for limb in range(limbs):
        index = group * limbs + limb
        picked = jnp.zeros(shape, jnp.int32)
        live = jnp.zeros(shape, jnp.int32)
        for n, level in enumerate(own_levels):
            active = jnp.where(index < level, 1, 0)
            picked = jnp.where(row == n, inverse[level - 1, index] * active, picked)
            live = jnp.where(row == n, active, live)
        picked = picked.astype(jnp.float32)
        high = jnp.floor((picked + 128.0) * (1.0 / 256.0))
        modulus = fill(moduli[index])
        columns[0, limb] = high
        columns[1, limb] = picked - 256.0 * high
        columns[2, limb] = live.astype(jnp.float32) / modulus
        columns[3, limb] = modulus
        columns[4, limb] = 1.0 / modulus

    left = group < 2
    inner = (group == 1) | (group == 2)
    order = (jnp.where(left, 2, 1), jnp.where(left, 3, 0), group ^ 1, group)
    entries = cross.shape[1]
    lane = lax.broadcasted_iota(jnp.int32, (block, source_count), 1)
    rank = lax.broadcasted_iota(jnp.int32, (block, source_count), 0)
    level_rank = jnp.zeros((block, source_count), jnp.int32)
    for n, level in enumerate(own_levels):
        level_rank = jnp.where(rank == n, level - 1, level_rank)
    onehot = jnp.where(lane == level_rank, 1.0, 0.0).astype(jnp.bfloat16)
    table = cross[...]
    low = (table & 0xFF).astype(jnp.float32).astype(jnp.bfloat16)
    high = lax.shift_right_logical(table, 8).astype(jnp.float32).astype(jnp.bfloat16)
    low = jnp.dot(onehot, low, preferred_element_type=jnp.float32)
    high = jnp.dot(onehot, high, preferred_element_type=jnp.float32)
    target_of = lax.broadcasted_iota(jnp.int32, (block, entries), 1) & (total - 1)
    rows = []
    for target in range(total):
        index = order[target // quarter] * quarter + target % quarter
        for part in (low, high):
            rows.append(jnp.where(target_of == index, part, 0.0))
    width = weights.shape[1]
    entry = lax.broadcasted_iota(jnp.int32, (entries, width), 0)
    column = lax.broadcasted_iota(jnp.int32, (entries, width), 1)
    received = lax.shift_right_logical(column, log2(2 * block * limbs))
    limb = lax.shift_right_logical(column, log2(2 * block)) & (limbs - 1)
    limb = limb + jnp.where(received == 0, group * limbs, (group ^ 1) * limbs)
    choose = jnp.where(lax.shift_right_logical(entry, log2(total)) == limb, 1.0, 0.0).astype(jnp.bfloat16)
    stacked = jnp.concatenate(rows, axis=0).astype(jnp.bfloat16)
    chosen = jnp.dot(stacked, choose, preferred_element_type=jnp.float32)
    column = lax.broadcasted_iota(jnp.int32, (block, width), 1)
    same = (column & (block - 1)) == lax.broadcasted_iota(jnp.int32, (block, width), 0)
    upper = (lax.shift_right_logical(column, log2(block)) & 1) == 1
    from_outer = lax.shift_right_logical(column, log2(2 * block * limbs)) == 1
    results = []
    for target in range(total):
        index = order[target // quarter] * quarter + target % quarter
        modulus = fill(moduli[source_count + index])
        inverse_modulus = 1.0 / modulus
        targets[0, target] = modulus
        targets[1, target] = inverse_modulus
        modulus, inverse_modulus = spread(modulus, width), spread(inverse_modulus, width)
        first = 2 * target * block
        value = chosen[first : first + block] + 256.0 * chosen[first + block : first + 2 * block]
        value = jnp.where(upper, residue(256.0 * value, modulus, inverse_modulus), value)
        use = jnp.where(inner, 1, 0) if target // quarter != 2 else 0
        value = jnp.where(same & ((from_outer == False) | (use > 0)), value, 0.0)
        high_byte = jnp.floor(value * (1.0 / 256.0))
        results += [value - 256.0 * high_byte, high_byte]
    weights[...] = jnp.concatenate(results, axis=0).astype(jnp.bfloat16)


def scale_tile(values, columns, stage, scaled, read, write):
    width = write.size
    for word in range(scaled.shape[0]):
        if values.dtype == jnp.int32:
            pair = halves(values[word, :, read])
        else:
            pair = (values[2 * word, :, read], values[2 * word + 1, :, read])
        results = []
        for side, value in enumerate(pair):
            limb = 2 * word + side
            value = value.astype(jnp.float32)
            high, low, share, modulus, inverse = (spread(columns[kind, limb], width) for kind in range(5))
            stage[limb, :, read] = value * share
            upper = centred(value * high, modulus, inverse)
            results.append(residue(256.0 * upper + value * low, modulus, inverse).astype(jnp.int32))
        scaled[word, :, write] = pack_pair(*results)


def out_copy(stage, out, start, step, tile, sem):
    return pltpu.make_async_copy(
        stage.at[:, :, span_of(step, tile)],
        out.at[:, :, pl.ds(pl.multiple_of(start + step * tile, tile), tile)],
        sem.at[step],
    )


def first_kernel(
    place, levels, moduli, inverse, cross, residues, columns, targets, weights, source, scaled, landing, stage, sems, out_sems
):
    _, block, width = stage.shape
    tile = width // sems.shape[0]
    home = place[1]

    def load(step):
        return pltpu.make_async_copy(
            residues.at[:, pl.ds(pl.multiple_of(home * block, block), block), span_of(step, tile)],
            landing.at[:, :, span_of(step, tile)],
            sems.at[step],
        )

    def store(step):
        return out_copy(stage, source, home * width, step, tile, out_sems)

    steps = width // tile
    loop(steps, lambda step: load(step).start())
    build_tables(place, levels, moduli, inverse, cross, columns, targets, weights)

    def body(step):
        load(step).wait()
        scale_tile(landing, columns, stage, scaled, span_of(step, tile), span_of(step, tile))
        store(step).start()

    loop(steps, body)
    loop(steps, lambda step: store(step).wait())


def tile_of(width):
    return min(width, 1024)


def first(place, levels, moduli, inverse_table, cross, residues, block, count):
    limbs, _, width = residues.shape
    source_count = inverse_table.shape[0]
    total = moduli.shape[0] - source_count
    steps = width // tile_of(width)
    return pl.pallas_call(
        first_kernel,
        in_specs=[SCALARS] * 4 + [HERE, FAR],
        out_specs=[HERE, HERE, HERE, FAR, HERE],
        out_shape=[
            pltpu.VMEM((5, limbs, block, LANES), jnp.float32),
            pltpu.VMEM((2, total, block, LANES), jnp.float32),
            pltpu.VMEM((2 * total * block, 4 * limbs * block), jnp.bfloat16),
            jax.ShapeDtypeStruct((limbs, block, width * count), jnp.float32),
            pltpu.VMEM((limbs // 2, block, width), jnp.int32),
        ],
        scratch_shapes=[
            pltpu.VMEM((limbs, block, width), jnp.float32),
            pltpu.VMEM((limbs, block, width), jnp.float32),
            pltpu.SemaphoreType.DMA((steps,)),
            pltpu.SemaphoreType.DMA((steps,)),
        ],
        compiler_params=params(8),
        cost_estimate=cost(limbs * block * width, 60, 10 * limbs * block * width),
        name="first",
    )(place, levels, moduli, inverse_table, cross, residues)


def pack_kernel(offsets, place, residues, *rest):
    outs, (landing, sems) = rest[:-2], rest[-2:]
    _, _, block, width = landing.shape
    tile = tile_of(width)

    def load(turn):
        peer = place[1] ^ offsets[turn]
        return pltpu.make_async_copy(
            residues.at[:, pl.ds(pl.multiple_of(peer * block, block), block), :], landing.at[turn], sems.at[turn]
        )

    for turn in range(len(outs)):
        load(turn).start()
    for turn, out in enumerate(outs):
        load(turn).wait()

        def body(step):
            span = span_of(step, tile)
            for word in range(out.shape[0]):
                one = landing[turn, 2 * word, :, span].astype(jnp.int32)
                two = landing[turn, 2 * word + 1, :, span].astype(jnp.int32)
                out[word, :, span] = pack_pair(one, two)

        loop(width // tile, body)


def pack_blocks(place, residues, offsets, block):
    limbs, _, width = residues.shape
    peers = len(offsets)
    return pl.pallas_call(
        functools.partial(pack_kernel, offsets),
        in_specs=[SCALARS, FAR],
        out_specs=[HERE] * peers,
        out_shape=[pltpu.VMEM((limbs // 2, block, width), jnp.int32)] * peers,
        scratch_shapes=[
            pltpu.VMEM((peers, limbs, block, width), jnp.float32),
            pltpu.SemaphoreType.DMA((peers,)),
        ],
        compiler_params=params(12),
        cost_estimate=cost(peers * limbs * block * width, 16, 6 * peers * limbs * block * width),
        name="pack",
    )(place, residues)


def scale_kernel(offsets, place, columns, *rest):
    values = rest[: len(offsets)]
    source, scaled, stage, sems = rest[len(offsets) + 1 :]
    width = values[0].shape[2]
    tile = tile_of(width)
    steps = width // tile
    stores = []
    for turn, offset in enumerate(offsets):
        start = (place[1] ^ offset) * width

        def store(step, turn=turn, start=start):
            return out_copy(stage.at[turn], source, start, step, tile, sems.at[turn])

        def body(step):
            write = pl.ds(pl.multiple_of(turn * width + step * tile, tile), tile)
            scale_tile(values[turn], columns, stage.at[turn], scaled, span_of(step, tile), write)
            store(step).start()

        loop(steps, body)
        stores.append(store)
    for store in stores:
        loop(steps, lambda step: store(step).wait())


def scale_chunk(place, columns, values, offsets, source):
    words, block, width = values[0].shape
    limbs = source.shape[0]
    parts = len(values)
    return pl.pallas_call(
        functools.partial(scale_kernel, offsets),
        in_specs=[SCALARS, HERE] + [HERE] * parts + [FAR],
        out_specs=[FAR, HERE],
        out_shape=[
            jax.ShapeDtypeStruct(source.shape, jnp.float32),
            pltpu.VMEM((words, block, width * parts), jnp.int32),
        ],
        scratch_shapes=[
            pltpu.VMEM((parts, limbs, block, width), jnp.float32),
            pltpu.SemaphoreType.DMA((parts, width // tile_of(width))),
        ],
        input_output_aliases={2 + parts: 0},
        compiler_params=params(8),
        cost_estimate=cost(parts * limbs * block * width, 40, 8 * parts * limbs * block * width),
        name="scale",
    )(place, columns, *values, source)


def mix_kernel(targets, weights, own, received, far_out, outer_out, mine_out):
    block = own.shape[1]
    tile = tile_of(own.shape[2])

    def body(step):
        span = span_of(step, tile)
        digits = []
        for words in (own, received):
            for word in range(words.shape[0]):
                value = words[word, :, span]
                for byte in range(4):
                    part = lax.shift_right_logical(value, 8 * byte) if byte else value
                    if byte < 3:
                        part = part & 0xFF
                    digits.append(part.astype(jnp.float32))
        stacked = jnp.concatenate(digits, axis=0).astype(jnp.bfloat16)
        sums = jnp.dot(weights[...], stacked, preferred_element_type=jnp.float32)
        reduced = []
        for target in range(targets.shape[1]):
            modulus, inverse = spread(targets[0, target], tile), spread(targets[1, target], tile)
            low = sums[2 * target * block : (2 * target + 1) * block]
            high = sums[(2 * target + 1) * block : (2 * target + 2) * block]
            upper = centred(high, modulus, inverse)
            reduced.append(residue(256.0 * upper + low, modulus, inverse).astype(jnp.int32))
        words = [pack_pair(reduced[t], reduced[t + 1]) for t in range(0, len(reduced), 2)]
        position = 0
        for out in (far_out, outer_out, mine_out):
            for word in range(out.shape[0]):
                out[word, :, span] = words[position]
                position += 1

    loop(own.shape[2] // tile, body)


def mix_chunk(own, received, weights, targets):
    words, block, length = own.shape
    total = targets.shape[1]
    counts = (total // 4, total // 8, total // 8)
    return pl.pallas_call(
        mix_kernel,
        in_specs=[HERE] * 4,
        out_specs=[HERE] * 3,
        out_shape=[pltpu.VMEM((count, block, length), jnp.int32) for count in counts],
        compiler_params=params(8),
        cost_estimate=cost(total * block * length, 40, 4 * (2 * words + 4) * block * length),
        name="mix",
    )(targets, weights, own, received)


def forward_kernel(first_target, moduli, outer, arrived, out):
    words = out.shape[0]
    tile = tile_of(out.shape[2])

    def body(step):
        span = span_of(step, tile)
        for word in range(words):
            pairs = zip(halves(outer[word, :, span]), halves(arrived[words + word, :, span]))
            out[word, :, span] = pack_pair(
                *(
                    join_residues(a, b, spread(moduli[0, first_target + 2 * word + side].astype(jnp.int32), tile))
                    for side, (a, b) in enumerate(pairs)
                )
            )

    loop(out.shape[2] // tile, body)


def forward_chunk(outer, arrived, targets):
    words, block, length = outer.shape
    return pl.pallas_call(
        functools.partial(forward_kernel, 4 * words),
        in_specs=[HERE] * 3,
        out_specs=HERE,
        out_shape=pltpu.VMEM(outer.shape, jnp.int32),
        compiler_params=params(4),
        cost_estimate=cost(words * block * length, 40, 12 * words * block * length),
        name="forward",
    )(targets, outer, arrived)


def finish_kernel(offsets, first_target, place, targets, mine, arrived, relayed, *rest):
    out, stage, sems = rest[-3:]
    width = stage.shape[2] // len(offsets)
    tile = tile_of(width)
    steps = width // tile
    inner = (place[0] == 1) | (place[0] == 2)

    def store(step, turn):
        return pltpu.make_async_copy(
            stage.at[:, :, pl.ds(turn * width + step * tile, tile)],
            out.at[:, :, pl.ds(pl.multiple_of((place[1] ^ offsets[turn]) * width + step * tile, tile), tile)],
            sems.at[turn, step],
        )

    for turn in range(len(offsets)):

        def body(step):
            span = pl.ds(pl.multiple_of(turn * width + step * tile, tile), tile)
            for word in range(mine.shape[0]):
                other = jnp.where(inner, arrived[word, :, span], relayed[word, :, span])
                for side, (a, b) in enumerate(zip(halves(mine[word, :, span]), halves(other))):
                    target = first_target + 2 * word + side
                    modulus = spread(targets[0, target].astype(jnp.int32), tile)
                    total = join_residues(a, b, modulus).astype(jnp.float32)
                    stage[2 * word + side, :, span] = total * spread(targets[1, target], tile)
            store(step, turn).start()

        loop(steps, body)
    for turn in range(len(offsets)):
        loop(steps, lambda step: store(step, turn).wait())


def finish_chunk(place, targets, mine, arrived, relayed, offsets, shape, buffer):
    words, block, length = mine.shape
    width = length // len(offsets)
    operands = [place, targets, mine, arrived, relayed]
    in_specs = [SCALARS] + [HERE] * 4
    aliases = {}
    if buffer is not None:
        aliases[len(operands)] = 0
        operands.append(buffer)
        in_specs.append(FAR)
    return pl.pallas_call(
        functools.partial(finish_kernel, offsets, 6 * words),
        in_specs=in_specs,
        out_specs=FAR,
        out_shape=jax.ShapeDtypeStruct(shape, jnp.float32),
        scratch_shapes=[
            pltpu.VMEM((2 * words, block, length), jnp.float32),
            pltpu.SemaphoreType.DMA((len(offsets), width // tile_of(width))),
        ],
        input_output_aliases=aliases,
        compiler_params=params(8),
        cost_estimate=cost(words * block * length, 40, 20 * words * block * length),
        name="finish",
    )(*operands)


def chunk_plan(count):
    if count == 8:
        return [(0,), (1,), (2,), (4,), (3,), (5,), (6,), (7,)]
    unit = max(1, count // 8)
    edges = sorted({0, 1} | set(range(unit, count + 1, unit)))
    return [tuple(range(start, end)) for start, end in zip(edges, edges[1:])]


def timeline(plan):
    steps = len(plan)
    events = ["first", "a0", "pack"]
    order = [offset for chunk in plan for offset in chunk if offset]
    ready = [offset for chunk in plan[1:4] for offset in chunk]
    events += [f"p{offset}" for offset in ready]
    events += ["scale1", "a1"] + [f"p{offset}" for offset in order if offset not in ready]
    for step in range(steps + 3):
        if step < steps:
            events += [f"mix{step}", f"b{step}"]
        if step + 2 < steps:
            events += [f"scale{step + 2}", f"a{step + 2}"]
        if 1 <= step < steps + 1:
            events += [f"forward{step - 1}", f"c{step - 1}"]
        if 2 <= step < steps + 2:
            events.append(f"finish{step - 2}")
    return events


def per_device(residues, levels, moduli, inverse_table, cross_table):
    source_count, _, target_count = cross_table.shape
    _, _, width = residues.shape
    count = lax.axis_size("coef")
    assert lax.axis_size("limb") == 4
    block = residues.shape[1] // count
    place = jnp.stack([lax.axis_index("limb"), lax.axis_index("coef")]).astype(jnp.int32)
    residues = pltpu.with_memory_space_constraint(residues, pltpu.HBM)
    cross = cross_table.reshape(source_count, source_count * target_count)
    plan = chunk_plan(count)
    steps = len(plan)

    scaled, received, mixed, crossed, relayed = ([None] * steps for _ in range(5))
    arrived = {}
    packed = {}
    result = None
    shape = (target_count // 4, block, width * count)
    for event in timeline(plan):
        kind = event.rstrip("0123456789")
        step = int(event[len(kind) :] or 0)
        if kind == "first":
            columns, targets, weights, source, scaled[0] = first(
                place, levels, moduli, inverse_table, cross, residues, block, count
            )
        elif kind == "pack":
            offsets = tuple(range(1, count))
            packed = dict(zip(offsets, pack_blocks(place, residues, offsets, block)))
        elif kind == "p":
            arrived[step] = lax.ppermute(packed[step], "coef", [(i, i ^ step) for i in range(count)])
        elif kind == "scale":
            values = [arrived[offset] for offset in plan[step]]
            source, scaled[step] = scale_chunk(place, columns, values, plan[step], source)
        elif kind == "a":
            received[step] = lax.ppermute(scaled[step], "limb", [(0, 1), (3, 2)])
        elif kind == "mix":
            mixed[step] = mix_chunk(scaled[step], received[step], weights, targets)
        elif kind == "b":
            crossed[step] = lax.ppermute(mixed[step][0], "limb", [(1, 2), (2, 1)])
        elif kind == "forward":
            relayed[step] = forward_chunk(mixed[step][1], crossed[step], targets)
        elif kind == "c":
            relayed[step] = lax.ppermute(relayed[step], "limb", [(1, 0), (2, 3)])
        else:
            result = finish_chunk(
                place, targets, mixed[step][2], crossed[step], relayed[step], plan[step], shape, result
            )
    return (source, result)


def solution(mesh):
    placed = (P("limb", None, "coef"), P(), P(), P(), P())

    return jax.shard_map(
        per_device,
        mesh=mesh,
        in_specs=placed,
        out_specs=(P("limb", "coef", None), P("limb", "coef", None)),
        check_vma=False,
    )
```

time: 465 us -> 212 us (0.46)
  waiting for transfers between devices: 316 us -> 106 us
  other arithmetic: 70.2 us -> 0.08 us
  Pallas kernels: 0 us -> 55.7 us
  local copies, waits for them, and re-layouts: 39.2 us -> 0.18 us
  starting transfers between devices: 9.81 us -> 48.2 us
  matrix products: 15.8 us -> 0 us
  between operations: 14.1 us -> 1.23 us
    reduce_scatter x1 -> x0, waiting for transfers between devices: 278 us -> none  [per_device(): lax.psum_scatter(reduce_targets(digit_sums, target_mod), 'limb', scatter_...]
    ppermute x0 -> x31, waiting for transfers between devices: none -> 106 us  [the longest x8 45.5 us: per_device(): received[step] = lax.ppermute(scaled[step], 'limb', [(0, 1), (3, 2)])]
    pallas_call x0 -> x33, Pallas kernels: none -> 55.7 us  [the longest x8 19.7 us: mix_chunk(): pl.pallas_call(mix_kernel, in_specs=[HERE] * 4, out_specs=[HERE] * 3, out...]
    ppermute x0 -> x31, starting transfers between devices: none -> 48.2 us  [the longest x8 24.2 us: per_device(): received[step] = lax.ppermute(scaled[step], 'limb', [(0, 1), (3, 2)])]
    another operation x4 -> x1, other arithmetic: 38.3 us -> 0.08 us  [per_device(): jnp.stack([lax.axis_index('limb'), lax.axis_index('coef')])]
    all_to_all x2 -> x0, waiting for transfers between devices: 37.5 us -> none  [the longest x1 37.5 us: per_device(): lax.all_to_all(result, 'coef', split_axis=1, concat_axis=2, tiled=True)]
    select_n x1 -> x0, other arithmetic: 25.8 us -> none  [modulo(): return jnp.where(remain >= modulus, remain - modulus, remain)]
    all_to_all x2 -> x0, local copies, waits for them, and re-layouts: 18.3 us -> none  [the longest x1 11.6 us: per_device(): lax.all_to_all(normalized, 'coef', split_axis=1, concat_axis=2, tiled=True)]
  transfers between devices with their start and end apart: 3 -> 31, of which waited for: 2 -> 17; matrix products, arithmetic and copies ran while one was open for 4% -> 0% of each run, Pallas kernels for 0% -> 23%
where the time goes in v1:
time: 212 us; the launch traced here: 211 us
  waiting for transfers between devices  106 us (50%)
  Pallas kernels  55.7 us (26%)
  starting transfers between devices  48.2 us (23%)
    ppermute x8, waiting for transfers between devices, per_device(): received[step] = lax.ppermute(scaled[step], 'limb', [(0, 1), (3, 2)])  45.5 us
    ppermute x8, waiting for transfers between devices, per_device(): relayed[step] = lax.ppermute(relayed[step], 'limb', [(1, 0), (2, 3)])  38.6 us
    ppermute x8, starting transfers between devices, per_device(): received[step] = lax.ppermute(scaled[step], 'limb', [(0, 1), (3, 2)])  24.2 us
    ppermute x7, waiting for transfers between devices, per_device(): lax.ppermute(packed[step], 'coef', [(i, i ^ step) for i in range(count)])  21.8 us
    pallas_call x8, Pallas kernels, mix_chunk(): pl.pallas_call(mix_kernel, in_specs=[HERE] * 4, out_specs=[HERE] * 3, out...  19.7 us
    pallas_call x7, Pallas kernels, scale_chunk(): pl.pallas_call(functools.partial(scale_kernel, offsets), in_specs=[SCALAR...  14.5 us
    pallas_call x8, Pallas kernels, finish_chunk(): pl.pallas_call(functools.partial(finish_kernel, offsets, 6 * words), in_s...  11.7 us
    ppermute x8, starting transfers between devices, per_device(): relayed[step] = lax.ppermute(relayed[step], 'limb', [(1, 0), (2, 3)])  10.3 us
  transfers between devices with their start and end apart: 31, of which 17 were waited for; matrix products, arithmetic and copies ran while one was open for 0% of the time, Pallas kernels for 23%

profile of v1, /device:TPU:0, one launch (start us, length us, event | category | flops | bytes accessed | tf_op | source)
XLA Modules:
  0.0 211.3 jit_solution(5965428333610378993)
XLA Ops:
  0.8 5.3 %pack.1 = (s32[2,8,8192]{2,1,0:T(8,128)}, s32[2,8,8192]{2,1,0:T(8,128)S(1)}, s32[2,8,8192]{2,1,0:T(8,128)}, s32[2,8,8192]{2,1,0:T(8,128)S(1)}, s32[2,8,8192]{2,1...) custom-call(s32[2]{0:T(128)S(1)} %pad_add_fusion.place, f32[4,64,8192]{2,1,0:T(8,128)} %residues.3), custom_call_target="tpu_custom_call" | custom-call | flops 29360128 | bytes 11010048 | tf_op jit(solution)/shard_map/pack/pallas_call | solution.py:265
  6.1 3.1 %collective-permute-start.4 = (s32[2,8,8192]{2,1,0:T(8,128)S(1)}, s32[2,8,8192]{2,1,0:T(8,128)S(1)}, u32[]{:S(2)}, u32[]{:S(2)}) collective-permute-start(s32[2,8,8192]{2,1,0:T(8,128)S(1)} %get-tuple-element.57), channel_id=1, source_target_pairs={{0,4},{1,5},{2,6},{3,7},{4,0},{5,1},{6,2},{7,3},{8,12},{9,13},{10,... | collective-permute-start | bytes 1572872 | tf_op jit(solution)/shard_map/ppermute | solution.py:520
  9.2 1.5 collective-permute-start.5
  11.3 10.6 %collective-permute-done.4.rest_0_ = s32[2,8,8192]{2,1,0:T(8,128)S(1)} collective-permute-done((s32[2,8,8192]{2,1,0:T(8,128)S(1)}, s32[2,8,8192]{2,1,0:T(8,128)S(1)}, u32[]{:S(2)}, u32[]{:S(2)}) %collective-permute-start.4) | collective-permute-done | bytes 524320 | tf_op jit(solution)/shard_map/ppermute | solution.py:520
  21.9 2.9 %collective-permute-start.1 = (s32[2,8,8192]{2,1,0:T(8,128)}, s32[2,8,8192]{2,1,0:T(8,128)S(1)}, u32[]{:S(2)}, u32[]{:S(2)}) collective-permute-start(s32[2,8,8192]{2,1,0:T(8,128)} %get-tuple-element.54), channel_id=1, source_target_pairs={{0,6},{1,7},{2,4},{3,5},{4,2},{5,3},{6,0},{7,1},{8,14},{9,15},{10,... | collective-permute-start | bytes 1572872 | tf_op jit(solution)/shard_map/ppermute | solution.py:520
  25.1 3.1 %first.1 = (f32[5,4,8,128]{3,2,1,0:T(8,128)S(1)}, f32[2,8,8,128]{3,2,1,0:T(8,128)S(1)}, bf16[128,128]{1,0:T(8,128)(2,1)S(1)}, f32[4,8,65536]{2,1,0:T(8,128)}, s32[2,8,8192]{2,1,0:T(8,128)S(1)}) custom-call(s32[2]{0:T(128)S(1)} %pad_add_fusion.place, s32[64]{0:T(128)S(1)} %copy-done.1, s32[24]{0:T(128)S(1)} %copy-done.2, s32[16,16]{1,0:T(8,128)S(1)} %copy-done, ...), custom_call_target="tpu_custom_call" | custom-call | flops 15728640 | bytes 2621440 | tf_op jit(solution)/shard_map/first/pallas_call | solution.py:213
  28.2 3.5 %collective-permute-start.28 = (s32[2,8,8192]{2,1,0:T(8,128)S(1)}, s32[2,8,8192]{2,1,0:T(8,128)S(1)}, u32[]{:S(2)}, u32[]{:S(2)}) collective-permute-start(s32[2,8,8192]{2,1,0:T(8,128)S(1)} %get-tuple-element.98.own), channel_id=1, source_target_pairs={{0,8},{24,16},{1,9},{25,17},{2,10},{26,18},{3,11},{27,19},{4,12},{... | collective-permute-start | bytes 1572872 | tf_op jit(solution)/shard_map/ppermute | solution.py:525
  31.7 2.5 %scale.7 = (f32[4,8,65536]{2,1,0:T(8,128)}, s32[2,8,8192]{2,1,0:T(8,128)S(1)}) custom-call(s32[2]{0:T(128)S(1)} %pad_add_fusion.place, f32[5,4,8,128]{3,2,1,0:T(8,128)S(1)} %get-tuple-element.52.columns, s32[2,8,8192]{2,1,0:T(8,128)} %collective-permute-done.6.rest_0_, f32[4,8,65536]{2,1,0:T(8,128)} %get-tuple-element.60.rest_1_), custom_call_target="tpu_custom_call", output_to_operand_aliasing={{0}: (3, {})} | custom-call | flops 10485760 | bytes 2097152 | tf_op jit(solution)/shard_map/scale/pallas_call | solution.py:308
  34.2 2.0 scale.8
  36.2 2.0 scale.9
  38.2 2.0 scale.10
  40.2 2.0 scale.11
  42.2 3.7 %collective-permute-done.1.rest_0_ = s32[2,8,8192]{2,1,0:T(8,128)S(1)} collective-permute-done((s32[2,8,8192]{2,1,0:T(8,128)}, s32[2,8,8192]{2,1,0:T(8,128)S(1)}, u32[]{:S(2)}, u32[]{:S(2)}) %collective-permute-start.1) | collective-permute-done | bytes 524320 | tf_op jit(solution)/shard_map/ppermute | solution.py:520
  45.9 2.0 scale.12
  47.9 7.4 %collective-permute-done.rest_0_ = s32[2,8,8192]{2,1,0:T(8,128)S(1)} collective-permute-done((s32[2,8,8192]{2,1,0:T(8,128)}, s32[2,8,8192]{2,1,0:T(8,128)S(1)}, u32[]{:S(2)}, u32[]{:S(2)}) %collective-permute-start) | collective-permute-done | bytes 524320 | tf_op jit(solution)/shard_map/ppermute | solution.py:520
  55.4 2.0 scale.13
  57.4 3.5 %collective-permute-start.7 = (s32[2,8,8192]{2,1,0:T(8,128)S(1)}, s32[2,8,8192]{2,1,0:T(8,128)S(1)}, u32[]{:S(2)}, u32[]{:S(2)}) collective-permute-start(s32[2,8,8192]{2,1,0:T(8,128)S(1)} %get-tuple-element.70.own), channel_id=1, source_target_pairs={{0,8},{24,16},{1,9},{25,17},{2,10},{26,18},{3,11},{27,19},{4,12},{... | collective-permute-start | bytes 1572872 | tf_op jit(solution)/shard_map/ppermute | solution.py:525
  60.9 1.3 collective-permute-start.10
  62.2 1.3 collective-permute-start.13
  63.5 1.3 collective-permute-start.22
  64.9 2.5 %mix.15 = (s32[2,8,8192]{2,1,0:T(8,128)S(1)}, s32[1,8,8192]{2,1,0:T(8,128)S(1)}, s32[1,8,8192]{2,1,0:T(8,128)S(1)}) custom-call(f32[2,8,8,128]{3,2,1,0:T(8,128)S(1)} %get-tuple-element.68.targets.moduli, bf16[128,128]{1,0:T(8,128)(2,1)S(1)} %get-tuple-element.69.weights, s32[2,8,8192]{2,1,0:T(8,128)S(1)} %get-tuple-element.98.own, ...), custom_call_target="tpu_custom_call" | custom-call | flops 20971520 | bytes 2097152 | tf_op jit(solution)/shard_map/mix/pallas_call | solution.py:365
  67.3 0.7 collective-permute-start.29
  68.0 5.1 %collective-permute-done.7.received = s32[2,8,8192]{2,1,0:T(8,128)S(1)} collective-permute-done((s32[2,8,8192]{2,1,0:T(8,128)S(1)}, s32[2,8,8192]{2,1,0:T(8,128)S(1)}, u32[]{:S(2)}, u32[]{:S(2)}) %collective-permute-start.7) | collective-permute-done | bytes 524320 | tf_op jit(solution)/shard_map/ppermute | solution.py:525
  73.1 4.4 %collective-permute-start.25 = (s32[2,8,8192]{2,1,0:T(8,128)S(1)}, s32[2,8,8192]{2,1,0:T(8,128)S(1)}, u32[]{:S(2)}, u32[]{:S(2)}) collective-permute-start(s32[2,8,8192]{2,1,0:T(8,128)S(1)} %get-tuple-element.94.own), channel_id=1, source_target_pairs={{0,8},{24,16},{1,9},{25,17},{2,10},{26,18},{3,11},{27,19},{4,12},{... | collective-permute-start | bytes 1572872 | tf_op jit(solution)/shard_map/ppermute | solution.py:525
  77.6 6.8 %collective-permute-done.10.received = s32[2,8,8192]{2,1,0:T(8,128)S(1)} collective-permute-done((s32[2,8,8192]{2,1,0:T(8,128)S(1)}, s32[2,8,8192]{2,1,0:T(8,128)S(1)}, u32[]{:S(2)}, u32[]{:S(2)}) %collective-permute-start.10) | collective-permute-done | bytes 524320 | tf_op jit(solution)/shard_map/ppermute | solution.py:525
  84.4 4.4 %collective-permute-start.19 = (s32[2,8,8192]{2,1,0:T(8,128)S(1)}, s32[2,8,8192]{2,1,0:T(8,128)S(1)}, u32[]{:S(2)}, u32[]{:S(2)}) collective-permute-start(s32[2,8,8192]{2,1,0:T(8,128)S(1)} %get-tuple-element.86.own), channel_id=1, source_target_pairs={{0,8},{24,16},{1,9},{25,17},{2,10},{26,18},{3,11},{27,19},{4,12},{... | collective-permute-start | bytes 1572872 | tf_op jit(solution)/shard_map/ppermute | solution.py:525
  88.8 6.8 %collective-permute-done.13.received = s32[2,8,8192]{2,1,0:T(8,128)S(1)} collective-permute-done((s32[2,8,8192]{2,1,0:T(8,128)S(1)}, s32[2,8,8192]{2,1,0:T(8,128)S(1)}, u32[]{:S(2)}, u32[]{:S(2)}) %collective-permute-start.13) | collective-permute-done | bytes 524320 | tf_op jit(solution)/shard_map/ppermute | solution.py:525
  95.6 4.4 %collective-permute-start.16 = (s32[2,8,8192]{2,1,0:T(8,128)S(1)}, s32[2,8,8192]{2,1,0:T(8,128)S(1)}, u32[]{:S(2)}, u32[]{:S(2)}) collective-permute-start(s32[2,8,8192]{2,1,0:T(8,128)S(1)} %get-tuple-element.82.own), channel_id=1, source_target_pairs={{0,8},{24,16},{1,9},{25,17},{2,10},{26,18},{3,11},{27,19},{4,12},{... | collective-permute-start | bytes 1572872 | tf_op jit(solution)/shard_map/ppermute | solution.py:525
  100.0 2.5 %mix.8 = (s32[2,8,8192]{2,1,0:T(8,128)S(1)}, s32[1,8,8192]{2,1,0:T(8,128)S(1)}, s32[1,8,8192]{2,1,0:T(8,128)S(1)}) custom-call(f32[2,8,8,128]{3,2,1,0:T(8,128)S(1)} %get-tuple-element.68.targets.moduli, bf16[128,128]{1,0:T(8,128)(2,1)S(1)} %get-tuple-element.69.weights, s32[2,8,8192]{2,1,0:T(8,128)S(1)} %get-tuple-element.70.own, ...), custom_call_target="tpu_custom_call" | custom-call | flops 20971520 | bytes 2097152 | tf_op jit(solution)/shard_map/mix/pallas_call | solution.py:365
  102.5 4.4 %collective-permute-done.22.received = s32[2,8,8192]{2,1,0:T(8,128)S(1)} collective-permute-done((s32[2,8,8192]{2,1,0:T(8,128)S(1)}, s32[2,8,8192]{2,1,0:T(8,128)S(1)}, u32[]{:S(2)}, u32[]{:S(2)}) %collective-permute-start.22) | collective-permute-done | bytes 524320 | tf_op jit(solution)/shard_map/ppermute | solution.py:525
  107.5 2.5 %mix.13 = (s32[2,8,8192]{2,1,0:T(8,128)S(1)}, s32[1,8,8192]{2,1,0:T(8,128)S(1)}, s32[1,8,8192]{2,1,0:T(8,128)S(1)}) custom-call(f32[2,8,8,128]{3,2,1,0:T(8,128)S(1)} %get-tuple-element.68.targets.moduli, bf16[128,128]{1,0:T(8,128)(2,1)S(1)} %get-tuple-element.69.weights, s32[2,8,8192]{2,1,0:T(8,128)S(1)} %get-tuple-element.90.own, ...), custom_call_target="tpu_custom_call" | custom-call | flops 20971520 | bytes 2097152 | tf_op jit(solution)/shard_map/mix/pallas_call | solution.py:365
  110.0 0.7 collective-permute-start.23
  110.9 7.2 %collective-permute-done.25.received = s32[2,8,8192]{2,1,0:T(8,128)S(1)} collective-permute-done((s32[2,8,8192]{2,1,0:T(8,128)S(1)}, s32[2,8,8192]{2,1,0:T(8,128)S(1)}, u32[]{:S(2)}, u32[]{:S(2)}) %collective-permute-start.25) | collective-permute-done | bytes 524320 | tf_op jit(solution)/shard_map/ppermute | solution.py:525
  118.1 1.3 collective-permute-start.30
  119.4 2.5 %mix.14 = (s32[2,8,8192]{2,1,0:T(8,128)S(1)}, s32[1,8,8192]{2,1,0:T(8,128)S(1)}, s32[1,8,8192]{2,1,0:T(8,128)S(1)}) custom-call(f32[2,8,8,128]{3,2,1,0:T(8,128)S(1)} %get-tuple-element.68.targets.moduli, bf16[128,128]{1,0:T(8,128)(2,1)S(1)} %get-tuple-element.69.weights, s32[2,8,8192]{2,1,0:T(8,128)S(1)} %get-tuple-element.94.own, ...), custom_call_target="tpu_custom_call" | custom-call | flops 20971520 | bytes 2097152 | tf_op jit(solution)/shard_map/mix/pallas_call | solution.py:365
  121.8 7.5 %collective-permute-done.19.received = s32[2,8,8192]{2,1,0:T(8,128)S(1)} collective-permute-done((s32[2,8,8192]{2,1,0:T(8,128)S(1)}, s32[2,8,8192]{2,1,0:T(8,128)S(1)}, u32[]{:S(2)}, u32[]{:S(2)}) %collective-permute-start.19) | collective-permute-done | bytes 524320 | tf_op jit(solution)/shard_map/ppermute | solution.py:525
  130.0 2.4 %mix.12 = (s32[2,8,8192]{2,1,0:T(8,128)S(1)}, s32[1,8,8192]{2,1,0:T(8,128)S(1)}, s32[1,8,8192]{2,1,0:T(8,128)S(1)}) custom-call(f32[2,8,8,128]{3,2,1,0:T(8,128)S(1)} %get-tuple-element.68.targets.moduli, bf16[128,128]{1,0:T(8,128)(2,1)S(1)} %get-tuple-element.69.weights, s32[2,8,8192]{2,1,0:T(8,128)S(1)} %get-tuple-element.86.own, ...), custom_call_target="tpu_custom_call" | custom-call | flops 20971520 | bytes 2097152 | tf_op jit(solution)/shard_map/mix/pallas_call | solution.py:365
  132.5 7.8 %collective-permute-done.16.received = s32[2,8,8192]{2,1,0:T(8,128)S(1)} collective-permute-done((s32[2,8,8192]{2,1,0:T(8,128)S(1)}, s32[2,8,8192]{2,1,0:T(8,128)S(1)}, u32[]{:S(2)}, u32[]{:S(2)}) %collective-permute-start.16) | collective-permute-done | bytes 524320 | tf_op jit(solution)/shard_map/ppermute | solution.py:525
  140.9 2.5 %mix.10 = (s32[2,8,8192]{2,1,0:T(8,128)S(1)}, s32[1,8,8192]{2,1,0:T(8,128)S(1)}, s32[1,8,8192]{2,1,0:T(8,128)S(1)}) custom-call(f32[2,8,8,128]{3,2,1,0:T(8,128)S(1)} %get-tuple-element.68.targets.moduli, bf16[128,128]{1,0:T(8,128)(2,1)S(1)} %get-tuple-element.69.weights, s32[2,8,8192]{2,1,0:T(8,128)S(1)} %get-tuple-element.78.own, ...), custom_call_target="tpu_custom_call" | custom-call | flops 20971520 | bytes 2097152 | tf_op jit(solution)/shard_map/mix/pallas_call | solution.py:365
  143.4 2.5 %mix.11 = (s32[2,8,8192]{2,1,0:T(8,128)S(1)}, s32[1,8,8192]{2,1,0:T(8,128)S(1)}, s32[1,8,8192]{2,1,0:T(8,128)S(1)}) custom-call(f32[2,8,8,128]{3,2,1,0:T(8,128)S(1)} %get-tuple-element.68.targets.moduli, bf16[128,128]{1,0:T(8,128)(2,1)S(1)} %get-tuple-element.69.weights, s32[2,8,8192]{2,1,0:T(8,128)S(1)} %get-tuple-element.82.own, ...), custom_call_target="tpu_custom_call" | custom-call | flops 20971520 | bytes 2097152 | tf_op jit(solution)/shard_map/mix/pallas_call | solution.py:365
  146.6 0.7 collective-permute-start.17
  147.3 2.5 %mix.9 = (s32[2,8,8192]{2,1,0:T(8,128)S(1)}, s32[1,8,8192]{2,1,0:T(8,128)S(1)}, s32[1,8,8192]{2,1,0:T(8,128)S(1)}) custom-call(f32[2,8,8,128]{3,2,1,0:T(8,128)S(1)} %get-tuple-element.68.targets.moduli, bf16[128,128]{1,0:T(8,128)(2,1)S(1)} %get-tuple-element.69.weights, s32[2,8,8192]{2,1,0:T(8,128)S(1)} %get-tuple-element.74.own, ...), custom_call_target="tpu_custom_call" | custom-call | flops 20971520 | bytes 2097152 | tf_op jit(solution)/shard_map/mix/pallas_call | solution.py:365
  150.7 1.3 collective-permute-start.24
  152.2 1.3 collective-permute-start.27
  153.7 1.3 collective-permute-start.21
  155.2 1.3 collective-permute-start.18
  156.7 1.3 collective-permute-start.15
  158.2 12.3 %collective-permute-done.24.relayed = s32[1,8,8192]{2,1,0:T(8,128)S(1)} collective-permute-done((s32[1,8,8192]{2,1,0:T(8,128)S(1)}, s32[1,8,8192]{2,1,0:T(8,128)S(1)}, u32[]{:S(2)}, u32[]{:S(2)}) %collective-permute-start.24) | collective-permute-done | bytes 262176 | tf_op jit(solution)/shard_map/ppermute | solution.py:533
  170.5 1.3 collective-permute-start.12
  172.0 2.1 %collective-permute-done.27.relayed = s32[1,8,8192]{2,1,0:T(8,128)S(1)} collective-permute-done((s32[1,8,8192]{2,1,0:T(8,128)S(1)}, s32[1,8,8192]{2,1,0:T(8,128)S(1)}, u32[]{:S(2)}, u32[]{:S(2)}) %collective-permute-start.27) | collective-permute-done | bytes 262176 | tf_op jit(solution)/shard_map/ppermute | solution.py:533
  174.1 1.3 collective-permute-start.9
  175.4 1.5 finish.8.rest_0_
  176.8 1.5 finish.9.rest_0_
  178.3 1.5 finish.10.rest_0_
  179.8 10.4 %collective-permute-done.21.relayed = s32[1,8,8192]{2,1,0:T(8,128)S(1)} collective-permute-done((s32[1,8,8192]{2,1,0:T(8,128)S(1)}, s32[1,8,8192]{2,1,0:T(8,128)S(1)}, u32[]{:S(2)}, u32[]{:S(2)}) %collective-permute-start.21) | collective-permute-done | bytes 262176 | tf_op jit(solution)/shard_map/ppermute | solution.py:533
  190.2 1.5 finish.11.rest_0_
  191.6 1.3 collective-permute-done.18.relayed
  193.0 1.5 finish.12.rest_0_
  194.4 5.9 %collective-permute-done.15.relayed = s32[1,8,8192]{2,1,0:T(8,128)S(1)} collective-permute-done((s32[1,8,8192]{2,1,0:T(8,128)S(1)}, s32[1,8,8192]{2,1,0:T(8,128)S(1)}, u32[]{:S(2)}, u32[]{:S(2)}) %collective-permute-start.15) | collective-permute-done | bytes 262176 | tf_op jit(solution)/shard_map/ppermute | solution.py:533
  200.3 1.5 finish.13.rest_0_
  201.8 4.2 %collective-permute-done.12.relayed = s32[1,8,8192]{2,1,0:T(8,128)S(1)} collective-permute-done((s32[1,8,8192]{2,1,0:T(8,128)S(1)}, s32[1,8,8192]{2,1,0:T(8,128)S(1)}, u32[]{:S(2)}, u32[]{:S(2)}) %collective-permute-start.12) | collective-permute-done | bytes 262176 | tf_op jit(solution)/shard_map/ppermute | solution.py:533
  206.0 1.5 finish.14.rest_0_
  207.4 2.4 %collective-permute-done.9.relayed = s32[1,8,8192]{2,1,0:T(8,128)S(1)} collective-permute-done((s32[1,8,8192]{2,1,0:T(8,128)S(1)}, s32[1,8,8192]{2,1,0:T(8,128)S(1)}, u32[]{:S(2)}, u32[]{:S(2)}) %collective-permute-start.9) | collective-permute-done | bytes 262176 | tf_op jit(solution)/shard_map/ppermute | solution.py:533
  209.8 1.5 finish.15
  (42 shorter events, 5.9 us)
Async XLA Ops:
  0.6 24.3 %copy-start.3 = (s32[16,16,8]{1,2,0:T(8,128)S(1)}, s32[16,16,8]{1,2,0:T(8,128)}, u32[]{:S(2)}) copy-start(s32[16,16,8]{1,2,0:T(8,128)} %param.9) | copy-start | bytes 24580
  0.6 24.4 %copy-start = (s32[16,16]{1,0:T(8,128)S(1)}, s32[16,16]{1,0:T(8,128)}, u32[]{:S(2)}) copy-start(s32[16,16]{1,0:T(8,128)} %inverse.1) | copy-start | bytes 3076
  0.7 24.4 %copy-start.2 = (s32[24]{0:T(128)S(1)}, s32[24]{0:T(128)}, u32[]{:S(2)}) copy-start(s32[24]{0:T(128)} %moduli.1) | copy-start | bytes 292
  0.7 24.4 %copy-start.1 = (s32[64]{0:T(128)S(1)}, s32[64]{0:T(128)}, u32[]{:S(2)}) copy-start(s32[64]{0:T(128)} %levels.1) | copy-start | bytes 772
  6.1 15.8 %collective-permute-start.4 = (s32[2,8,8192]{2,1,0:T(8,128)S(1)}, s32[2,8,8192]{2,1,0:T(8,128)S(1)}, u32[]{:S(2)}, u32[]{:S(2)}) collective-permute-start(s32[2,8,8192]{2,1,0:T(8,128)S(1)} %get-tuple-element.57), channel_id=1, source_target_pairs={{0,4},{1,5},{2,6},{3,7},{4,0},{5,1},{6,2},{7,3},{8,12},{9,13},{10,... | collective-permute-start | bytes 1572872 | tf_op jit(solution)/shard_map/ppermute | solution.py:520
  9.2 15.7 %collective-permute-start.5 = (s32[2,8,8192]{2,1,0:T(8,128)S(1)}, s32[2,8,8192]{2,1,0:T(8,128)S(1)}, u32[]{:S(2)}, u32[]{:S(2)}) collective-permute-start(s32[2,8,8192]{2,1,0:T(8,128)S(1)} %get-tuple-element.58), channel_id=1, source_target_pairs={{0,2},{1,3},{2,0},{3,1},{4,6},{5,7},{6,4},{7,5},{8,10},{9,11},{10,... | collective-permute-start | bytes 1572872 | tf_op jit(solution)/shard_map/ppermute | solution.py:520
  10.6 17.5 %collective-permute-start.6 = (s32[2,8,8192]{2,1,0:T(8,128)}, s32[2,8,8192]{2,1,0:T(8,128)}, u32[]{:S(2)}, u32[]{:S(2)}) collective-permute-start(s32[2,8,8192]{2,1,0:T(8,128)} %get-tuple-element.59), channel_id=1, source_target_pairs={{0,1},{1,0},{2,3},{3,2},{4,5},{5,4},{6,7},{7,6},{8,9},{9,8},{10,11... | collective-permute-start | bytes 1572872 | tf_op jit(solution)/shard_map/ppermute | solution.py:520
  10.7 27.5 %collective-permute-start.3 = (s32[2,8,8192]{2,1,0:T(8,128)}, s32[2,8,8192]{2,1,0:T(8,128)S(1)}, u32[]{:S(2)}, u32[]{:S(2)}) collective-permute-start(s32[2,8,8192]{2,1,0:T(8,128)} %get-tuple-element.56), channel_id=1, source_target_pairs={{0,3},{1,2},{2,1},{3,0},{4,7},{5,6},{6,5},{7,4},{8,11},{9,10},{10,... | collective-permute-start | bytes 1572872 | tf_op jit(solution)/shard_map/ppermute | solution.py:520
  11.3 28.9 %collective-permute-start.2 = (s32[2,8,8192]{2,1,0:T(8,128)}, s32[2,8,8192]{2,1,0:T(8,128)S(1)}, u32[]{:S(2)}, u32[]{:S(2)}) collective-permute-start(s32[2,8,8192]{2,1,0:T(8,128)} %get-tuple-element.55), channel_id=1, source_target_pairs={{0,5},{1,4},{2,7},{3,6},{4,1},{5,0},{6,3},{7,2},{8,13},{9,12},{10,... | collective-permute-start | bytes 1572872 | tf_op jit(solution)/shard_map/ppermute | solution.py:520
  21.9 24.0 %collective-permute-start.1 = (s32[2,8,8192]{2,1,0:T(8,128)}, s32[2,8,8192]{2,1,0:T(8,128)S(1)}, u32[]{:S(2)}, u32[]{:S(2)}) collective-permute-start(s32[2,8,8192]{2,1,0:T(8,128)} %get-tuple-element.54), channel_id=1, source_target_pairs={{0,6},{1,7},{2,4},{3,5},{4,2},{5,3},{6,0},{7,1},{8,14},{9,15},{10,... | collective-permute-start | bytes 1572872 | tf_op jit(solution)/shard_map/ppermute | solution.py:520
  24.9 30.5 %collective-permute-start = (s32[2,8,8192]{2,1,0:T(8,128)}, s32[2,8,8192]{2,1,0:T(8,128)S(1)}, u32[]{:S(2)}, u32[]{:S(2)}) collective-permute-start(s32[2,8,8192]{2,1,0:T(8,128)} %get-tuple-element.53), channel_id=1, source_target_pairs={{0,7},{1,6},{2,5},{3,4},{4,3},{5,2},{6,1},{7,0},{8,15},{9,14},{10,... | collective-permute-start | bytes 1572872 | tf_op jit(solution)/shard_map/ppermute | solution.py:520
  28.2 36.7 %collective-permute-start.28 = (s32[2,8,8192]{2,1,0:T(8,128)S(1)}, s32[2,8,8192]{2,1,0:T(8,128)S(1)}, u32[]{:S(2)}, u32[]{:S(2)}) collective-permute-start(s32[2,8,8192]{2,1,0:T(8,128)S(1)} %get-tuple-element.98.own), channel_id=1, source_target_pairs={{0,8},{24,16},{1,9},{25,17},{2,10},{26,18},{3,11},{27,19},{4,12},{... | collective-permute-start | bytes 1572872 | tf_op jit(solution)/shard_map/ppermute | solution.py:525
  57.4 15.8 %collective-permute-start.7 = (s32[2,8,8192]{2,1,0:T(8,128)S(1)}, s32[2,8,8192]{2,1,0:T(8,128)S(1)}, u32[]{:S(2)}, u32[]{:S(2)}) collective-permute-start(s32[2,8,8192]{2,1,0:T(8,128)S(1)} %get-tuple-element.70.own), channel_id=1, source_target_pairs={{0,8},{24,16},{1,9},{25,17},{2,10},{26,18},{3,11},{27,19},{4,12},{... | collective-permute-start | bytes 1572872 | tf_op jit(solution)/shard_map/ppermute | solution.py:525
  60.9 23.5 %collective-permute-start.10 = (s32[2,8,8192]{2,1,0:T(8,128)S(1)}, s32[2,8,8192]{2,1,0:T(8,128)S(1)}, u32[]{:S(2)}, u32[]{:S(2)}) collective-permute-start(s32[2,8,8192]{2,1,0:T(8,128)S(1)} %get-tuple-element.74.own), channel_id=1, source_target_pairs={{0,8},{24,16},{1,9},{25,17},{2,10},{26,18},{3,11},{27,19},{4,12},{... | collective-permute-start | bytes 1572872 | tf_op jit(solution)/shard_map/ppermute | solution.py:525
  62.2 33.4 %collective-permute-start.13 = (s32[2,8,8192]{2,1,0:T(8,128)S(1)}, s32[2,8,8192]{2,1,0:T(8,128)S(1)}, u32[]{:S(2)}, u32[]{:S(2)}) collective-permute-start(s32[2,8,8192]{2,1,0:T(8,128)S(1)} %get-tuple-element.78.own), channel_id=1, source_target_pairs={{0,8},{24,16},{1,9},{25,17},{2,10},{26,18},{3,11},{27,19},{4,12},{... | collective-permute-start | bytes 1572872 | tf_op jit(solution)/shard_map/ppermute | solution.py:525
  63.5 43.3 %collective-permute-start.22 = (s32[2,8,8192]{2,1,0:T(8,128)S(1)}, s32[2,8,8192]{2,1,0:T(8,128)S(1)}, u32[]{:S(2)}, u32[]{:S(2)}) collective-permute-start(s32[2,8,8192]{2,1,0:T(8,128)S(1)} %get-tuple-element.90.own), channel_id=1, source_target_pairs={{0,8},{24,16},{1,9},{25,17},{2,10},{26,18},{3,11},{27,19},{4,12},{... | collective-permute-start | bytes 1572872 | tf_op jit(solution)/shard_map/ppermute | solution.py:525
  67.3 42.7 %collective-permute-start.29 = (s32[2,8,8192]{2,1,0:T(8,128)S(1)}, s32[2,8,8192]{2,1,0:T(8,128)S(1)}, u32[]{:S(2)}, u32[]{:S(2)}) collective-permute-start(s32[2,8,8192]{2,1,0:T(8,128)S(1)} %get-tuple-element.100), channel_id=1, source_target_pairs={{8,16},{16,8},{9,17},{17,9},{10,18},{18,10},{11,19},{19,11},{12,20... | collective-permute-start | bytes 1572872 | tf_op jit(solution)/shard_map/ppermute | solution.py:529
  73.1 44.9 %collective-permute-start.25 = (s32[2,8,8192]{2,1,0:T(8,128)S(1)}, s32[2,8,8192]{2,1,0:T(8,128)S(1)}, u32[]{:S(2)}, u32[]{:S(2)}) collective-permute-start(s32[2,8,8192]{2,1,0:T(8,128)S(1)} %get-tuple-element.94.own), channel_id=1, source_target_pairs={{0,8},{24,16},{1,9},{25,17},{2,10},{26,18},{3,11},{27,19},{4,12},{... | collective-permute-start | bytes 1572872 | tf_op jit(solution)/shard_map/ppermute | solution.py:525
  84.4 44.9 %collective-permute-start.19 = (s32[2,8,8192]{2,1,0:T(8,128)S(1)}, s32[2,8,8192]{2,1,0:T(8,128)S(1)}, u32[]{:S(2)}, u32[]{:S(2)}) collective-permute-start(s32[2,8,8192]{2,1,0:T(8,128)S(1)} %get-tuple-element.86.own), channel_id=1, source_target_pairs={{0,8},{24,16},{1,9},{25,17},{2,10},{26,18},{3,11},{27,19},{4,12},{... | collective-permute-start | bytes 1572872 | tf_op jit(solution)/shard_map/ppermute | solution.py:525
  95.6 44.6 %collective-permute-start.16 = (s32[2,8,8192]{2,1,0:T(8,128)S(1)}, s32[2,8,8192]{2,1,0:T(8,128)S(1)}, u32[]{:S(2)}, u32[]{:S(2)}) collective-permute-start(s32[2,8,8192]{2,1,0:T(8,128)S(1)} %get-tuple-element.82.own), channel_id=1, source_target_pairs={{0,8},{24,16},{1,9},{25,17},{2,10},{26,18},{3,11},{27,19},{4,12},{... | collective-permute-start | bytes 1572872 | tf_op jit(solution)/shard_map/ppermute | solution.py:525
  106.8 39.7 %collective-permute-start.8 = (s32[2,8,8192]{2,1,0:T(8,128)S(1)}, s32[2,8,8192]{2,1,0:T(8,128)S(1)}, u32[]{:S(2)}, u32[]{:S(2)}) collective-permute-start(s32[2,8,8192]{2,1,0:T(8,128)S(1)} %get-tuple-element.72), channel_id=1, source_target_pairs={{8,16},{16,8},{9,17},{17,9},{10,18},{18,10},{11,19},{19,11},{12,20... | collective-permute-start | bytes 1572872 | tf_op jit(solution)/shard_map/ppermute | solution.py:529
  110.0 39.7 %collective-permute-start.23 = (s32[2,8,8192]{2,1,0:T(8,128)S(1)}, s32[2,8,8192]{2,1,0:T(8,128)S(1)}, u32[]{:S(2)}, u32[]{:S(2)}) collective-permute-start(s32[2,8,8192]{2,1,0:T(8,128)S(1)} %get-tuple-element.92), channel_id=1, source_target_pairs={{8,16},{16,8},{9,17},{17,9},{10,18},{18,10},{11,19},{19,11},{12,20... | collective-permute-start | bytes 1572872 | tf_op jit(solution)/shard_map/ppermute | solution.py:529
  118.1 27.8 %collective-permute-start.30 = (s32[1,8,8192]{2,1,0:T(8,128)S(1)}, s32[1,8,8192]{2,1,0:T(8,128)S(1)}, u32[]{:S(2)}, u32[]{:S(2)}) collective-permute-start(s32[1,8,8192]{2,1,0:T(8,128)S(1)} %forward.15), channel_id=1, source_target_pairs={{8,0},{16,24},{9,1},{17,25},{10,2},{18,26},{11,3},{19,27},{12,4},{... | collective-permute-start | bytes 786440 | tf_op jit(solution)/shard_map/ppermute | solution.py:533
  129.3 21.3 %collective-permute-start.26 = (s32[2,8,8192]{2,1,0:T(8,128)S(1)}, s32[2,8,8192]{2,1,0:T(8,128)S(1)}, u32[]{:S(2)}, u32[]{:S(2)}) collective-permute-start(s32[2,8,8192]{2,1,0:T(8,128)S(1)} %get-tuple-element.96), channel_id=1, source_target_pairs={{8,16},{16,8},{9,17},{17,9},{10,18},{18,10},{11,19},{19,11},{12,20... | collective-permute-start | bytes 1572872 | tf_op jit(solution)/shard_map/ppermute | solution.py:529
  140.2 11.9 %collective-permute-start.20 = (s32[2,8,8192]{2,1,0:T(8,128)S(1)}, s32[2,8,8192]{2,1,0:T(8,128)S(1)}, u32[]{:S(2)}, u32[]{:S(2)}) collective-permute-start(s32[2,8,8192]{2,1,0:T(8,128)S(1)} %get-tuple-element.88), channel_id=1, source_target_pairs={{8,16},{16,8},{9,17},{17,9},{10,18},{18,10},{11,19},{19,11},{12,20... | collective-permute-start | bytes 1572872 | tf_op jit(solution)/shard_map/ppermute | solution.py:529
  145.9 9.3 %collective-permute-start.14 = (s32[2,8,8192]{2,1,0:T(8,128)S(1)}, s32[2,8,8192]{2,1,0:T(8,128)S(1)}, u32[]{:S(2)}, u32[]{:S(2)}) collective-permute-start(s32[2,8,8192]{2,1,0:T(8,128)S(1)} %get-tuple-element.80), channel_id=1, source_target_pairs={{8,16},{16,8},{9,17},{17,9},{10,18},{18,10},{11,19},{19,11},{12,20... | collective-permute-start | bytes 1572872 | tf_op jit(solution)/shard_map/ppermute | solution.py:529
  146.6 7.1 %collective-permute-start.17 = (s32[2,8,8192]{2,1,0:T(8,128)S(1)}, s32[2,8,8192]{2,1,0:T(8,128)S(1)}, u32[]{:S(2)}, u32[]{:S(2)}) collective-permute-start(s32[2,8,8192]{2,1,0:T(8,128)S(1)} %get-tuple-element.84), channel_id=1, source_target_pairs={{8,16},{16,8},{9,17},{17,9},{10,18},{18,10},{11,19},{19,11},{12,20... | collective-permute-start | bytes 1572872 | tf_op jit(solution)/shard_map/ppermute | solution.py:529
  149.8 6.9 %collective-permute-start.11 = (s32[2,8,8192]{2,1,0:T(8,128)S(1)}, s32[2,8,8192]{2,1,0:T(8,128)S(1)}, u32[]{:S(2)}, u32[]{:S(2)}) collective-permute-start(s32[2,8,8192]{2,1,0:T(8,128)S(1)} %get-tuple-element.76), channel_id=1, source_target_pairs={{8,16},{16,8},{9,17},{17,9},{10,18},{18,10},{11,19},{19,11},{12,20... | collective-permute-start | bytes 1572872 | tf_op jit(solution)/shard_map/ppermute | solution.py:529
  150.7 19.8 %collective-permute-start.24 = (s32[1,8,8192]{2,1,0:T(8,128)S(1)}, s32[1,8,8192]{2,1,0:T(8,128)S(1)}, u32[]{:S(2)}, u32[]{:S(2)}) collective-permute-start(s32[1,8,8192]{2,1,0:T(8,128)S(1)} %forward.13), channel_id=1, source_target_pairs={{8,0},{16,24},{9,1},{17,25},{10,2},{18,26},{11,3},{19,27},{12,4},{... | collective-permute-start | bytes 786440 | tf_op jit(solution)/shard_map/ppermute | solution.py:533
  152.2 21.9 %collective-permute-start.27 = (s32[1,8,8192]{2,1,0:T(8,128)S(1)}, s32[1,8,8192]{2,1,0:T(8,128)S(1)}, u32[]{:S(2)}, u32[]{:S(2)}) collective-permute-start(s32[1,8,8192]{2,1,0:T(8,128)S(1)} %forward.14), channel_id=1, source_target_pairs={{8,0},{16,24},{9,1},{17,25},{10,2},{18,26},{11,3},{19,27},{12,4},{... | collective-permute-start | bytes 786440 | tf_op jit(solution)/shard_map/ppermute | solution.py:533
  153.7 36.5 %collective-permute-start.21 = (s32[1,8,8192]{2,1,0:T(8,128)S(1)}, s32[1,8,8192]{2,1,0:T(8,128)S(1)}, u32[]{:S(2)}, u32[]{:S(2)}) collective-permute-start(s32[1,8,8192]{2,1,0:T(8,128)S(1)} %forward.12), channel_id=1, source_target_pairs={{8,0},{16,24},{9,1},{17,25},{10,2},{18,26},{11,3},{19,27},{12,4},{... | collective-permute-start | bytes 786440 | tf_op jit(solution)/shard_map/ppermute | solution.py:533
  155.2 37.8 %collective-permute-start.18 = (s32[1,8,8192]{2,1,0:T(8,128)S(1)}, s32[1,8,8192]{2,1,0:T(8,128)S(1)}, u32[]{:S(2)}, u32[]{:S(2)}) collective-permute-start(s32[1,8,8192]{2,1,0:T(8,128)S(1)} %forward.11), channel_id=1, source_target_pairs={{8,0},{16,24},{9,1},{17,25},{10,2},{18,26},{11,3},{19,27},{12,4},{... | collective-permute-start | bytes 786440 | tf_op jit(solution)/shard_map/ppermute | solution.py:533
  156.7 43.7 %collective-permute-start.15 = (s32[1,8,8192]{2,1,0:T(8,128)S(1)}, s32[1,8,8192]{2,1,0:T(8,128)S(1)}, u32[]{:S(2)}, u32[]{:S(2)}) collective-permute-start(s32[1,8,8192]{2,1,0:T(8,128)S(1)} %forward.10), channel_id=1, source_target_pairs={{8,0},{16,24},{9,1},{17,25},{10,2},{18,26},{11,3},{19,27},{12,4},{... | collective-permute-start | bytes 786440 | tf_op jit(solution)/shard_map/ppermute | solution.py:533
  170.5 35.5 %collective-permute-start.12 = (s32[1,8,8192]{2,1,0:T(8,128)S(1)}, s32[1,8,8192]{2,1,0:T(8,128)S(1)}, u32[]{:S(2)}, u32[]{:S(2)}) collective-permute-start(s32[1,8,8192]{2,1,0:T(8,128)S(1)} %forward.9), channel_id=1, source_target_pairs={{8,0},{16,24},{9,1},{17,25},{10,2},{18,26},{11,3},{19,27},{12,4},{... | collective-permute-start | bytes 786440 | tf_op jit(solution)/shard_map/ppermute | solution.py:533
  174.1 35.7 %collective-permute-start.9 = (s32[1,8,8192]{2,1,0:T(8,128)S(1)}, s32[1,8,8192]{2,1,0:T(8,128)S(1)}, u32[]{:S(2)}, u32[]{:S(2)}) collective-permute-start(s32[1,8,8192]{2,1,0:T(8,128)S(1)} %forward.8), channel_id=1, source_target_pairs={{8,0},{16,24},{9,1},{17,25},{10,2},{18,26},{11,3},{19,27},{12,4},{... | collective-permute-start | bytes 786440 | tf_op jit(solution)/shard_map/ppermute | solution.py:533

commit v2 on v1

v2 whole, which is shorter than its diff:
```python
import functools

import jax
import jax.numpy as jnp
from jax import lax
from jax.experimental import pallas as pl
from jax.experimental.pallas import tpu as pltpu
from jax.sharding import PartitionSpec as P

LANES = 128
MIB = 1024 * 1024
HERE = pl.BlockSpec(memory_space=pltpu.VMEM)
FAR = pl.BlockSpec(memory_space=pl.ANY)
SCALARS = pl.BlockSpec(memory_space=pltpu.SMEM)


def log2(number):
    assert number & (number - 1) == 0
    return number.bit_length() - 1


def pack_pair(first, second):
    return first | lax.shift_left(second, 16)


def halves(word):
    return word & 0xFFFF, lax.shift_right_logical(word, 16)


def centred(amount, modulus, inverse):
    return amount - jnp.round(amount * inverse) * modulus


def residue(amount, modulus, inverse):
    remain = centred(amount, modulus, inverse)
    return jnp.where(remain < 0, remain + modulus, remain)


def join_residues(first, second, modulus):
    total = first + second
    less = total - modulus
    return jnp.where(less < 0, total, less)


def spread(column, width):
    return jnp.concatenate([column] * (width // LANES), axis=1)


def params(limit):
    return pltpu.CompilerParams(vmem_limit_bytes=limit * MIB)


def cost(elements, ops, moved):
    return pl.CostEstimate(flops=elements * ops, bytes_accessed=moved, transcendentals=0)


def loop(count, body):
    lax.fori_loop(0, count, lambda step, carry: (body(step), carry)[1], 0)


def span_of(step, tile):
    return pl.ds(pl.multiple_of(step * tile, tile), tile)


def constants(limit):
    return lambda number: jnp.full(limit, number, jnp.int32).astype(jnp.float32)


def build_tables(place, levels, moduli, inverse, cross, columns, targets, weights):
    group, home = place[0], place[1]
    limbs, block = columns.shape[1], columns.shape[2]
    source_count = inverse.shape[0]
    lane = lax.broadcasted_iota(jnp.int32, (block, source_count), 1)
    rank = lax.broadcasted_iota(jnp.int32, (block, source_count), 0)
    own_levels = [levels[home * block + n] for n in range(block)]
    level_rank = jnp.zeros((block, source_count), jnp.int32)
    for n, level in enumerate(own_levels):
        level_rank = jnp.where(rank == n, level - 1, level_rank)
    onehot = jnp.where(lane == level_rank, 1.0, 0.0).astype(jnp.bfloat16)

    def bytes_of(table):
        parts = (table & 0xFF, lax.shift_right_logical(table, 8))
        return [part.astype(jnp.float32).astype(jnp.bfloat16) for part in parts]

    def product(left, right):
        return jnp.dot(left, right, preferred_element_type=jnp.float32)

    inverse_low, inverse_high = (product(onehot, part) for part in bytes_of(inverse[...]))
    inverse_rows = jnp.where(lane <= level_rank, inverse_low + 256.0 * inverse_high, 0.0)
    live_rows = jnp.where(lane <= level_rank, 1.0, 0.0)
    total = targets.shape[1]
    quarter = total // 4
    shape = (block, LANES)
    fill = constants(shape)
    for limb in range(limbs):
        index = group * limbs + limb
        here = lane == index
        picked = jnp.sum(jnp.where(here, inverse_rows, 0.0), axis=1, keepdims=True)
        picked = jnp.broadcast_to(picked, shape)
        live = jnp.broadcast_to(jnp.sum(jnp.where(here, live_rows, 0.0), axis=1, keepdims=True), shape)
        high = jnp.floor((picked + 128.0) * (1.0 / 256.0))
        modulus = fill(moduli[index])
        columns[0, limb] = high
        columns[1, limb] = picked - 256.0 * high
        columns[2, limb] = live / modulus
        columns[3, limb] = modulus
        columns[4, limb] = 1.0 / modulus

    left = group < 2
    inner = (group == 1) | (group == 2)
    order = (jnp.where(left, 2, 1), jnp.where(left, 3, 0), group ^ 1, group)
    rows = []
    for target in range(total):
        index = order[target // quarter] * quarter + target % quarter
        rows += [product(onehot, part) for part in bytes_of(cross[:, index, :])]
    width = weights.shape[1]
    entry = lax.broadcasted_iota(jnp.int32, (source_count, width), 0)
    column = lax.broadcasted_iota(jnp.int32, (source_count, width), 1)
    received = lax.shift_right_logical(column, log2(2 * block * limbs))
    limb = lax.shift_right_logical(column, log2(2 * block)) & (limbs - 1)
    limb = limb + jnp.where(received == 0, group * limbs, (group ^ 1) * limbs)
    choose = jnp.where(entry == limb, 1.0, 0.0).astype(jnp.bfloat16)
    chosen = product(jnp.concatenate(rows, axis=0).astype(jnp.bfloat16), choose)
    column = lax.broadcasted_iota(jnp.int32, (block, width), 1)
    same = (column & (block - 1)) == lax.broadcasted_iota(jnp.int32, (block, width), 0)
    upper = (lax.shift_right_logical(column, log2(block)) & 1) == 1
    from_outer = lax.shift_right_logical(column, log2(2 * block * limbs)) == 1
    results = []
    for target in range(total):
        index = order[target // quarter] * quarter + target % quarter
        modulus = fill(moduli[source_count + index])
        inverse_modulus = 1.0 / modulus
        targets[0, target] = modulus
        targets[1, target] = inverse_modulus
        modulus, inverse_modulus = spread(modulus, width), spread(inverse_modulus, width)
        first = 2 * target * block
        value = chosen[first : first + block] + 256.0 * chosen[first + block : first + 2 * block]
        value = jnp.where(upper, residue(256.0 * value, modulus, inverse_modulus), value)
        use = jnp.where(inner, 1, 0) if target // quarter != 2 else 0
        value = jnp.where(same & ((from_outer == False) | (use > 0)), value, 0.0)
        high_byte = jnp.floor(value * (1.0 / 256.0))
        results += [value - 256.0 * high_byte, high_byte]
    weights[...] = jnp.concatenate(results, axis=0).astype(jnp.bfloat16)


def scale_tile(values, columns, stage, scaled, read, write, local):
    width = write.size
    for word in range(scaled.shape[0]):
        if values.dtype == jnp.int32:
            pair = halves(values[word, :, read])
        else:
            pair = (values[2 * word, :, read], values[2 * word + 1, :, read])
        results = []
        for side, value in enumerate(pair):
            limb = 2 * word + side
            value = value.astype(jnp.float32)
            high, low, share, modulus, inverse = (spread(columns[kind, limb], width) for kind in range(5))
            if stage is not None:
                stage[limb, :, local] = value * share
            upper = centred(value * high, modulus, inverse)
            results.append(residue(256.0 * upper + value * low, modulus, inverse).astype(jnp.int32))
        scaled[word, :, write] = pack_pair(*results)


def out_copy(stage, out, start, step, tile, sem):
    return pltpu.make_async_copy(
        stage.at[:, :, span_of(step, tile)],
        out.at[:, :, pl.ds(pl.multiple_of(start + step * tile, tile), tile)],
        sem.at[step],
    )


def first_kernel(place, *rest):
    tables, residues = rest[:4], rest[4]
    columns, targets, weights, source, scaled = rest[5:10]
    landing, stage, *copies = rest[10:-3]
    sems, out_sems, table_sems = rest[-3:]
    block, width = stage.shape[1:]
    tile = width // sems.shape[0]
    home = place[1]
    start = home * residues.shape[2]

    def load(step):
        return pltpu.make_async_copy(
            residues.at[:, pl.ds(pl.multiple_of(home * block, block), block), span_of(step, tile)],
            landing.at[:, :, span_of(step, tile)],
            sems.at[step],
        )

    def store(step):
        return out_copy(stage, source, start, step, tile, out_sems)

    steps = width // tile
    fetches = [pltpu.make_async_copy(a, b, table_sems.at[i]) for i, (a, b) in enumerate(zip(tables, copies))]
    for fetch in fetches:
        fetch.start()
    loop(steps, lambda step: load(step).start())
    for fetch in fetches:
        fetch.wait()
    build_tables(place, *copies, columns, targets, weights)

    def body(step):
        load(step).wait()
        span = span_of(step, tile)
        scale_tile(landing, columns, stage, scaled, span, span, span)
        store(step).start()

    loop(steps, body)
    loop(steps, lambda step: store(step).wait())


def tile_of(width):
    return min(width, 1024)


def first(place, levels, moduli, inverse_table, cross, residues, block, count, length):
    limbs, _, width = residues.shape
    source_count = inverse_table.shape[0]
    total = moduli.shape[0] - source_count
    steps = length // tile_of(length)
    return pl.pallas_call(
        first_kernel,
        in_specs=[SCALARS] + [FAR] * 5,
        out_specs=[HERE, HERE, HERE, FAR, HERE],
        out_shape=[
            pltpu.VMEM((5, limbs, block, LANES), jnp.float32),
            pltpu.VMEM((2, total, block, LANES), jnp.float32),
            pltpu.VMEM((2 * total * block, 4 * limbs * block), jnp.bfloat16),
            jax.ShapeDtypeStruct((limbs, block, width * count), jnp.float32),
            pltpu.VMEM((limbs // 2, block, length), jnp.int32),
        ],
        scratch_shapes=[
            pltpu.VMEM((limbs, block, length), jnp.float32),
            pltpu.VMEM((limbs, block, length), jnp.float32),
            pltpu.SMEM(levels.shape, jnp.int32),
            pltpu.SMEM(moduli.shape, jnp.int32),
            pltpu.VMEM(inverse_table.shape, jnp.int32),
            pltpu.VMEM(cross.shape, jnp.int32),
            pltpu.SemaphoreType.DMA((steps,)),
            pltpu.SemaphoreType.DMA((steps,)),
            pltpu.SemaphoreType.DMA((4,)),
        ],
        compiler_params=params(8),
        cost_estimate=cost(limbs * block * length, 60, 10 * limbs * block * length),
        name="first",
    )(place, *(far(x) for x in (levels, moduli, inverse_table, cross, residues)))


def far(array):
    return pltpu.with_memory_space_constraint(array, pltpu.HBM)


def pack_kernel(offsets, place, residues, *rest):
    outs, (landing, sems) = rest[:-2], rest[-2:]
    _, _, block, width = landing.shape
    tile = tile_of(width)

    def load(turn):
        peer = place[1] ^ offsets[turn]
        return pltpu.make_async_copy(
            residues.at[:, pl.ds(pl.multiple_of(peer * block, block), block), :], landing.at[turn], sems.at[turn]
        )

    for turn in range(len(outs)):
        load(turn).start()
    for turn, out in enumerate(outs):
        load(turn).wait()

        def body(step):
            span = span_of(step, tile)
            for word in range(out.shape[0]):
                one = landing[turn, 2 * word, :, span].astype(jnp.int32)
                two = landing[turn, 2 * word + 1, :, span].astype(jnp.int32)
                out[word, :, span] = pack_pair(one, two)

        loop(width // tile, body)


def pack_blocks(place, residues, offsets, block):
    limbs, _, width = residues.shape
    peers = len(offsets)
    return pl.pallas_call(
        functools.partial(pack_kernel, offsets),
        in_specs=[SCALARS, FAR],
        out_specs=[HERE] * peers,
        out_shape=[pltpu.VMEM((limbs // 2, block, width), jnp.int32)] * peers,
        scratch_shapes=[
            pltpu.VMEM((peers, limbs, block, width), jnp.float32),
            pltpu.SemaphoreType.DMA((peers,)),
        ],
        compiler_params=params(12),
        cost_estimate=cost(peers * limbs * block * width, 16, 6 * peers * limbs * block * width),
        name="pack",
    )(place, residues)


def scale_kernel(chunk, relay, emit, place, columns, targets, *rest):
    offsets, low, high = chunk
    values, rest = rest[: len(offsets)], rest[len(offsets) :]
    if relay:
        outer, arrived, *rest = rest
    if emit:
        source, scaled, *rest = rest[1:]
        stage, sems = rest[-2:]
    else:
        scaled, *rest = rest
    send = rest[0] if relay else None
    width = values[0].shape[2]
    length = high - low
    tile = tile_of(length)
    steps = length // tile
    inner = (place[0] == 1) | (place[0] == 2)
    stores = []
    for turn, offset in enumerate(offsets):
        start = (place[1] ^ offset) * width + low

        def store(step, turn=turn, start=start):
            return out_copy(stage.at[turn], source, start, step, tile, sems.at[turn])

        def body(step):
            write = pl.ds(pl.multiple_of(turn * length + step * tile, tile), tile)
            read = pl.ds(pl.multiple_of(low + step * tile, tile), tile)
            local = span_of(step, tile)
            scale_tile(values[turn], columns, stage.at[turn] if emit else None, scaled, read, write, local)
            if relay:
                for word in range(send.shape[0]):
                    words = scaled[word, :, write]
                    if word < outer.shape[0]:
                        words = jnp.where(inner, relay_word(targets, outer, arrived, word, write), words)
                    send[word, :, write] = words
            if emit:
                store(step).start()

        loop(steps, body)
        stores.append(store)
    if emit:
        for store in stores:
            loop(steps, lambda step: store(step).wait())


def scale_chunk(place, columns, targets, values, chunk, source, relay=None):
    words, block, _ = values[0].shape
    _, low, high = chunk
    length = high - low
    parts = len(values)
    limbs = 2 * words
    emit = source is not None
    operands = [place, columns, targets, *values, *(relay or ())]
    in_specs = [SCALARS] + [HERE] * (len(operands) - 1)
    whole = pltpu.VMEM((words, block, length * parts), jnp.int32)
    out_shape, out_specs, scratch, aliases = [whole], [HERE], [], {}
    if relay:
        out_shape, out_specs = out_shape + [whole], out_specs + [HERE]
    if emit:
        aliases = {len(operands): 0}
        operands.append(source)
        in_specs.append(FAR)
        out_shape = [jax.ShapeDtypeStruct(source.shape, jnp.float32)] + out_shape
        out_specs = [FAR] + out_specs
        scratch = [
            pltpu.VMEM((parts, limbs, block, length), jnp.float32),
            pltpu.SemaphoreType.DMA((parts, length // tile_of(length))),
        ]
    results = pl.pallas_call(
        functools.partial(scale_kernel, chunk, relay is not None, emit),
        in_specs=in_specs,
        out_specs=out_specs,
        out_shape=out_shape,
        scratch_shapes=scratch,
        input_output_aliases=aliases,
        compiler_params=params(8),
        cost_estimate=cost(parts * limbs * block * length, 40, 8 * parts * limbs * block * length),
        name="scale",
    )(*operands)
    if emit:
        source, *results = results
    scaled = results[0]
    return source, scaled, results[1] if relay else scaled


def spread_kernel(pieces, place, columns, *rest):
    values = rest[: len(pieces)]
    source, stage, sems = rest[-3:]
    tile = stage.shape[3]
    stores = []
    for turn, (offset, low, high, width) in enumerate(pieces):
        steps = (high - low) // tile
        base = sum((p[2] - p[1]) // tile for p in pieces[:turn])

        def store(step, base=base, offset=offset, low=low, width=width):
            return pltpu.make_async_copy(
                stage.at[base + step],
                source.at[:, :, pl.ds(pl.multiple_of((place[1] ^ offset) * width + low + step * tile, tile), tile)],
                sems.at[base + step],
            )

        def body(step):
            read = pl.ds(pl.multiple_of(low + step * tile, tile), tile)
            for word in range(values[turn].shape[0]):
                for side, value in enumerate(halves(values[turn][word, :, read])):
                    limb = 2 * word + side
                    stage[base + step, limb] = value.astype(jnp.float32) * spread(columns[2, limb], tile)
            store(step).start()

        loop(steps, body)
        stores.append((steps, store))
    for steps, store in stores:
        loop(steps, lambda step: store(step).wait())


def spread_blocks(place, columns, values, pieces, source):
    words, block, width = values[0].shape
    tile = min(tile_of(high - low) for _, low, high in pieces)
    pieces = tuple((offset, low, high, width) for offset, low, high in pieces)
    slots = sum((high - low) // tile for _, low, high, _ in pieces)
    operands = [place, columns, *values, source]
    return pl.pallas_call(
        functools.partial(spread_kernel, pieces),
        in_specs=[SCALARS] + [HERE] * (len(operands) - 2) + [FAR],
        out_specs=FAR,
        out_shape=jax.ShapeDtypeStruct(source.shape, jnp.float32),
        scratch_shapes=[
            pltpu.VMEM((slots, 2 * words, block, tile), jnp.float32),
            pltpu.SemaphoreType.DMA((slots,)),
        ],
        input_output_aliases={len(operands) - 1: 0},
        compiler_params=params(12),
        cost_estimate=cost(slots * 2 * words * block * tile, 20, 6 * slots * 2 * words * block * tile),
        name="spread",
    )(*operands)


def mix_kernel(targets, weights, own, received, far_out, outer_out, mine_out):
    block = own.shape[1]
    tile = min(own.shape[2], 2048)

    def body(step):
        span = span_of(step, tile)
        digits = []
        for words in (own, received):
            for word in range(words.shape[0]):
                value = words[word, :, span]
                for byte in range(4):
                    part = lax.shift_right_logical(value, 8 * byte) if byte else value
                    if byte < 3:
                        part = part & 0xFF
                    digits.append(part.astype(jnp.float32))
        stacked = jnp.concatenate(digits, axis=0).astype(jnp.bfloat16)
        sums = jnp.dot(weights[...], stacked, preferred_element_type=jnp.float32)
        reduced = []
        for target in range(targets.shape[1]):
            modulus, inverse = spread(targets[0, target], tile), spread(targets[1, target], tile)
            low = sums[2 * target * block : (2 * target + 1) * block]
            high = sums[(2 * target + 1) * block : (2 * target + 2) * block]
            upper = centred(high, modulus, inverse)
            reduced.append(residue(256.0 * upper + low, modulus, inverse).astype(jnp.int32))
        words = [pack_pair(reduced[t], reduced[t + 1]) for t in range(0, len(reduced), 2)]
        position = 0
        for out in (far_out, outer_out, mine_out):
            for word in range(out.shape[0]):
                out[word, :, span] = words[position]
                position += 1

    loop(own.shape[2] // tile, body)


def mix_chunk(own, received, weights, targets):
    words, block, length = own.shape
    total = targets.shape[1]
    counts = (total // 4, total // 8, total // 8)
    return pl.pallas_call(
        mix_kernel,
        in_specs=[HERE] * 4,
        out_specs=[HERE] * 3,
        out_shape=[pltpu.VMEM((count, block, length), jnp.int32) for count in counts],
        compiler_params=params(8),
        cost_estimate=cost(total * block * length, 40, 4 * (2 * words + 4) * block * length),
        name="mix",
    )(targets, weights, own, received)


def relay_word(targets, outer, arrived, word, span):
    words = outer.shape[0]
    results = []
    for side, (a, b) in enumerate(zip(halves(outer[word, :, span]), halves(arrived[words + word, :, span]))):
        modulus = spread(targets[0, 4 * words + 2 * word + side].astype(jnp.int32), span.size)
        results.append(join_residues(a, b, modulus))
    return pack_pair(*results)


def forward_kernel(targets, outer, arrived, out):
    tile = tile_of(out.shape[2])

    def body(step):
        span = span_of(step, tile)
        for word in range(out.shape[0]):
            out[word, :, span] = relay_word(targets, outer, arrived, word, span)

    loop(out.shape[2] // tile, body)


def forward_chunk(outer, arrived, targets):
    words, block, length = outer.shape
    return pl.pallas_call(
        forward_kernel,
        in_specs=[HERE] * 3,
        out_specs=HERE,
        out_shape=pltpu.VMEM(outer.shape, jnp.int32),
        compiler_params=params(4),
        cost_estimate=cost(words * block * length, 40, 12 * words * block * length),
        name="forward",
    )(targets, outer, arrived)


def finish_kernel(chunks, full, place, targets, *rest):
    out, stage, sems = rest[-3:]
    tile = stage.shape[3]
    inner = (place[0] == 1) | (place[0] == 2)
    stores = []
    slot = 0
    for turn, (offsets, low, high) in enumerate(chunks):
        mine, arrived, relayed = rest[3 * turn : 3 * turn + 3]
        first_target = 6 * mine.shape[0]
        steps = (high - low) // tile
        for part, offset in enumerate(offsets):

            def store(step, offset=offset, low=low, base=slot):
                start = (place[1] ^ offset) * full + low
                return pltpu.make_async_copy(
                    stage.at[base + step],
                    out.at[:, :, pl.ds(pl.multiple_of(start + step * tile, tile), tile)],
                    sems.at[base + step],
                )

            def body(step):
                span = pl.ds(pl.multiple_of(part * (high - low) + step * tile, tile), tile)
                for word in range(mine.shape[0]):
                    other = jnp.where(inner, arrived[word, :, span], relayed[word, :, span])
                    for side, (a, b) in enumerate(zip(halves(mine[word, :, span]), halves(other))):
                        target = first_target + 2 * word + side
                        modulus = spread(targets[0, target].astype(jnp.int32), tile)
                        total = join_residues(a, b, modulus).astype(jnp.float32)
                        stage[slot + step, 2 * word + side] = total * spread(targets[1, target], tile)
                store(step).start()

            loop(steps, body)
            stores.append((steps, store))
            slot += steps
    for steps, store in stores:
        loop(steps, lambda step: store(step).wait())


def finish_chunks(place, targets, triples, chunks, shape, full, buffer):
    words, block, _ = triples[0][0].shape
    tile = min(tile_of(high - low) for _, low, high in chunks)
    slots = sum(len(offsets) * (high - low) // tile for offsets, low, high in chunks)
    operands = [place, targets, *(array for triple in triples for array in triple)]
    in_specs = [SCALARS] + [HERE] * (len(operands) - 1)
    aliases = {}
    if buffer is not None:
        aliases[len(operands)] = 0
        operands.append(buffer)
        in_specs.append(FAR)
    return pl.pallas_call(
        functools.partial(finish_kernel, chunks, full),
        in_specs=in_specs,
        out_specs=FAR,
        out_shape=jax.ShapeDtypeStruct(shape, jnp.float32),
        scratch_shapes=[
            pltpu.VMEM((slots, 2 * words, block, tile), jnp.float32),
            pltpu.SemaphoreType.DMA((slots,)),
        ],
        input_output_aliases=aliases,
        compiler_params=params(8),
        cost_estimate=cost(2 * words * block * slots * tile, 20, 10 * 2 * words * block * slots * tile),
        name="finish",
    )(*operands)


def chunk_plan(count, width):
    if count == 8:
        return [((offset,), 0, width) for offset in (0, 1, 2, 4, 3, 5, 6, 7)]
    unit = max(1, count // 8)
    edges = sorted({0, 1} | set(range(unit, count + 1, unit)))
    return [(tuple(range(start, end)), 0, width) for start, end in zip(edges, edges[1:])]


LAG = 3
LATE = 4


def length_of(chunk):
    return len(chunk[0]) * (chunk[2] - chunk[1])


def riders(plan):
    return {
        step: step - LAG
        for step in range(LAG, len(plan))
        if length_of(plan[step]) == length_of(plan[step - LAG])
    }


def timeline(plan):
    steps = len(plan)
    ride = riders(plan)
    events = ["first", "a0", "pack"]
    order = list(dict.fromkeys(offset for chunk in plan for offset in chunk[0] if offset))
    ready = list(dict.fromkeys(offset for chunk in plan[:4] for offset in chunk[0] if offset))
    events += [f"p{offset}" for offset in ready]
    events += ["scale1", "a1"] + [f"p{offset}" for offset in order if offset not in ready]
    alone = [step for step in range(steps) if step not in ride.values()]
    for step in range(steps):
        events += [f"mix{step}", f"b{step}"]
        if step + 2 < steps:
            events += [f"scale{step + 2}", f"a{step + 2}"]
        if step - 1 in alone:
            events += [f"forward{step - 1}", f"c{step - 1}"]
    joined = [step for step in range(steps) if step not in alone]
    tail = steps - 1
    events[events.index(f"b{tail}") + 1 : events.index(f"b{tail}") + 1] = ["spread"]
    events += ["finish" + "_".join(map(str, joined + alone[:-2]))]
    events += [f"forward{tail}", f"c{tail}", f"finish{tail - 1}", f"finish{tail}"]
    return events


def late(plan):
    return set(range(len(plan) - LATE, len(plan)))


def per_device(residues, levels, moduli, inverse_table, cross_table):
    target_count = cross_table.shape[2]
    _, _, width = residues.shape
    count = lax.axis_size("coef")
    assert lax.axis_size("limb") == 4
    block = residues.shape[1] // count
    place = jnp.stack([lax.axis_index("limb"), lax.axis_index("coef")]).astype(jnp.int32)
    cross = jnp.transpose(cross_table, (0, 2, 1))
    plan = chunk_plan(count, width)
    steps = len(plan)
    ride = riders(plan)

    scaled, send, received, mixed, crossed, relayed = ([None] * steps for _ in range(6))
    arrived = {}
    packed = {}
    result = None
    shape = (target_count // 4, block, width * count)
    for event in timeline(plan):
        kind = event.rstrip("0123456789_")
        step = int(event[len(kind) :] or 0) if "_" not in event else 0
        if kind == "first":
            columns, targets, weights, source, scaled[0] = first(
                place, levels, moduli, inverse_table, cross, residues, block, count, plan[0][2]
            )
            send[0] = scaled[0]
        elif kind == "pack":
            offsets = tuple(range(1, count))
            packed = dict(zip(offsets, pack_blocks(place, far(residues), offsets, block)))
        elif kind == "p":
            arrived[step] = lax.ppermute(packed[step], "coef", [(i, i ^ step) for i in range(count)])
        elif kind == "scale":
            values = [arrived[offset] for offset in plan[step][0]]
            relay = (mixed[ride[step]][1], crossed[ride[step]]) if step in ride else None
            buffer = None if step in late(plan) else source
            buffer, scaled[step], send[step] = scale_chunk(place, columns, targets, values, plan[step], buffer, relay)
            source = source if step in late(plan) else buffer
        elif kind == "a":
            pairs = [(0, 1), (3, 2)] + ([(1, 0), (2, 3)] if step in ride else [])
            received[step] = lax.ppermute(send[step], "limb", pairs)
            if step in ride:
                relayed[ride[step]] = received[step]
        elif kind == "mix":
            mixed[step] = mix_chunk(scaled[step], received[step], weights, targets)
        elif kind == "b":
            crossed[step] = lax.ppermute(mixed[step][0], "limb", [(1, 2), (2, 1)])
        elif kind == "forward":
            relayed[step] = forward_chunk(mixed[step][1], crossed[step], targets)
        elif kind == "c":
            relayed[step] = lax.ppermute(relayed[step], "limb", [(1, 0), (2, 3)])
        elif kind == "spread":
            pieces = [(offset, low, high) for i in sorted(late(plan)) for offset, low, high in [(o, *plan[i][1:]) for o in plan[i][0]]]
            source = spread_blocks(place, columns, [arrived[p[0]] for p in pieces], pieces, source)
        else:
            chosen = [int(i) for i in event[len(kind) :].split("_")]
            triples = [(mixed[i][2], crossed[i], relayed[i]) for i in chosen]
            result = finish_chunks(
                place, targets, triples, tuple(plan[i] for i in chosen), shape, width, result
            )
    return (source, result)


def solution(mesh):
    placed = (P("limb", None, "coef"), P(), P(), P(), P())

    return jax.shard_map(
        per_device,
        mesh=mesh,
        in_specs=placed,
        out_specs=(P("limb", "coef", None), P("limb", "coef", None)),
        check_vma=False,
    )
```

time: 212 us -> 160 us (0.75)
  waiting for transfers between devices: 106 us -> 67.5 us
  Pallas kernels: 55.7 us -> 42.4 us
    ppermute x8 -> x3, waiting for transfers between devices: 38.6 us -> 10.2 us  [per_device(): relayed[step] = lax.ppermute(relayed[step], 'limb', [(1, 0), (2, 3)])]
    ppermute x7, waiting for transfers between devices: 21.8 us -> 10.4 us  [per_device(): lax.ppermute(packed[step], 'coef', [(i, i ^ step) for i in range(count)])]
    ppermute x8, starting transfers between devices: 24.2 us -> 31.4 us  [per_device(): received[step] = lax.ppermute(send[step], 'limb', pairs)]
    pallas_call x24 -> x15, Pallas kernels: 30.7 us -> 24.2 us  [the longest x7 11.7 us: scale_chunk(): pl.pallas_call(functools.partial(scale_kernel, chunk, relay is not None,...]
    ppermute x8 -> x3, starting transfers between devices: 10.3 us -> 3.88 us  [per_device(): relayed[step] = lax.ppermute(relayed[step], 'limb', [(1, 0), (2, 3)])]
    pallas_call x8, Pallas kernels: 19.7 us -> 14.3 us  [mix_chunk(): pl.pallas_call(mix_kernel, in_specs=[HERE] * 4, out_specs=[HERE] * 3, out...]
  transfers between devices with their start and end apart: 31 -> 26, of which waited for: 17 -> 12; matrix products, arithmetic and copies ran while one was open for 0% -> 0% of each run, Pallas kernels for 23% -> 23%
where the time goes in v2:
time: 160 us; the launch traced here: 159 us
  waiting for transfers between devices  67.5 us (42%)
  starting transfers between devices  48.2 us (30%)
  Pallas kernels  42.4 us (26%)
    ppermute x8, waiting for transfers between devices, per_device(): received[step] = lax.ppermute(send[step], 'limb', pairs)  46.8 us
    ppermute x8, starting transfers between devices, per_device(): received[step] = lax.ppermute(send[step], 'limb', pairs)  31.4 us
    pallas_call x8, Pallas kernels, mix_chunk(): pl.pallas_call(mix_kernel, in_specs=[HERE] * 4, out_specs=[HERE] * 3, out...  14.3 us
    pallas_call x7, Pallas kernels, scale_chunk(): pl.pallas_call(functools.partial(scale_kernel, chunk, relay is not None,...  11.7 us
    ppermute x7, waiting for transfers between devices, per_device(): lax.ppermute(packed[step], 'coef', [(i, i ^ step) for i in range(count)])  10.4 us
    ppermute x3, waiting for transfers between devices, per_device(): relayed[step] = lax.ppermute(relayed[step], 'limb', [(1, 0), (2, 3)])  10.2 us
    ppermute x7, starting transfers between devices, per_device(): lax.ppermute(packed[step], 'coef', [(i, i ^ step) for i in range(count)])  7.41 us
    pallas_call x3, Pallas kernels, finish_chunks(): pl.pallas_call(functools.partial(finish_kernel, chunks, full), in_specs=i...  5.79 us
  transfers between devices with their start and end apart: 26, of which 12 were waited for; matrix products, arithmetic and copies ran while one was open for 0% of the time, Pallas kernels for 23%

profile of v2, /device:TPU:0, one launch (start us, length us, event | category | flops | bytes accessed | tf_op | source)
XLA Modules:
  0.0 159.1 jit_solution(17483696765772575696)
XLA Ops:
  0.6 0.1 pad_add_fusion.place
  0.7 3.9 %pack.1 = (s32[2,8,8192]{2,1,0:T(8,128)S(1)}, s32[2,8,8192]{2,1,0:T(8,128)S(1)}, s32[2,8,8192]{2,1,0:T(8,128)S(1)}, s32[2,8,8192]{2,1,0:T(8,128)S(1)}, s32[2,8,8...) custom-call(s32[2]{0:T(128)S(1)} %pad_add_fusion.place, f32[4,64,8192]{2,1,0:T(8,128)} %residues.1), custom_call_target="tpu_custom_call" | custom-call | flops 29360128 | bytes 11010048 | tf_op jit(solution)/shard_map/pack/pallas_call | solution.py:282
  4.6 0.6 collective-permute-start.8
  5.1 3.4 %first.1 = (f32[5,4,8,128]{3,2,1,0:T(8,128)S(1)}, f32[2,8,8,128]{3,2,1,0:T(8,128)S(1)}, bf16[128,128]{1,0:T(8,128)(2,1)S(1)}, f32[4,8,65536]{2,1,0:T(8,128)}, s32[2,8,8192]{2,1,0:T(8,128)S(1)}) custom-call(s32[2]{0:T(128)S(1)} %pad_add_fusion.place, s32[64]{0:T(128)} %rest_0_.1, s32[24]{0:T(128)} %rest_1_.1, s32[16,16]{1,0:T(8,128)} %rest_2_.1, ...), custom_call_target="tpu_custom_call" | custom-call | flops 15728640 | bytes 2621440 | tf_op jit(solution)/shard_map/first/pallas_call | solution.py:221
  8.5 4.5 %collective-permute-start.5 = (s32[2,8,8192]{2,1,0:T(8,128)S(1)}, s32[2,8,8192]{2,1,0:T(8,128)S(1)}, u32[]{:S(2)}, u32[]{:S(2)}) collective-permute-start(s32[2,8,8192]{2,1,0:T(8,128)S(1)} %get-tuple-element.61.own), channel_id=1, source_target_pairs={{0,8},{24,16},{1,9},{25,17},{2,10},{26,18},{3,11},{27,19},{4,12},{... | collective-permute-start | bytes 1572872 | tf_op jit(solution)/shard_map/ppermute | solution.py:669
  13.0 0.0 collective-permute-done.8.rest_0_
  13.0 2.0 %scale.7 = (f32[4,8,65536]{2,1,0:T(8,128)}, s32[2,8,8192]{2,1,0:T(8,128)S(1)}) custom-call(s32[2]{0:T(128)S(1)} %pad_add_fusion.place, f32[5,4,8,128]{3,2,1,0:T(8,128)S(1)} %get-tuple-element.53.columns, f32[2,8,8,128]{3,2,1,0:T(8,128)S(1)} %get-tuple-element.58.targets, ...), custom_call_target="tpu_custom_call", output_to_operand_aliasing={{0}: (4, {})} | custom-call | flops 10485760 | bytes 2097152 | tf_op jit(solution)/shard_map/scale/pallas_call | solution.py:364
  15.0 1.3 collective-permute-start.9
  16.4 1.6 collective-permute-start.4
  17.9 1.5 collective-permute-start.7
  19.4 5.9 %collective-permute-done.5.received = s32[2,8,8192]{2,1,0:T(8,128)S(1)} collective-permute-done((s32[2,8,8192]{2,1,0:T(8,128)S(1)}, s32[2,8,8192]{2,1,0:T(8,128)S(1)}, u32[]{:S(2)}, u32[]{:S(2)}) %collective-permute-start.5) | collective-permute-done | bytes 524320 | tf_op jit(solution)/shard_map/ppermute | solution.py:669
  25.3 1.8 %mix.8 = (s32[2,8,8192]{2,1,0:T(8,128)S(1)}, s32[1,8,8192]{2,1,0:T(8,128)S(1)}, s32[1,8,8192]{2,1,0:T(8,128)S(1)}) custom-call(f32[2,8,8,128]{3,2,1,0:T(8,128)S(1)} %get-tuple-element.58.targets, bf16[128,128]{1,0:T(8,128)(2,1)S(1)} %get-tuple-element.60.weights, s32[2,8,8192]{2,1,0:T(8,128)S(1)} %get-tuple-element.61.own, ...), custom_call_target="tpu_custom_call" | custom-call | flops 20971520 | bytes 2097152 | tf_op jit(solution)/shard_map/mix/pallas_call | solution.py:471
  27.1 0.7 collective-permute-start.6
  27.8 0.3 collective-permute-start
  28.1 7.9 %collective-permute-done.9.received = s32[2,8,8192]{2,1,0:T(8,128)S(1)} collective-permute-done((s32[2,8,8192]{2,1,0:T(8,128)S(1)}, s32[2,8,8192]{2,1,0:T(8,128)S(1)}, u32[]{:S(2)}, u32[]{:S(2)}) %collective-permute-start.9) | collective-permute-done | bytes 524320 | tf_op jit(solution)/shard_map/ppermute | solution.py:669
  36.0 1.8 %mix.9 = (s32[2,8,8192]{2,1,0:T(8,128)S(1)}, s32[1,8,8192]{2,1,0:T(8,128)S(1)}, s32[1,8,8192]{2,1,0:T(8,128)S(1)}) custom-call(f32[2,8,8,128]{3,2,1,0:T(8,128)S(1)} %get-tuple-element.58.targets, bf16[128,128]{1,0:T(8,128)(2,1)S(1)} %get-tuple-element.60.weights, s32[2,8,8192]{2,1,0:T(8,128)S(1)} %get-tuple-element.70.own, ...), custom_call_target="tpu_custom_call" | custom-call | flops 20971520 | bytes 2097152 | tf_op jit(solution)/shard_map/mix/pallas_call | solution.py:471
  37.8 0.7 collective-permute-start.10
  38.5 0.0 collective-permute-done.7.rest_0_
  38.6 2.0 %scale.8 = (f32[4,8,65536]{2,1,0:T(8,128)}, s32[2,8,8192]{2,1,0:T(8,128)S(1)}) custom-call(s32[2]{0:T(128)S(1)} %pad_add_fusion.place, f32[5,4,8,128]{3,2,1,0:T(8,128)S(1)} %get-tuple-element.53.columns, f32[2,8,8,128]{3,2,1,0:T(8,128)S(1)} %get-tuple-element.58.targets, ...), custom_call_target="tpu_custom_call", output_to_operand_aliasing={{0}: (4, {})} | custom-call | flops 10485760 | bytes 2097152 | tf_op jit(solution)/shard_map/scale/pallas_call | solution.py:364
  40.6 7.2 %collective-permute-start.21 = (s32[2,8,8192]{2,1,0:T(8,128)S(1)}, s32[2,8,8192]{2,1,0:T(8,128)S(1)}, u32[]{:S(2)}, u32[]{:S(2)}) collective-permute-start(s32[2,8,8192]{2,1,0:T(8,128)S(1)} %get-tuple-element.93.own), channel_id=1, source_target_pairs={{0,8},{24,16},{1,9},{25,17},{2,10},{26,18},{3,11},{27,19},{4,12},{... | collective-permute-start | bytes 1572872 | tf_op jit(solution)/shard_map/ppermute | solution.py:669
  47.8 2.1 %scale.9 = (f32[4,8,65536]{2,1,0:T(8,128)}, s32[2,8,8192]{2,1,0:T(8,128)S(1)}, s32[2,8,8192]{2,1,0:T(8,128)S(1)}) custom-call(s32[2]{0:T(128)S(1)} %pad_add_fusion.place, f32[5,4,8,128]{3,2,1,0:T(8,128)S(1)} %get-tuple-element.53.columns, f32[2,8,8,128]{3,2,1,0:T(8,128)S(1)} %get-tuple-element.58.targets, ...), custom_call_target="tpu_custom_call", output_to_operand_aliasing={{0}: (6, {})} | custom-call | flops 10485760 | bytes 2097152 | tf_op jit(solution)/shard_map/scale/pallas_call | solution.py:364
  49.9 0.1 collective-permute-start.16
  50.0 1.4 scale.10
  51.4 5.7 %collective-permute-start.11 = (s32[2,8,8192]{2,1,0:T(8,128)S(1)}, s32[2,8,8192]{2,1,0:T(8,128)S(1)}, u32[]{:S(2)}, u32[]{:S(2)}) collective-permute-start(s32[2,8,8192]{2,1,0:T(8,128)S(1)} %get-tuple-element.74), channel_id=1, source_target_pairs={{0,8},{24,16},{8,0},{16,24},{1,9},{25,17},{9,1},{17,25},{2,10},{26... | collective-permute-start | bytes 1572872 | tf_op jit(solution)/shard_map/ppermute | solution.py:669
  57.1 2.5 %collective-permute-start.2 = (s32[2,8,8192]{2,1,0:T(8,128)S(1)}, s32[2,8,8192]{2,1,0:T(8,128)S(1)}, u32[]{:S(2)}, u32[]{:S(2)}) collective-permute-start(s32[2,8,8192]{2,1,0:T(8,128)S(1)} %get-tuple-element.56), channel_id=1, source_target_pairs={{0,6},{1,7},{2,4},{3,5},{4,2},{5,3},{6,0},{7,1},{8,14},{9,15},{10,... | collective-permute-start | bytes 1572872 | tf_op jit(solution)/shard_map/ppermute | solution.py:660
  59.6 0.4 collective-permute-done.21.received
  60.0 1.0 collective-permute-start.3
  61.0 1.8 %mix.14 = (s32[2,8,8192]{2,1,0:T(8,128)S(1)}, s32[1,8,8192]{2,1,0:T(8,128)S(1)}, s32[1,8,8192]{2,1,0:T(8,128)S(1)}) custom-call(f32[2,8,8,128]{3,2,1,0:T(8,128)S(1)} %get-tuple-element.58.targets, bf16[128,128]{1,0:T(8,128)(2,1)S(1)} %get-tuple-element.60.weights, s32[2,8,8192]{2,1,0:T(8,128)S(1)} %get-tuple-element.93.own, ...), custom_call_target="tpu_custom_call" | custom-call | flops 20971520 | bytes 2097152 | tf_op jit(solution)/shard_map/mix/pallas_call | solution.py:471
  62.8 8.4 %collective-permute-done.16.received.rest_2_ = s32[2,8,8192]{2,1,0:T(8,128)S(1)} collective-permute-done((s32[2,8,8192]{2,1,0:T(8,128)S(1)}, s32[2,8,8192]{2,1,0:T(8,128)S(1)}, u32[]{:S(2)}, u32[]{:S(2)}) %collective-permute-start.16) | collective-permute-done | bytes 524320 | tf_op jit(solution)/shard_map/ppermute | solution.py:669
  71.3 0.7 collective-permute-start.22
  72.0 1.8 %mix.12 = (s32[2,8,8192]{2,1,0:T(8,128)S(1)}, s32[1,8,8192]{2,1,0:T(8,128)S(1)}, s32[1,8,8192]{2,1,0:T(8,128)S(1)}) custom-call(f32[2,8,8,128]{3,2,1,0:T(8,128)S(1)} %get-tuple-element.58.targets, bf16[128,128]{1,0:T(8,128)(2,1)S(1)} %get-tuple-element.60.weights, s32[2,8,8192]{2,1,0:T(8,128)S(1)} %get-tuple-element.82.own, ...), custom_call_target="tpu_custom_call" | custom-call | flops 20971520 | bytes 2097152 | tf_op jit(solution)/shard_map/mix/pallas_call | solution.py:471
  73.8 7.1 %collective-permute-done.11.received.rest_5_ = s32[2,8,8192]{2,1,0:T(8,128)S(1)} collective-permute-done((s32[2,8,8192]{2,1,0:T(8,128)S(1)}, s32[2,8,8192]{2,1,0:T(8,128)S(1)}, u32[]{:S(2)}, u32[]{:S(2)}) %collective-permute-start.11) | collective-permute-done | bytes 524320 | tf_op jit(solution)/shard_map/ppermute | solution.py:669
  80.9 0.7 collective-permute-start.17
  81.6 1.8 %mix.10 = (s32[2,8,8192]{2,1,0:T(8,128)S(1)}, s32[1,8,8192]{2,1,0:T(8,128)S(1)}, s32[1,8,8192]{2,1,0:T(8,128)S(1)}) custom-call(f32[2,8,8,128]{3,2,1,0:T(8,128)S(1)} %get-tuple-element.58.targets, bf16[128,128]{1,0:T(8,128)(2,1)S(1)} %get-tuple-element.60.weights, s32[2,8,8192]{2,1,0:T(8,128)S(1)} %get-tuple-element.73.own, ...), custom_call_target="tpu_custom_call" | custom-call | flops 20971520 | bytes 2097152 | tf_op jit(solution)/shard_map/mix/pallas_call | solution.py:471
  83.4 10.4 %collective-permute-done.1.rest_1_.rest_0_ = s32[2,8,8192]{2,1,0:T(8,128)S(1)} collective-permute-done((s32[2,8,8192]{2,1,0:T(8,128)S(1)}, s32[2,8,8192]{2,1,0:T(8,128)S(1)}, u32[]{:S(2)}, u32[]{:S(2)}) %collective-permute-start.1) | collective-permute-done | bytes 524320 | tf_op jit(solution)/shard_map/ppermute | solution.py:660
  93.8 0.7 collective-permute-start.12
  94.5 1.4 scale.13
  95.9 3.0 %collective-permute-start.23 = (s32[2,8,8192]{2,1,0:T(8,128)S(1)}, s32[2,8,8192]{2,1,0:T(8,128)S(1)}, u32[]{:S(2)}, u32[]{:S(2)}) collective-permute-start(s32[2,8,8192]{2,1,0:T(8,128)S(1)} %get-tuple-element.97), channel_id=1, source_target_pairs={{0,8},{24,16},{8,0},{16,24},{1,9},{25,17},{9,1},{17,25},{2,10},{26... | collective-permute-start | bytes 1572872 | tf_op jit(solution)/shard_map/ppermute | solution.py:669
  98.8 1.4 scale.12
  100.2 0.1 collective-permute-start.18
  100.3 1.4 scale.11
  101.7 9.5 %collective-permute-start.13 = (s32[2,8,8192]{2,1,0:T(8,128)S(1)}, s32[2,8,8192]{2,1,0:T(8,128)S(1)}, u32[]{:S(2)}, u32[]{:S(2)}) collective-permute-start(s32[2,8,8192]{2,1,0:T(8,128)S(1)} %get-tuple-element.78), channel_id=1, source_target_pairs={{0,8},{24,16},{8,0},{16,24},{1,9},{25,17},{9,1},{17,25},{2,10},{26... | collective-permute-start | bytes 1572872 | tf_op jit(solution)/shard_map/ppermute | solution.py:669
  111.2 0.4 collective-permute-done.23.received.rest_8_
  111.6 1.8 %mix.15 = (s32[2,8,8192]{2,1,0:T(8,128)S(1)}, s32[1,8,8192]{2,1,0:T(8,128)S(1)}, s32[1,8,8192]{2,1,0:T(8,128)S(1)}) custom-call(f32[2,8,8,128]{3,2,1,0:T(8,128)S(1)} %get-tuple-element.58.targets, bf16[128,128]{1,0:T(8,128)(2,1)S(1)} %get-tuple-element.60.weights, s32[2,8,8192]{2,1,0:T(8,128)S(1)} %get-tuple-element.100.own, ...), custom_call_target="tpu_custom_call" | custom-call | flops 20971520 | bytes 2097152 | tf_op jit(solution)/shard_map/mix/pallas_call | solution.py:471
  113.4 0.7 collective-permute-start.24
  114.1 8.7 %collective-permute-done.18.received.rest_11_ = s32[2,8,8192]{2,1,0:T(8,128)S(1)} collective-permute-done((s32[2,8,8192]{2,1,0:T(8,128)S(1)}, s32[2,8,8192]{2,1,0:T(8,128)S(1)}, u32[]{:S(2)}, u32[]{:S(2)}) %collective-permute-start.18) | collective-permute-done | bytes 524320 | tf_op jit(solution)/shard_map/ppermute | solution.py:669
  122.8 1.8 %mix.13 = (s32[2,8,8192]{2,1,0:T(8,128)S(1)}, s32[1,8,8192]{2,1,0:T(8,128)S(1)}, s32[1,8,8192]{2,1,0:T(8,128)S(1)}) custom-call(f32[2,8,8,128]{3,2,1,0:T(8,128)S(1)} %get-tuple-element.58.targets, bf16[128,128]{1,0:T(8,128)(2,1)S(1)} %get-tuple-element.60.weights, s32[2,8,8192]{2,1,0:T(8,128)S(1)} %get-tuple-element.86.own, ...), custom_call_target="tpu_custom_call" | custom-call | flops 20971520 | bytes 2097152 | tf_op jit(solution)/shard_map/mix/pallas_call | solution.py:471
  124.7 0.7 collective-permute-start.19
  125.4 7.9 %collective-permute-done.13.received.rest_14_ = s32[2,8,8192]{2,1,0:T(8,128)S(1)} collective-permute-done((s32[2,8,8192]{2,1,0:T(8,128)S(1)}, s32[2,8,8192]{2,1,0:T(8,128)S(1)}, u32[]{:S(2)}, u32[]{:S(2)}) %collective-permute-start.13) | collective-permute-done | bytes 524320 | tf_op jit(solution)/shard_map/ppermute | solution.py:669
  133.3 1.8 %mix.11 = (s32[2,8,8192]{2,1,0:T(8,128)S(1)}, s32[1,8,8192]{2,1,0:T(8,128)S(1)}, s32[1,8,8192]{2,1,0:T(8,128)S(1)}) custom-call(f32[2,8,8,128]{3,2,1,0:T(8,128)S(1)} %get-tuple-element.58.targets, bf16[128,128]{1,0:T(8,128)(2,1)S(1)} %get-tuple-element.60.weights, s32[2,8,8192]{2,1,0:T(8,128)S(1)} %get-tuple-element.77.own, ...), custom_call_target="tpu_custom_call" | custom-call | flops 20971520 | bytes 2097152 | tf_op jit(solution)/shard_map/mix/pallas_call | solution.py:471
  135.1 0.7 collective-permute-start.14
  135.8 0.2 forward.5
  136.0 1.3 collective-permute-start.25
  137.3 0.2 forward.4
  137.5 1.3 collective-permute-start.20
  138.8 0.2 forward.3
  139.0 1.3 collective-permute-start.15
  140.3 2.8 %spread.1 = f32[4,8,65536]{2,1,0:T(8,128)} custom-call(s32[2]{0:T(128)S(1)} %pad_add_fusion.place, f32[5,4,8,128]{3,2,1,0:T(8,128)S(1)} %get-tuple-element.53.columns, s32[2,8,8192]{2,1,0:T(8,128)S(1)} %collective-permute-done.rest_0_, s32[2,8,8192]{2,1,0:T(8,128)S(1)} %collective-permute-done.1.rest_1_.rest_0_, ...), custom_call_target="tpu_custom_call", output_to_operand_aliasing={{}: (6, {})} | custom-call | flops 20971520 | bytes 6291456 | tf_op jit(solution)/shard_map/spread/pallas_call | solution.py:417
  143.1 4.7 %collective-permute-done.25.rest_17_ = s32[1,8,8192]{2,1,0:T(8,128)S(1)} collective-permute-done((s32[1,8,8192]{2,1,0:T(8,128)S(1)}, s32[1,8,8192]{2,1,0:T(8,128)S(1)}, u32[]{:S(2)}, u32[]{:S(2)}) %collective-permute-start.25) | collective-permute-done | bytes 262176 | tf_op jit(solution)/shard_map/ppermute | solution.py:679
  147.8 2.9 %finish.3.rest_3_ = f32[2,8,65536]{2,1,0:T(8,128)} custom-call(s32[2]{0:T(128)S(1)} %pad_add_fusion.place, f32[2,8,8,128]{3,2,1,0:T(8,128)S(1)} %get-tuple-element.58.targets, s32[1,8,8192]{2,1,0:T(8,128)S(1)} %get-tuple-element.91.rest_0_, s32[2,8,8192]{2,1,0:T(8,128)S(1)} %collective-permute-done.6.rest_2_.rest_1_, ...), custom_call_target="tpu_custom_call" | custom-call | flops 15728640 | bytes 7864320 | tf_op jit(solution)/shard_map/finish/pallas_call | solution.py:564
  150.7 0.9 collective-permute-done.20.rest_2_
  151.5 1.5 finish.4.rest_3_
  153.0 4.7 %collective-permute-done.15.rest_2_ = s32[1,8,8192]{2,1,0:T(8,128)S(1)} collective-permute-done((s32[1,8,8192]{2,1,0:T(8,128)S(1)}, s32[1,8,8192]{2,1,0:T(8,128)S(1)}, u32[]{:S(2)}, u32[]{:S(2)}) %collective-permute-start.15) | collective-permute-done | bytes 262176 | tf_op jit(solution)/shard_map/ppermute | solution.py:679
  157.7 1.5 finish.5
  (13 shorter events, 0.0 us)
Async XLA Ops:
  4.6 8.4 %collective-permute-start.8 = (s32[2,8,8192]{2,1,0:T(8,128)S(1)}, s32[2,8,8192]{2,1,0:T(8,128)S(1)}, u32[]{:S(2)}, u32[]{:S(2)}) collective-permute-start(s32[2,8,8192]{2,1,0:T(8,128)S(1)} %get-tuple-element.65), channel_id=1, source_target_pairs={{0,1},{1,0},{2,3},{3,2},{4,5},{5,4},{6,7},{7,6},{8,9},{9,8},{10,11... | collective-permute-start | bytes 1572872 | tf_op jit(solution)/shard_map/ppermute | solution.py:660
  8.5 16.8 %collective-permute-start.5 = (s32[2,8,8192]{2,1,0:T(8,128)S(1)}, s32[2,8,8192]{2,1,0:T(8,128)S(1)}, u32[]{:S(2)}, u32[]{:S(2)}) collective-permute-start(s32[2,8,8192]{2,1,0:T(8,128)S(1)} %get-tuple-element.61.own), channel_id=1, source_target_pairs={{0,8},{24,16},{1,9},{25,17},{2,10},{26,18},{3,11},{27,19},{4,12},{... | collective-permute-start | bytes 1572872 | tf_op jit(solution)/shard_map/ppermute | solution.py:669
  15.0 21.0 %collective-permute-start.9 = (s32[2,8,8192]{2,1,0:T(8,128)S(1)}, s32[2,8,8192]{2,1,0:T(8,128)S(1)}, u32[]{:S(2)}, u32[]{:S(2)}) collective-permute-start(s32[2,8,8192]{2,1,0:T(8,128)S(1)} %get-tuple-element.70.own), channel_id=1, source_target_pairs={{0,8},{24,16},{1,9},{25,17},{2,10},{26,18},{3,11},{27,19},{4,12},{... | collective-permute-start | bytes 1572872 | tf_op jit(solution)/shard_map/ppermute | solution.py:669
  16.4 31.4 %collective-permute-start.4 = (s32[2,8,8192]{2,1,0:T(8,128)S(1)}, s32[2,8,8192]{2,1,0:T(8,128)S(1)}, u32[]{:S(2)}, u32[]{:S(2)}) collective-permute-start(s32[2,8,8192]{2,1,0:T(8,128)S(1)} %get-tuple-element.59), channel_id=1, source_target_pairs={{0,4},{1,5},{2,6},{3,7},{4,0},{5,1},{6,2},{7,3},{8,12},{9,13},{10,... | collective-permute-start | bytes 1572872 | tf_op jit(solution)/shard_map/ppermute | solution.py:660
  17.9 20.6 %collective-permute-start.7 = (s32[2,8,8192]{2,1,0:T(8,128)S(1)}, s32[2,8,8192]{2,1,0:T(8,128)S(1)}, u32[]{:S(2)}, u32[]{:S(2)}) collective-permute-start(s32[2,8,8192]{2,1,0:T(8,128)S(1)} %get-tuple-element.64), channel_id=1, source_target_pairs={{0,2},{1,3},{2,0},{3,1},{4,6},{5,7},{6,4},{7,5},{8,10},{9,11},{10,... | collective-permute-start | bytes 1572872 | tf_op jit(solution)/shard_map/ppermute | solution.py:660
  27.1 20.7 %collective-permute-start.6 = (s32[2,8,8192]{2,1,0:T(8,128)S(1)}, s32[2,8,8192]{2,1,0:T(8,128)S(1)}, u32[]{:S(2)}, u32[]{:S(2)}) collective-permute-start(s32[2,8,8192]{2,1,0:T(8,128)S(1)} %get-tuple-element.63), channel_id=1, source_target_pairs={{8,16},{16,8},{9,17},{17,9},{10,18},{18,10},{11,19},{19,11},{12,20... | collective-permute-start | bytes 1572872 | tf_op jit(solution)/shard_map/ppermute | solution.py:675
  27.8 22.2 %collective-permute-start = (s32[2,8,8192]{2,1,0:T(8,128)S(1)}, s32[2,8,8192]{2,1,0:T(8,128)S(1)}, u32[]{:S(2)}, u32[]{:S(2)}) collective-permute-start(s32[2,8,8192]{2,1,0:T(8,128)S(1)} %get-tuple-element.54), channel_id=1, source_target_pairs={{0,3},{1,2},{2,1},{3,0},{4,7},{5,6},{6,5},{7,4},{8,11},{9,10},{10,... | collective-permute-start | bytes 1572872 | tf_op jit(solution)/shard_map/ppermute | solution.py:660
  37.8 12.2 %collective-permute-start.10 = (s32[2,8,8192]{2,1,0:T(8,128)S(1)}, s32[2,8,8192]{2,1,0:T(8,128)S(1)}, u32[]{:S(2)}, u32[]{:S(2)}) collective-permute-start(s32[2,8,8192]{2,1,0:T(8,128)S(1)} %get-tuple-element.72), channel_id=1, source_target_pairs={{8,16},{16,8},{9,17},{17,9},{10,18},{18,10},{11,19},{19,11},{12,20... | collective-permute-start | bytes 1572872 | tf_op jit(solution)/shard_map/ppermute | solution.py:675
  40.6 19.5 %collective-permute-start.21 = (s32[2,8,8192]{2,1,0:T(8,128)S(1)}, s32[2,8,8192]{2,1,0:T(8,128)S(1)}, u32[]{:S(2)}, u32[]{:S(2)}) collective-permute-start(s32[2,8,8192]{2,1,0:T(8,128)S(1)} %get-tuple-element.93.own), channel_id=1, source_target_pairs={{0,8},{24,16},{1,9},{25,17},{2,10},{26,18},{3,11},{27,19},{4,12},{... | collective-permute-start | bytes 1572872 | tf_op jit(solution)/shard_map/ppermute | solution.py:669
  49.9 21.3 %collective-permute-start.16 = (s32[2,8,8192]{2,1,0:T(8,128)S(1)}, s32[2,8,8192]{2,1,0:T(8,128)S(1)}, u32[]{:S(2)}, u32[]{:S(2)}) collective-permute-start(s32[2,8,8192]{2,1,0:T(8,128)S(1)} %get-tuple-element.83), channel_id=1, source_target_pairs={{0,8},{24,16},{8,0},{16,24},{1,9},{25,17},{9,1},{17,25},{2,10},{26... | collective-permute-start | bytes 1572872 | tf_op jit(solution)/shard_map/ppermute | solution.py:669
  51.4 29.5 %collective-permute-start.11 = (s32[2,8,8192]{2,1,0:T(8,128)S(1)}, s32[2,8,8192]{2,1,0:T(8,128)S(1)}, u32[]{:S(2)}, u32[]{:S(2)}) collective-permute-start(s32[2,8,8192]{2,1,0:T(8,128)S(1)} %get-tuple-element.74), channel_id=1, source_target_pairs={{0,8},{24,16},{8,0},{16,24},{1,9},{25,17},{9,1},{17,25},{2,10},{26... | collective-permute-start | bytes 1572872 | tf_op jit(solution)/shard_map/ppermute | solution.py:669
  57.1 36.6 %collective-permute-start.1 = (s32[2,8,8192]{2,1,0:T(8,128)S(1)}, s32[2,8,8192]{2,1,0:T(8,128)S(1)}, u32[]{:S(2)}, u32[]{:S(2)}) collective-permute-start(s32[2,8,8192]{2,1,0:T(8,128)S(1)} %get-tuple-element.55), channel_id=1, source_target_pairs={{0,5},{1,4},{2,7},{3,6},{4,1},{5,0},{6,3},{7,2},{8,13},{9,12},{10,... | collective-permute-start | bytes 1572872 | tf_op jit(solution)/shard_map/ppermute | solution.py:660
  57.1 41.7 %collective-permute-start.2 = (s32[2,8,8192]{2,1,0:T(8,128)S(1)}, s32[2,8,8192]{2,1,0:T(8,128)S(1)}, u32[]{:S(2)}, u32[]{:S(2)}) collective-permute-start(s32[2,8,8192]{2,1,0:T(8,128)S(1)} %get-tuple-element.56), channel_id=1, source_target_pairs={{0,6},{1,7},{2,4},{3,5},{4,2},{5,3},{6,0},{7,1},{8,14},{9,15},{10,... | collective-permute-start | bytes 1572872 | tf_op jit(solution)/shard_map/ppermute | solution.py:660
  60.0 40.3 %collective-permute-start.3 = (s32[2,8,8192]{2,1,0:T(8,128)S(1)}, s32[2,8,8192]{2,1,0:T(8,128)S(1)}, u32[]{:S(2)}, u32[]{:S(2)}) collective-permute-start(s32[2,8,8192]{2,1,0:T(8,128)S(1)} %get-tuple-element.57), channel_id=1, source_target_pairs={{0,7},{1,6},{2,5},{3,4},{4,3},{5,2},{6,1},{7,0},{8,15},{9,14},{10,... | collective-permute-start | bytes 1572872 | tf_op jit(solution)/shard_map/ppermute | solution.py:660
  71.3 23.2 %collective-permute-start.22 = (s32[2,8,8192]{2,1,0:T(8,128)S(1)}, s32[2,8,8192]{2,1,0:T(8,128)S(1)}, u32[]{:S(2)}, u32[]{:S(2)}) collective-permute-start(s32[2,8,8192]{2,1,0:T(8,128)S(1)} %get-tuple-element.95), channel_id=1, source_target_pairs={{8,16},{16,8},{9,17},{17,9},{10,18},{18,10},{11,19},{19,11},{12,20... | collective-permute-start | bytes 1572872 | tf_op jit(solution)/shard_map/ppermute | solution.py:675
  80.9 18.0 %collective-permute-start.17 = (s32[2,8,8192]{2,1,0:T(8,128)S(1)}, s32[2,8,8192]{2,1,0:T(8,128)S(1)}, u32[]{:S(2)}, u32[]{:S(2)}) collective-permute-start(s32[2,8,8192]{2,1,0:T(8,128)S(1)} %get-tuple-element.85), channel_id=1, source_target_pairs={{8,16},{16,8},{9,17},{17,9},{10,18},{18,10},{11,19},{19,11},{12,20... | collective-permute-start | bytes 1572872 | tf_op jit(solution)/shard_map/ppermute | solution.py:675
  93.8 6.6 %collective-permute-start.12 = (s32[2,8,8192]{2,1,0:T(8,128)S(1)}, s32[2,8,8192]{2,1,0:T(8,128)S(1)}, u32[]{:S(2)}, u32[]{:S(2)}) collective-permute-start(s32[2,8,8192]{2,1,0:T(8,128)S(1)} %get-tuple-element.76), channel_id=1, source_target_pairs={{8,16},{16,8},{9,17},{17,9},{10,18},{18,10},{11,19},{19,11},{12,20... | collective-permute-start | bytes 1572872 | tf_op jit(solution)/shard_map/ppermute | solution.py:675
  95.9 15.7 %collective-permute-start.23 = (s32[2,8,8192]{2,1,0:T(8,128)S(1)}, s32[2,8,8192]{2,1,0:T(8,128)S(1)}, u32[]{:S(2)}, u32[]{:S(2)}) collective-permute-start(s32[2,8,8192]{2,1,0:T(8,128)S(1)} %get-tuple-element.97), channel_id=1, source_target_pairs={{0,8},{24,16},{8,0},{16,24},{1,9},{25,17},{9,1},{17,25},{2,10},{26... | collective-permute-start | bytes 1572872 | tf_op jit(solution)/shard_map/ppermute | solution.py:669
  100.2 22.6 %collective-permute-start.18 = (s32[2,8,8192]{2,1,0:T(8,128)S(1)}, s32[2,8,8192]{2,1,0:T(8,128)S(1)}, u32[]{:S(2)}, u32[]{:S(2)}) collective-permute-start(s32[2,8,8192]{2,1,0:T(8,128)S(1)} %get-tuple-element.87), channel_id=1, source_target_pairs={{0,8},{24,16},{8,0},{16,24},{1,9},{25,17},{9,1},{17,25},{2,10},{26... | collective-permute-start | bytes 1572872 | tf_op jit(solution)/shard_map/ppermute | solution.py:669
  101.7 31.5 %collective-permute-start.13 = (s32[2,8,8192]{2,1,0:T(8,128)S(1)}, s32[2,8,8192]{2,1,0:T(8,128)S(1)}, u32[]{:S(2)}, u32[]{:S(2)}) collective-permute-start(s32[2,8,8192]{2,1,0:T(8,128)S(1)} %get-tuple-element.78), channel_id=1, source_target_pairs={{0,8},{24,16},{8,0},{16,24},{1,9},{25,17},{9,1},{17,25},{2,10},{26... | collective-permute-start | bytes 1572872 | tf_op jit(solution)/shard_map/ppermute | solution.py:669
  113.4 22.4 %collective-permute-start.24 = (s32[2,8,8192]{2,1,0:T(8,128)S(1)}, s32[2,8,8192]{2,1,0:T(8,128)S(1)}, u32[]{:S(2)}, u32[]{:S(2)}) collective-permute-start(s32[2,8,8192]{2,1,0:T(8,128)S(1)} %get-tuple-element.102), channel_id=1, source_target_pairs={{8,16},{16,8},{9,17},{17,9},{10,18},{18,10},{11,19},{19,11},{12,20... | collective-permute-start | bytes 1572872 | tf_op jit(solution)/shard_map/ppermute | solution.py:675
  124.7 12.6 %collective-permute-start.19 = (s32[2,8,8192]{2,1,0:T(8,128)S(1)}, s32[2,8,8192]{2,1,0:T(8,128)S(1)}, u32[]{:S(2)}, u32[]{:S(2)}) collective-permute-start(s32[2,8,8192]{2,1,0:T(8,128)S(1)} %get-tuple-element.89), channel_id=1, source_target_pairs={{8,16},{16,8},{9,17},{17,9},{10,18},{18,10},{11,19},{19,11},{12,20... | collective-permute-start | bytes 1572872 | tf_op jit(solution)/shard_map/ppermute | solution.py:675
  135.1 3.7 %collective-permute-start.14 = (s32[2,8,8192]{2,1,0:T(8,128)S(1)}, s32[2,8,8192]{2,1,0:T(8,128)S(1)}, u32[]{:S(2)}, u32[]{:S(2)}) collective-permute-start(s32[2,8,8192]{2,1,0:T(8,128)S(1)} %get-tuple-element.80), channel_id=1, source_target_pairs={{8,16},{16,8},{9,17},{17,9},{10,18},{18,10},{11,19},{19,11},{12,20... | collective-permute-start | bytes 1572872 | tf_op jit(solution)/shard_map/ppermute | solution.py:675
  136.0 11.8 %collective-permute-start.25 = (s32[1,8,8192]{2,1,0:T(8,128)S(1)}, s32[1,8,8192]{2,1,0:T(8,128)S(1)}, u32[]{:S(2)}, u32[]{:S(2)}) collective-permute-start(s32[1,8,8192]{2,1,0:T(8,128)S(1)} %forward.5), channel_id=1, source_target_pairs={{8,0},{16,24},{9,1},{17,25},{10,2},{18,26},{11,3},{19,27},{12,4},{... | collective-permute-start | bytes 786440 | tf_op jit(solution)/shard_map/ppermute | solution.py:679
  137.5 14.1 %collective-permute-start.20 = (s32[1,8,8192]{2,1,0:T(8,128)S(1)}, s32[1,8,8192]{2,1,0:T(8,128)S(1)}, u32[]{:S(2)}, u32[]{:S(2)}) collective-permute-start(s32[1,8,8192]{2,1,0:T(8,128)S(1)} %forward.4), channel_id=1, source_target_pairs={{8,0},{16,24},{9,1},{17,25},{10,2},{18,26},{11,3},{19,27},{12,4},{... | collective-permute-start | bytes 786440 | tf_op jit(solution)/shard_map/ppermute | solution.py:679
  139.0 18.7 %collective-permute-start.15 = (s32[1,8,8192]{2,1,0:T(8,128)S(1)}, s32[1,8,8192]{2,1,0:T(8,128)S(1)}, u32[]{:S(2)}, u32[]{:S(2)}) collective-permute-start(s32[1,8,8192]{2,1,0:T(8,128)S(1)} %forward.3), channel_id=1, source_target_pairs={{8,0},{16,24},{9,1},{17,25},{10,2},{18,26},{11,3},{19,27},{12,4},{... | collective-permute-start | bytes 786440 | tf_op jit(solution)/shard_map/ppermute | solution.py:679

commit v3 on v2

--- a/solution.py
+++ b/solution.py
@@ -66,30 +66,31 @@
     return lambda number: jnp.full(limit, number, jnp.int32).astype(jnp.float32)
 
 
-def build_tables(place, levels, moduli, inverse, cross, columns, targets, weights):
-    group, home = place[0], place[1]
-    limbs, block = columns.shape[1], columns.shape[2]
-    source_count = inverse.shape[0]
+def product(left, right):
+    return jnp.dot(left, right, preferred_element_type=jnp.float32)
+
+
+def bytes_of(table):
+    parts = (table & 0xFF, lax.shift_right_logical(table, 8))
+    return [part.astype(jnp.float32).astype(jnp.bfloat16) for part in parts]
+
+
+def level_rows(place, levels, block, source_count):
     lane = lax.broadcasted_iota(jnp.int32, (block, source_count), 1)
     rank = lax.broadcasted_iota(jnp.int32, (block, source_count), 0)
-    own_levels = [levels[home * block + n] for n in range(block)]
     level_rank = jnp.zeros((block, source_count), jnp.int32)
-    for n, level in enumerate(own_levels):
-        level_rank = jnp.where(rank == n, level - 1, level_rank)
-    onehot = jnp.where(lane == level_rank, 1.0, 0.0).astype(jnp.bfloat16)
-
-    def bytes_of(table):
-        parts = (table & 0xFF, lax.shift_right_logical(table, 8))
-        return [part.astype(jnp.float32).astype(jnp.bfloat16) for part in parts]
-
-    def product(left, right):
-        return jnp.dot(left, right, preferred_element_type=jnp.float32)
-
+    for n in range(block):
+        level_rank = jnp.where(rank == n, levels[place[1] * block + n] - 1, level_rank)
+    return lane, level_rank, jnp.where(lane == level_rank, 1.0, 0.0).astype(jnp.bfloat16)
+
+
+def build_columns(place, levels, moduli, inverse, columns):
+    group = place[0]
+    limbs, block = columns.shape[1], columns.shape[2]
+    lane, level_rank, onehot = level_rows(place, levels, block, inverse.shape[0])
     inverse_low, inverse_high = (product(onehot, part) for part in bytes_of(inverse[...]))
     inverse_rows = jnp.where(lane <= level_rank, inverse_low + 256.0 * inverse_high, 0.0)
     live_rows = jnp.where(lane <= level_rank, 1.0, 0.0)
-    total = targets.shape[1]
-    quarter = total // 4
     shape = (block, LANES)
     fill = constants(shape)
     for limb in range(limbs):
@@ -106,6 +107,14 @@
         columns[3, limb] = modulus
         columns[4, limb] = 1.0 / modulus
 
+
+def build_weights(place, levels, moduli, cross, limbs, targets, weights):
+    group = place[0]
+    total, block = targets.shape[1:3]
+    source_count = cross.shape[0]
+    quarter = total // 4
+    fill = constants((block, LANES))
+    onehot = level_rows(place, levels, block, source_count)[2]
     left = group < 2
     inner = (group == 1) | (group == 2)
     order = (jnp.where(left, 2, 1), jnp.where(left, 3, 0), group ^ 1, group)
@@ -171,24 +180,17 @@
 
 
 def first_kernel(place, *rest):
-    tables, residues = rest[:4], rest[4]
-    columns, targets, weights, source, scaled = rest[5:10]
-    landing, stage, *copies = rest[10:-3]
-    sems, out_sems, table_sems = rest[-3:]
-    block, width = stage.shape[1:]
+    tables, residues, columns, scaled, landing = rest[:3], *rest[3:7]
+    copies, (sems, table_sems) = rest[7:-2], rest[-2:]
+    block, width = landing.shape[1:]
     tile = width // sems.shape[0]
-    home = place[1]
-    start = home * residues.shape[2]
 
     def load(step):
         return pltpu.make_async_copy(
-            residues.at[:, pl.ds(pl.multiple_of(home * block, block), block), span_of(step, tile)],
+            residues.at[:, pl.ds(pl.multiple_of(place[1] * block, block), block), span_of(step, tile)],
             landing.at[:, :, span_of(step, tile)],
             sems.at[step],
         )
-
-    def store(step):
-        return out_copy(stage, source, start, step, tile, out_sems)
 
     steps = width // tile
     fetches = [pltpu.make_async_copy(a, b, table_sems.at[i]) for i, (a, b) in enumerate(zip(tables, copies))]
@@ -197,62 +199,52 @@
     loop(steps, lambda step: load(step).start())
     for fetch in fetches:
         fetch.wait()
-    build_tables(place, *copies, columns, targets, weights)
+    build_columns(place, *copies, columns)
 
     def body(step):
         load(step).wait()
         span = span_of(step, tile)
-        scale_tile(landing, columns, stage, scaled, span, span, span)
-        store(step).start()
+        scale_tile(landing, columns, None, scaled, span, span, span)
 
     loop(steps, body)
-    loop(steps, lambda step: store(step).wait())
 
 
 def tile_of(width):
     return min(width, 1024)
 
 
-def first(place, levels, moduli, inverse_table, cross, residues, block, count, length):
-    limbs, _, width = residues.shape
-    source_count = inverse_table.shape[0]
-    total = moduli.shape[0] - source_count
+def first(place, levels, moduli, inverse_table, residues, block, length):
+    limbs = residues.shape[0]
     steps = length // tile_of(length)
     return pl.pallas_call(
         first_kernel,
-        in_specs=[SCALARS] + [FAR] * 5,
-        out_specs=[HERE, HERE, HERE, FAR, HERE],
+        in_specs=[SCALARS] + [FAR] * 4,
+        out_specs=[HERE, HERE],
         out_shape=[
             pltpu.VMEM((5, limbs, block, LANES), jnp.float32),
-            pltpu.VMEM((2, total, block, LANES), jnp.float32),
-            pltpu.VMEM((2 * total * block, 4 * limbs * block), jnp.bfloat16),
-            jax.ShapeDtypeStruct((limbs, block, width * count), jnp.float32),
             pltpu.VMEM((limbs // 2, block, length), jnp.int32),
         ],
         scratch_shapes=[
             pltpu.VMEM((limbs, block, length), jnp.float32),
-            pltpu.VMEM((limbs, block, length), jnp.float32),
             pltpu.SMEM(levels.shape, jnp.int32),
             pltpu.SMEM(moduli.shape, jnp.int32),
             pltpu.VMEM(inverse_table.shape, jnp.int32),
-            pltpu.VMEM(cross.shape, jnp.int32),
             pltpu.SemaphoreType.DMA((steps,)),
-            pltpu.SemaphoreType.DMA((steps,)),
-            pltpu.SemaphoreType.DMA((4,)),
+            pltpu.SemaphoreType.DMA((3,)),
         ],
         compiler_params=params(8),
         cost_estimate=cost(limbs * block * length, 60, 10 * limbs * block * length),
         name="first",
-    )(place, *(far(x) for x in (levels, moduli, inverse_table, cross, residues)))
+    )(place, *(far(x) for x in (levels, moduli, inverse_table, residues)))
 
 
 def far(array):
     return pltpu.with_memory_space_constraint(array, pltpu.HBM)
 
 
-def pack_kernel(offsets, place, residues, *rest):
-    outs, (landing, sems) = rest[:-2], rest[-2:]
-    _, _, block, width = landing.shape
+def pack_kernel(offsets, place, columns, levels, moduli, cross, residues, targets, weights, source, *rest):
+    outs, (landing, stage, level_copy, moduli_copy, cross_copy, sems, own_sems, table_sems) = rest[:-8], rest[-8:]
+    _, limbs, block, width = landing.shape
     tile = tile_of(width)
 
     def load(turn):
@@ -261,37 +253,70 @@
             residues.at[:, pl.ds(pl.multiple_of(peer * block, block), block), :], landing.at[turn], sems.at[turn]
         )
 
-    for turn in range(len(outs)):
+    fetches = [
+        pltpu.make_async_copy(array, copy, table_sems.at[i])
+        for i, (array, copy) in enumerate(((levels, level_copy), (moduli, moduli_copy), (cross, cross_copy)))
+    ]
+    for fetch in fetches:
+        fetch.start()
+    for turn in range(len(offsets)):
         load(turn).start()
-    for turn, out in enumerate(outs):
+    for fetch in fetches:
+        fetch.wait()
+    build_weights(place, level_copy, moduli_copy, cross_copy, limbs, targets, weights)
+
+    def store(step):
+        return out_copy(stage, source, place[1] * width, step, tile, own_sems)
+
+    for turn, out in enumerate((None, *outs)):
         load(turn).wait()
 
         def body(step):
             span = span_of(step, tile)
-            for word in range(out.shape[0]):
+            if out is None:
+                for limb in range(limbs):
+                    stage[limb, :, span] = landing[turn, limb, :, span] * spread(columns[2, limb], tile)
+                store(step).start()
+                return
+            for word in range(limbs // 2):
                 one = landing[turn, 2 * word, :, span].astype(jnp.int32)
                 two = landing[turn, 2 * word + 1, :, span].astype(jnp.int32)
                 out[word, :, span] = pack_pair(one, two)
 
         loop(width // tile, body)
-
-
-def pack_blocks(place, residues, offsets, block):
+    loop(width // tile, lambda step: store(step).wait())
+
+
+def pack_blocks(place, columns, levels, moduli, cross, residues, block, count):
     limbs, _, width = residues.shape
-    peers = len(offsets)
-    return pl.pallas_call(
+    total, _ = cross.shape[1:]
+    offsets = tuple(range(count))
+    peers = count - 1
+    results = pl.pallas_call(
         functools.partial(pack_kernel, offsets),
-        in_specs=[SCALARS, FAR],
-        out_specs=[HERE] * peers,
-        out_shape=[pltpu.VMEM((limbs // 2, block, width), jnp.int32)] * peers,
+        in_specs=[SCALARS, HERE] + [FAR] * 4,
+        out_specs=[HERE, HERE, FAR] + [HERE] * peers,
+        out_shape=[
+            pltpu.VMEM((2, total, block, LANES), jnp.float32),
+            pltpu.VMEM((2 * total * block, 4 * limbs * block), jnp.bfloat16),
+            jax.ShapeDtypeStruct((limbs, block, width * count), jnp.float32),
+        ]
+        + [pltpu.VMEM((limbs // 2, block, width), jnp.int32)] * peers,
         scratch_shapes=[
-            pltpu.VMEM((peers, limbs, block, width), jnp.float32),
-            pltpu.SemaphoreType.DMA((peers,)),
+            pltpu.VMEM((count, limbs, block, width), jnp.float32),
+            pltpu.VMEM((limbs, block, width), jnp.float32),
+            pltpu.SMEM(levels.shape, jnp.int32),
+            pltpu.SMEM(moduli.shape, jnp.int32),
+            pltpu.VMEM(cross.shape, jnp.int32),
+            pltpu.SemaphoreType.DMA((count,)),
+            pltpu.SemaphoreType.DMA((width // tile_of(width),)),
+            pltpu.SemaphoreType.DMA((3,)),
         ],
-        compiler_params=params(12),
+        compiler_params=params(14),
         cost_estimate=cost(peers * limbs * block * width, 16, 6 * peers * limbs * block * width),
         name="pack",
-    )(place, residues)
+    )(place, columns, *(far(x) for x in (levels, moduli, cross, residues)))
+    return *results[:3], dict(zip(offsets[1:], results[3:]))
 
 
 def scale_kernel(chunk, relay, emit, place, columns, targets, *rest):
@@ -430,7 +455,7 @@
     )(*operands)
 
 
-def mix_kernel(targets, weights, own, received, far_out, outer_out, mine_out):
+def mix_kernel(targets, weights, own, received, *outs):
     block = own.shape[1]
     tile = min(own.shape[2], 2048)
 
@@ -456,7 +481,7 @@
             reduced.append(residue(256.0 * upper + low, modulus, inverse).astype(jnp.int32))
         words = [pack_pair(reduced[t], reduced[t + 1]) for t in range(0, len(reduced), 2)]
         position = 0
-        for out in (far_out, outer_out, mine_out):
+        for out in outs:
             for word in range(out.shape[0]):
                 out[word, :, span] = words[position]
                 position += 1
@@ -464,14 +489,15 @@
     loop(own.shape[2] // tile, body)
 
 
-def mix_chunk(own, received, weights, targets):
+def mix_chunk(own, received, weights, targets, split):
     words, block, length = own.shape
     total = targets.shape[1]
-    counts = (total // 4, total // 8, total // 8)
+    part = total // 8
+    counts = (part, part, part, part) if split else (2 * part, part, part)
     return pl.pallas_call(
         mix_kernel,
         in_specs=[HERE] * 4,
-        out_specs=[HERE] * 3,
+        out_specs=[HERE] * len(counts),
         out_shape=[pltpu.VMEM((count, block, length), jnp.int32) for count in counts],
         compiler_params=params(8),
         cost_estimate=cost(total * block * length, 40, 4 * (2 * words + 4) * block * length),
@@ -512,14 +538,16 @@
     )(targets, outer, arrived)
 
 
-def finish_kernel(chunks, full, place, targets, *rest):
+def finish_kernel(chunks, full, widths, place, targets, *rest):
     out, stage, sems = rest[-3:]
     tile = stage.shape[3]
     inner = (place[0] == 1) | (place[0] == 2)
     stores = []
     slot = 0
+    position = 0
     for turn, (offsets, low, high) in enumerate(chunks):
-        mine, arrived, relayed = rest[3 * turn : 3 * turn + 3]
+        mine, arrived, relayed, *direct = rest[position : position + widths[turn]]
+        position += widths[turn]
         first_target = 6 * mine.shape[0]
         steps = (high - low) // tile
         for part, offset in enumerate(offsets):
@@ -536,10 +564,14 @@
                 span = pl.ds(pl.multiple_of(part * (high - low) + step * tile, tile), tile)
                 for word in range(mine.shape[0]):
                     other = jnp.where(inner, arrived[word, :, span], relayed[word, :, span])
-                    for side, (a, b) in enumerate(zip(halves(mine[word, :, span]), halves(other))):
+                    parts = [halves(mine[word, :, span]), halves(other)]
+                    parts += [halves(jnp.where(inner, 0, more[word, :, span])) for more in direct]
+                    for side, (total, *terms) in enumerate(zip(*parts)):
                         target = first_target + 2 * word + side
                         modulus = spread(targets[0, target].astype(jnp.int32), tile)
-                        total = join_residues(a, b, modulus).astype(jnp.float32)
+                        for term in terms:
+                            total = join_residues(total, term, modulus)
+                        total = total.astype(jnp.float32)
                         stage[slot + step, 2 * word + side] = total * spread(targets[1, target], tile)
                 store(step).start()
 
@@ -562,7 +594,7 @@
         operands.append(buffer)
         in_specs.append(FAR)
     return pl.pallas_call(
-        functools.partial(finish_kernel, chunks, full),
+        functools.partial(finish_kernel, chunks, full, [len(triple) for triple in triples]),
         in_specs=in_specs,
         out_specs=FAR,
         out_shape=jax.ShapeDtypeStruct(shape, jnp.float32),
@@ -612,15 +644,16 @@
     alone = [step for step in range(steps) if step not in ride.values()]
     for step in range(steps):
         events += [f"mix{step}", f"b{step}"]
+        if step == steps - 1:
+            events += [f"d{step}", f"c{step}"]
         if step + 2 < steps:
             events += [f"scale{step + 2}", f"a{step + 2}"]
         if step - 1 in alone:
             events += [f"forward{step - 1}", f"c{step - 1}"]
     joined = [step for step in range(steps) if step not in alone]
     tail = steps - 1
-    events[events.index(f"b{tail}") + 1 : events.index(f"b{tail}") + 1] = ["spread"]
-    events += ["finish" + "_".join(map(str, joined + alone[:-2]))]
-    events += [f"forward{tail}", f"c{tail}", f"finish{tail - 1}", f"finish{tail}"]
+    events[events.index(f"c{tail}") + 1 : events.index(f"c{tail}") + 1] = ["spread"]
+    events += ["finish" + "_".join(map(str, joined + alone[:-2])), f"finish{tail - 1}", f"finish{tail}"]
     return events
 
 
@@ -642,20 +675,18 @@
 
     scaled, send, received, mixed, crossed, relayed = ([None] * steps for _ in range(6))
     arrived = {}
-    packed = {}
     result = None
     shape = (target_count // 4, block, width * count)
     for event in timeline(plan):
         kind = event.rstrip("0123456789_")
         step = int(event[len(kind) :] or 0) if "_" not in event else 0
         if kind == "first":
-            columns, targets, weights, source, scaled[0] = first(
-                place, levels, moduli, inverse_table, cross, residues, block, count, plan[0][2]
-            )
+            columns, scaled[0] = first(place, levels, moduli, inverse_table, residues, block, plan[0][2])
             send[0] = scaled[0]
         elif kind == "pack":
-            offsets = tuple(range(1, count))
-            packed = dict(zip(offsets, pack_blocks(place, far(residues), offsets, block)))
+            targets, weights, source, packed = pack_blocks(
+                place, columns, levels, moduli, cross, residues, block, count
+            )
         elif kind == "p":
             arrived[step] = lax.ppermute(packed[step], "coef", [(i, i ^ step) for i in range(count)])
         elif kind == "scale":
@@ -670,19 +701,24 @@
             if step in ride:
                 relayed[ride[step]] = received[step]
         elif kind == "mix":
-            mixed[step] = mix_chunk(scaled[step], received[step], weights, targets)
+            mixed[step] = mix_chunk(scaled[step], received[step], weights, targets, step == steps - 1)
         elif kind == "b":
             crossed[step] = lax.ppermute(mixed[step][0], "limb", [(1, 2), (2, 1)])
         elif kind == "forward":
             relayed[step] = forward_chunk(mixed[step][1], crossed[step], targets)
         elif kind == "c":
-            relayed[step] = lax.ppermute(relayed[step], "limb", [(1, 0), (2, 3)])
+            share = mixed[step][2] if step == steps - 1 else relayed[step]
+            relayed[step] = lax.ppermute(share, "limb", [(1, 0), (2, 3)])
+        elif kind == "d":
+            direct = lax.ppermute(mixed[step][1], "limb", [(1, 3), (2, 0)])
         elif kind == "spread":
             pieces = [(offset, low, high) for i in sorted(late(plan)) for offset, low, high in [(o, *plan[i][1:]) for o in plan[i][0]]]
             source = spread_blocks(place, columns, [arrived[p[0]] for p in pieces], pieces, source)
         else:
             chosen = [int(i) for i in event[len(kind) :].split("_")]
-            triples = [(mixed[i][2], crossed[i], relayed[i]) for i in chosen]
+            triples = [(mixed[i][-1], crossed[i], relayed[i]) for i in chosen]
+            if chosen[-1] == steps - 1:
+                triples[-1] += (direct,)
             result = finish_chunks(
                 place, targets, triples, tuple(plan[i] for i in chosen), shape, width, result
             )

time: 160 us -> 153 us (0.956)
  waiting for transfers between devices: 67.5 us -> 49.7 us
  starting transfers between devices: 48.2 us -> 58.5 us
    ppermute x8, starting transfers between devices: 31.4 us -> 42.2 us  [per_device(): received[step] = lax.ppermute(send[step], 'limb', pairs)]
    ppermute x7, waiting for transfers between devices: 10.4 us -> 0.02 us  [per_device(): lax.ppermute(packed[step], 'coef', [(i, i ^ step) for i in range(count)])]
    ppermute x8, waiting for transfers between devices: 46.8 us -> 37.3 us  [per_device(): received[step] = lax.ppermute(send[step], 'limb', pairs)]
    ppermute x3 -> x4, waiting for transfers between devices: 10.2 us -> 12.4 us  [the longest x3 7.68 us: per_device(): relayed[step] = lax.ppermute(share, 'limb', [(1, 0), (2, 3)])]
    ppermute x7, starting transfers between devices: 7.41 us -> 5.65 us  [per_device(): lax.ppermute(packed[step], 'coef', [(i, i ^ step) for i in range(count)])]
    ppermute x3 -> x4, starting transfers between devices: 3.88 us -> 5.17 us  [the longest x3 3.88 us: per_device(): relayed[step] = lax.ppermute(share, 'limb', [(1, 0), (2, 3)])]
  transfers between devices with their start and end apart: 26 -> 27, of which waited for: 12 -> 10; matrix products, arithmetic and copies ran while one was open for 0% -> 0% of each run, Pallas kernels for 23% -> 26%
where the time goes in v3:
time: 153 us; the launch traced here: 152 us
  starting transfers between devices  58.5 us (38%)
  waiting for transfers between devices  49.7 us (32%)
  Pallas kernels  42.7 us (28%)
    ppermute x8, starting transfers between devices, per_device(): received[step] = lax.ppermute(send[step], 'limb', pairs)  42.2 us
    ppermute x8, waiting for transfers between devices, per_device(): received[step] = lax.ppermute(send[step], 'limb', pairs)  37.3 us
    pallas_call x8, Pallas kernels, mix_chunk(): pl.pallas_call(mix_kernel, in_specs=[HERE] * 4, out_specs=[HERE] * len(co...  14.3 us
    pallas_call x7, Pallas kernels, scale_chunk(): pl.pallas_call(functools.partial(scale_kernel, chunk, relay is not None,...  11.7 us
    ppermute x3, waiting for transfers between devices, per_device(): relayed[step] = lax.ppermute(share, 'limb', [(1, 0), (2, 3)])  7.68 us
    pallas_call x3, Pallas kernels, finish_chunks(): pl.pallas_call(functools.partial(finish_kernel, chunks, full, [len(triple...  5.89 us
    ppermute x7, starting transfers between devices, per_device(): lax.ppermute(packed[step], 'coef', [(i, i ^ step) for i in range(count)])  5.65 us
    ppermute x8, starting transfers between devices, per_device(): crossed[step] = lax.ppermute(mixed[step][0], 'limb', [(1, 2), (2, 1)])  5.52 us
  transfers between devices with their start and end apart: 27, of which 10 were waited for; matrix products, arithmetic and copies ran while one was open for 0% of the time, Pallas kernels for 26%

profile of v3, /device:TPU:0, one launch (start us, length us, event | category | flops | bytes accessed | tf_op | source)
XLA Modules:
  0.0 152.1 jit_solution(13989260523588783774)
XLA Ops:
  0.6 0.1 pad_add_fusion.place
  0.7 2.3 %first.1 = (f32[5,4,8,128]{3,2,1,0:T(8,128)S(1)}, s32[2,8,8192]{2,1,0:T(8,128)S(1)}) custom-call(s32[2]{0:T(128)S(1)} %pad_add_fusion.place, s32[64]{0:T(128)} %levels.1, s32[24]{0:T(128)} %moduli.1, s32[16,16]{1,0:T(8,128)} %rest_2_.1, f32[4,64,8192]{2,1,0:T(8,128)} %residues.1), custom_call_target="tpu_custom_call" | custom-call | flops 15728640 | bytes 2621440 | tf_op jit(solution)/shard_map/first/pallas_call | solution.py:219
  3.0 5.0 %collective-permute-start.5 = (s32[2,8,8192]{2,1,0:T(8,128)S(1)}, s32[2,8,8192]{2,1,0:T(8,128)S(1)}, u32[]{:S(2)}, u32[]{:S(2)}) collective-permute-start(s32[2,8,8192]{2,1,0:T(8,128)S(1)} %get-tuple-element.62.own), channel_id=1, source_target_pairs={{0,8},{24,16},{1,9},{25,17},{2,10},{26,18},{3,11},{27,19},{4,12},{... | collective-permute-start | bytes 1572872 | tf_op jit(solution)/shard_map/ppermute | solution.py:700
  8.0 5.4 %pack.1 = (f32[2,8,8,128]{3,2,1,0:T(8,128)S(1)}, bf16[128,128]{1,0:T(8,128)(2,1)S(1)}, f32[4,8,65536]{2,1,0:T(8,128)}, s32[2,8,8192]{2,1,0:T(8,128)S(1)}, s32[2,...) custom-call(s32[2]{0:T(128)S(1)} %pad_add_fusion.place, ...), custom_call_target="tpu_custom_call" | custom-call | flops 29360128 | bytes 11010048 | tf_op jit(solution)/shard_map/pack/pallas_call | solution.py:295
  13.4 0.1 collective-permute-start.8
  13.5 1.6 %collective-permute-start.4 = (s32[2,8,8192]{2,1,0:T(8,128)S(1)}, s32[2,8,8192]{2,1,0:T(8,128)S(1)}, u32[]{:S(2)}, u32[]{:S(2)}) collective-permute-start(s32[2,8,8192]{2,1,0:T(8,128)S(1)} %get-tuple-element.60), channel_id=1, source_target_pairs={{0,4},{1,5},{2,6},{3,7},{4,0},{5,1},{6,2},{7,3},{8,12},{9,13},{10,... | collective-permute-start | bytes 1572872 | tf_op jit(solution)/shard_map/ppermute | solution.py:691
  15.0 1.5 collective-permute-start.7
  16.5 2.6 %collective-permute-done.5.received = s32[2,8,8192]{2,1,0:T(8,128)S(1)} collective-permute-done((s32[2,8,8192]{2,1,0:T(8,128)S(1)}, s32[2,8,8192]{2,1,0:T(8,128)S(1)}, u32[]{:S(2)}, u32[]{:S(2)}) %collective-permute-start.5) | collective-permute-done | bytes 524320 | tf_op jit(solution)/shard_map/ppermute | solution.py:700
  19.1 1.8 %mix.8 = (s32[2,8,8192]{2,1,0:T(8,128)S(1)}, s32[1,8,8192]{2,1,0:T(8,128)S(1)}, s32[1,8,8192]{2,1,0:T(8,128)S(1)}) custom-call(f32[2,8,8,128]{3,2,1,0:T(8,128)S(1)} %get-tuple-element.59.targets, bf16[128,128]{1,0:T(8,128)(2,1)S(1)} %get-tuple-element.61.weights, s32[2,8,8192]{2,1,0:T(8,128)S(1)} %get-tuple-element.62.own, ...), custom_call_target="tpu_custom_call" | custom-call | flops 20971520 | bytes 2097152 | tf_op jit(solution)/shard_map/mix/pallas_call | solution.py:497
  20.9 0.7 collective-permute-start.6
  21.6 0.0 collective-permute-done.8.rest_0_
  21.6 2.0 %scale.7 = (f32[4,8,65536]{2,1,0:T(8,128)}, s32[2,8,8192]{2,1,0:T(8,128)S(1)}) custom-call(s32[2]{0:T(128)S(1)} %pad_add_fusion.place, f32[5,4,8,128]{3,2,1,0:T(8,128)S(1)} %get-tuple-element.54.columns, f32[2,8,8,128]{3,2,1,0:T(8,128)S(1)} %get-tuple-element.59.targets, ...), custom_call_target="tpu_custom_call", output_to_operand_aliasing={{0}: (4, {})} | custom-call | flops 10485760 | bytes 2097152 | tf_op jit(solution)/shard_map/scale/pallas_call | solution.py:389
  23.6 7.2 %collective-permute-start.9 = (s32[2,8,8192]{2,1,0:T(8,128)S(1)}, s32[2,8,8192]{2,1,0:T(8,128)S(1)}, u32[]{:S(2)}, u32[]{:S(2)}) collective-permute-start(s32[2,8,8192]{2,1,0:T(8,128)S(1)} %get-tuple-element.71.own), channel_id=1, source_target_pairs={{0,8},{24,16},{1,9},{25,17},{2,10},{26,18},{3,11},{27,19},{4,12},{... | collective-permute-start | bytes 1572872 | tf_op jit(solution)/shard_map/ppermute | solution.py:700
  30.9 2.0 %scale.8 = (f32[4,8,65536]{2,1,0:T(8,128)}, s32[2,8,8192]{2,1,0:T(8,128)S(1)}) custom-call(s32[2]{0:T(128)S(1)} %pad_add_fusion.place, f32[5,4,8,128]{3,2,1,0:T(8,128)S(1)} %get-tuple-element.54.columns, f32[2,8,8,128]{3,2,1,0:T(8,128)S(1)} %get-tuple-element.59.targets, ...), custom_call_target="tpu_custom_call", output_to_operand_aliasing={{0}: (4, {})} | custom-call | flops 10485760 | bytes 2097152 | tf_op jit(solution)/shard_map/scale/pallas_call | solution.py:389
  32.9 1.3 collective-permute-start.22
  34.2 0.0 collective-permute-done.4.rest_0_
  34.2 2.1 %scale.9 = (f32[4,8,65536]{2,1,0:T(8,128)}, s32[2,8,8192]{2,1,0:T(8,128)S(1)}, s32[2,8,8192]{2,1,0:T(8,128)S(1)}) custom-call(s32[2]{0:T(128)S(1)} %pad_add_fusion.place, f32[5,4,8,128]{3,2,1,0:T(8,128)S(1)} %get-tuple-element.54.columns, f32[2,8,8,128]{3,2,1,0:T(8,128)S(1)} %get-tuple-element.59.targets, ...), custom_call_target="tpu_custom_call", output_to_operand_aliasing={{0}: (6, {})} | custom-call | flops 10485760 | bytes 2097152 | tf_op jit(solution)/shard_map/scale/pallas_call | solution.py:389
  36.4 3.9 %collective-permute-start.17 = (s32[2,8,8192]{2,1,0:T(8,128)S(1)}, s32[2,8,8192]{2,1,0:T(8,128)S(1)}, u32[]{:S(2)}, u32[]{:S(2)}) collective-permute-start(s32[2,8,8192]{2,1,0:T(8,128)S(1)} %get-tuple-element.85), channel_id=1, source_target_pairs={{0,8},{24,16},{8,0},{16,24},{1,9},{25,17},{9,1},{17,25},{2,10},{26... | collective-permute-start | bytes 1572872 | tf_op jit(solution)/shard_map/ppermute | solution.py:700
  40.3 2.8 %collective-permute-done.9.received = s32[2,8,8192]{2,1,0:T(8,128)S(1)} collective-permute-done((s32[2,8,8192]{2,1,0:T(8,128)S(1)}, s32[2,8,8192]{2,1,0:T(8,128)S(1)}, u32[]{:S(2)}, u32[]{:S(2)}) %collective-permute-start.9) | collective-permute-done | bytes 524320 | tf_op jit(solution)/shard_map/ppermute | solution.py:700
  43.1 1.8 %mix.9 = (s32[2,8,8192]{2,1,0:T(8,128)S(1)}, s32[1,8,8192]{2,1,0:T(8,128)S(1)}, s32[1,8,8192]{2,1,0:T(8,128)S(1)}) custom-call(f32[2,8,8,128]{3,2,1,0:T(8,128)S(1)} %get-tuple-element.59.targets, bf16[128,128]{1,0:T(8,128)(2,1)S(1)} %get-tuple-element.61.weights, s32[2,8,8192]{2,1,0:T(8,128)S(1)} %get-tuple-element.71.own, ...), custom_call_target="tpu_custom_call" | custom-call | flops 20971520 | bytes 2097152 | tf_op jit(solution)/shard_map/mix/pallas_call | solution.py:497
  44.9 0.7 collective-permute-start.10
  45.6 0.1 collective-permute-start.1
  45.7 8.7 %collective-permute-done.22.received = s32[2,8,8192]{2,1,0:T(8,128)S(1)} collective-permute-done((s32[2,8,8192]{2,1,0:T(8,128)S(1)}, s32[2,8,8192]{2,1,0:T(8,128)S(1)}, u32[]{:S(2)}, u32[]{:S(2)}) %collective-permute-start.22) | collective-permute-done | bytes 524320 | tf_op jit(solution)/shard_map/ppermute | solution.py:700
  54.4 2.4 %collective-permute-start.2 = (s32[2,8,8192]{2,1,0:T(8,128)S(1)}, s32[2,8,8192]{2,1,0:T(8,128)S(1)}, u32[]{:S(2)}, u32[]{:S(2)}) collective-permute-start(s32[2,8,8192]{2,1,0:T(8,128)S(1)} %get-tuple-element.57), channel_id=1, source_target_pairs={{0,6},{1,7},{2,4},{3,5},{4,2},{5,3},{6,0},{7,1},{8,14},{9,15},{10,... | collective-permute-start | bytes 1572872 | tf_op jit(solution)/shard_map/ppermute | solution.py:691
  56.8 1.8 %mix.14 = (s32[2,8,8192]{2,1,0:T(8,128)S(1)}, s32[1,8,8192]{2,1,0:T(8,128)S(1)}, s32[1,8,8192]{2,1,0:T(8,128)S(1)}) custom-call(f32[2,8,8,128]{3,2,1,0:T(8,128)S(1)} %get-tuple-element.59.targets, bf16[128,128]{1,0:T(8,128)(2,1)S(1)} %get-tuple-element.61.weights, s32[2,8,8192]{2,1,0:T(8,128)S(1)} %get-tuple-element.95.own, ...), custom_call_target="tpu_custom_call" | custom-call | flops 20971520 | bytes 2097152 | tf_op jit(solution)/shard_map/mix/pallas_call | solution.py:497
  58.6 4.7 %collective-permute-done.17.received.rest_2_ = s32[2,8,8192]{2,1,0:T(8,128)S(1)} collective-permute-done((s32[2,8,8192]{2,1,0:T(8,128)S(1)}, s32[2,8,8192]{2,1,0:T(8,128)S(1)}, u32[]{:S(2)}, u32[]{:S(2)}) %collective-permute-start.17) | collective-permute-done | bytes 524320 | tf_op jit(solution)/shard_map/ppermute | solution.py:700
  63.3 0.7 collective-permute-start.23
  64.0 1.8 %mix.12 = (s32[2,8,8192]{2,1,0:T(8,128)S(1)}, s32[1,8,8192]{2,1,0:T(8,128)S(1)}, s32[1,8,8192]{2,1,0:T(8,128)S(1)}) custom-call(f32[2,8,8,128]{3,2,1,0:T(8,128)S(1)} %get-tuple-element.59.targets, bf16[128,128]{1,0:T(8,128)(2,1)S(1)} %get-tuple-element.61.weights, s32[2,8,8192]{2,1,0:T(8,128)S(1)} %get-tuple-element.84.own, ...), custom_call_target="tpu_custom_call" | custom-call | flops 20971520 | bytes 2097152 | tf_op jit(solution)/shard_map/mix/pallas_call | solution.py:497
  65.8 0.0 collective-permute-done.rest_0_
  65.8 0.7 collective-permute-start.18
  66.5 1.4 scale.10
  67.9 7.0 %collective-permute-start.11 = (s32[2,8,8192]{2,1,0:T(8,128)S(1)}, s32[2,8,8192]{2,1,0:T(8,128)S(1)}, u32[]{:S(2)}, u32[]{:S(2)}) collective-permute-start(s32[2,8,8192]{2,1,0:T(8,128)S(1)} %get-tuple-element.75), channel_id=1, source_target_pairs={{0,8},{24,16},{8,0},{16,24},{1,9},{25,17},{9,1},{17,25},{2,10},{26... | collective-permute-start | bytes 1572872 | tf_op jit(solution)/shard_map/ppermute | solution.py:700
  75.0 1.4 scale.13
  76.4 7.6 %collective-permute-start.24 = (s32[2,8,8192]{2,1,0:T(8,128)S(1)}, s32[2,8,8192]{2,1,0:T(8,128)S(1)}, u32[]{:S(2)}, u32[]{:S(2)}) collective-permute-start(s32[2,8,8192]{2,1,0:T(8,128)S(1)} %get-tuple-element.99), channel_id=1, source_target_pairs={{0,8},{24,16},{8,0},{16,24},{1,9},{25,17},{9,1},{17,25},{2,10},{26... | collective-permute-start | bytes 1572872 | tf_op jit(solution)/shard_map/ppermute | solution.py:700
  83.9 1.4 scale.12
  85.3 6.7 %collective-permute-start.19 = (s32[2,8,8192]{2,1,0:T(8,128)S(1)}, s32[2,8,8192]{2,1,0:T(8,128)S(1)}, u32[]{:S(2)}, u32[]{:S(2)}) collective-permute-start(s32[2,8,8192]{2,1,0:T(8,128)S(1)} %get-tuple-element.89), channel_id=1, source_target_pairs={{0,8},{24,16},{8,0},{16,24},{1,9},{25,17},{9,1},{17,25},{2,10},{26... | collective-permute-start | bytes 1572872 | tf_op jit(solution)/shard_map/ppermute | solution.py:700
  92.0 0.0 collective-permute-done.11.received.rest_5_
  92.0 1.8 %mix.10 = (s32[2,8,8192]{2,1,0:T(8,128)S(1)}, s32[1,8,8192]{2,1,0:T(8,128)S(1)}, s32[1,8,8192]{2,1,0:T(8,128)S(1)}) custom-call(f32[2,8,8,128]{3,2,1,0:T(8,128)S(1)} %get-tuple-element.59.targets, bf16[128,128]{1,0:T(8,128)(2,1)S(1)} %get-tuple-element.61.weights, s32[2,8,8192]{2,1,0:T(8,128)S(1)} %get-tuple-element.74.own, ...), custom_call_target="tpu_custom_call" | custom-call | flops 20971520 | bytes 2097152 | tf_op jit(solution)/shard_map/mix/pallas_call | solution.py:497
  93.8 0.7 collective-permute-start.12
  94.5 4.4 %collective-permute-done.24.received.rest_8_ = s32[2,8,8192]{2,1,0:T(8,128)S(1)} collective-permute-done((s32[2,8,8192]{2,1,0:T(8,128)S(1)}, s32[2,8,8192]{2,1,0:T(8,128)S(1)}, u32[]{:S(2)}, u32[]{:S(2)}) %collective-permute-start.24) | collective-permute-done | bytes 524320 | tf_op jit(solution)/shard_map/ppermute | solution.py:700
  99.0 1.8 %mix.15 = (s32[2,8,8192]{2,1,0:T(8,128)S(1)}, s32[1,8,8192]{2,1,0:T(8,128)S(1)}, s32[1,8,8192]{2,1,0:T(8,128)S(1)}) custom-call(f32[2,8,8,128]{3,2,1,0:T(8,128)S(1)} %get-tuple-element.59.targets, bf16[128,128]{1,0:T(8,128)(2,1)S(1)} %get-tuple-element.61.weights, s32[2,8,8192]{2,1,0:T(8,128)S(1)} %get-tuple-element.102.own, ...), custom_call_target="tpu_custom_call" | custom-call | flops 20971520 | bytes 2097152 | tf_op jit(solution)/shard_map/mix/pallas_call | solution.py:497
  100.8 0.7 collective-permute-start.25
  101.5 5.3 %collective-permute-done.19.received.rest_11_ = s32[2,8,8192]{2,1,0:T(8,128)S(1)} collective-permute-done((s32[2,8,8192]{2,1,0:T(8,128)S(1)}, s32[2,8,8192]{2,1,0:T(8,128)S(1)}, u32[]{:S(2)}, u32[]{:S(2)}) %collective-permute-start.19) | collective-permute-done | bytes 524320 | tf_op jit(solution)/shard_map/ppermute | solution.py:700
  106.8 1.8 %mix.13 = (s32[2,8,8192]{2,1,0:T(8,128)S(1)}, s32[1,8,8192]{2,1,0:T(8,128)S(1)}, s32[1,8,8192]{2,1,0:T(8,128)S(1)}) custom-call(f32[2,8,8,128]{3,2,1,0:T(8,128)S(1)} %get-tuple-element.59.targets, bf16[128,128]{1,0:T(8,128)(2,1)S(1)} %get-tuple-element.61.weights, s32[2,8,8192]{2,1,0:T(8,128)S(1)} %get-tuple-element.88.own, ...), custom_call_target="tpu_custom_call" | custom-call | flops 20971520 | bytes 2097152 | tf_op jit(solution)/shard_map/mix/pallas_call | solution.py:497
  108.6 0.7 collective-permute-start.20
  109.3 0.0 collective-permute-done.3.rest_3_.rest_0_
  109.3 1.4 scale.11
  110.7 3.4 %collective-permute-start.13 = (s32[2,8,8192]{2,1,0:T(8,128)S(1)}, s32[2,8,8192]{2,1,0:T(8,128)S(1)}, u32[]{:S(2)}, u32[]{:S(2)}) collective-permute-start(s32[2,8,8192]{2,1,0:T(8,128)S(1)} %get-tuple-element.79), channel_id=1, source_target_pairs={{0,8},{24,16},{8,0},{16,24},{1,9},{25,17},{9,1},{17,25},{2,10},{26... | collective-permute-start | bytes 1572872 | tf_op jit(solution)/shard_map/ppermute | solution.py:700
  114.1 0.2 forward.3
  114.3 1.3 collective-permute-start.26
  115.6 0.2 forward.2
  115.8 1.3 collective-permute-start.21
  117.1 8.8 %collective-permute-done.13.received.rest_14_ = s32[2,8,8192]{2,1,0:T(8,128)S(1)} collective-permute-done((s32[2,8,8192]{2,1,0:T(8,128)S(1)}, s32[2,8,8192]{2,1,0:T(8,128)S(1)}, u32[]{:S(2)}, u32[]{:S(2)}) %collective-permute-start.13) | collective-permute-done | bytes 524320 | tf_op jit(solution)/shard_map/ppermute | solution.py:700
  125.9 1.8 %mix.11 = (s32[1,8,8192]{2,1,0:T(8,128)S(1)}, s32[1,8,8192]{2,1,0:T(8,128)S(1)}, s32[1,8,8192]{2,1,0:T(8,128)S(1)}, s32[1,8,8192]{2,1,0:T(8,128)S(1)}) custom-call(f32[2,8,8,128]{3,2,1,0:T(8,128)S(1)} %get-tuple-element.59.targets, bf16[128,128]{1,0:T(8,128)(2,1)S(1)} %get-tuple-element.61.weights, s32[2,8,8192]{2,1,0:T(8,128)S(1)} %get-tuple-element.78.own, ...), custom_call_target="tpu_custom_call" | custom-call | flops 20971520 | bytes 2097152 | tf_op jit(solution)/shard_map/mix/pallas_call | solution.py:497
  127.7 0.7 collective-permute-start.14
  128.4 1.3 collective-permute-start.15
  129.7 1.3 collective-permute-start.16
  131.0 2.8 %spread.1 = f32[4,8,65536]{2,1,0:T(8,128)} custom-call(s32[2]{0:T(128)S(1)} %pad_add_fusion.place, f32[5,4,8,128]{3,2,1,0:T(8,128)S(1)} %get-tuple-element.54.columns, s32[2,8,8192]{2,1,0:T(8,128)S(1)} %collective-permute-done.rest_0_, s32[2,8,8192]{2,1,0:T(8,128)S(1)} %collective-permute-done.1.rest_1_.rest_0_, ...), custom_call_target="tpu_custom_call", output_to_operand_aliasing={{}: (6, {})} | custom-call | flops 20971520 | bytes 6291456 | tf_op jit(solution)/shard_map/spread/pallas_call | solution.py:442
  133.8 2.9 %finish.3.rest_3_ = f32[2,8,65536]{2,1,0:T(8,128)} custom-call(s32[2]{0:T(128)S(1)} %pad_add_fusion.place, f32[2,8,8,128]{3,2,1,0:T(8,128)S(1)} %get-tuple-element.59.targets, s32[1,8,8192]{2,1,0:T(8,128)S(1)} %get-tuple-element.93.rest_0_, s32[2,8,8192]{2,1,0:T(8,128)S(1)} %collective-permute-done.6.rest_2_.rest_1_, ...), custom_call_target="tpu_custom_call" | custom-call | flops 15728640 | bytes 7864320 | tf_op jit(solution)/shard_map/finish/pallas_call | solution.py:596
  136.7 2.7 %collective-permute-done.21.rest_2_ = s32[1,8,8192]{2,1,0:T(8,128)S(1)} collective-permute-done((s32[1,8,8192]{2,1,0:T(8,128)S(1)}, s32[1,8,8192]{2,1,0:T(8,128)S(1)}, u32[]{:S(2)}, u32[]{:S(2)}) %collective-permute-start.21) | collective-permute-done | bytes 262176 | tf_op jit(solution)/shard_map/ppermute | solution.py:711
  139.4 1.5 finish.4.rest_4_
  140.9 5.0 %collective-permute-done.15.rest_2_ = s32[1,8,8192]{2,1,0:T(8,128)S(1)} collective-permute-done((s32[1,8,8192]{2,1,0:T(8,128)S(1)}, s32[1,8,8192]{2,1,0:T(8,128)S(1)}, u32[]{:S(2)}, u32[]{:S(2)}) %collective-permute-start.15) | collective-permute-done | bytes 262176 | tf_op jit(solution)/shard_map/ppermute | solution.py:711
  145.9 4.7 %collective-permute-done.16.rest_3_ = s32[1,8,8192]{2,1,0:T(8,128)S(1)} collective-permute-done((s32[1,8,8192]{2,1,0:T(8,128)S(1)}, s32[1,8,8192]{2,1,0:T(8,128)S(1)}, u32[]{:S(2)}, u32[]{:S(2)}) %collective-permute-start.16) | collective-permute-done | bytes 262176 | tf_op jit(solution)/shard_map/ppermute | solution.py:713
  150.6 1.6 %finish.5 = f32[2,8,65536]{2,1,0:T(8,128)} custom-call(s32[2]{0:T(128)S(1)} %pad_add_fusion.place, f32[2,8,8,128]{3,2,1,0:T(8,128)S(1)} %get-tuple-element.59.targets, s32[1,8,8192]{2,1,0:T(8,128)S(1)} %get-tuple-element.80.rest_0_, s32[1,8,8192]{2,1,0:T(8,128)S(1)} %collective-permute-done.14.rest_1_, ...), custom_call_target="tpu_custom_call", output_to_operand_aliasing={{}: (6, {})} | custom-call | flops 2621440 | bytes 1310720 | tf_op jit(solution)/shard_map/finish/pallas_call | solution.py:596
  (14 shorter events, 0.0 us)
Async XLA Ops:
  3.0 16.1 %collective-permute-start.5 = (s32[2,8,8192]{2,1,0:T(8,128)S(1)}, s32[2,8,8192]{2,1,0:T(8,128)S(1)}, u32[]{:S(2)}, u32[]{:S(2)}) collective-permute-start(s32[2,8,8192]{2,1,0:T(8,128)S(1)} %get-tuple-element.62.own), channel_id=1, source_target_pairs={{0,8},{24,16},{1,9},{25,17},{2,10},{26,18},{3,11},{27,19},{4,12},{... | collective-permute-start | bytes 1572872 | tf_op jit(solution)/shard_map/ppermute | solution.py:700
  13.4 8.3 %collective-permute-start.8 = (s32[2,8,8192]{2,1,0:T(8,128)S(1)}, s32[2,8,8192]{2,1,0:T(8,128)S(1)}, u32[]{:S(2)}, u32[]{:S(2)}) collective-permute-start(s32[2,8,8192]{2,1,0:T(8,128)S(1)} %get-tuple-element.66), channel_id=1, source_target_pairs={{0,1},{1,0},{2,3},{3,2},{4,5},{5,4},{6,7},{7,6},{8,9},{9,8},{10,11... | collective-permute-start | bytes 1572872 | tf_op jit(solution)/shard_map/ppermute | solution.py:691
  13.5 20.8 %collective-permute-start.4 = (s32[2,8,8192]{2,1,0:T(8,128)S(1)}, s32[2,8,8192]{2,1,0:T(8,128)S(1)}, u32[]{:S(2)}, u32[]{:S(2)}) collective-permute-start(s32[2,8,8192]{2,1,0:T(8,128)S(1)} %get-tuple-element.60), channel_id=1, source_target_pairs={{0,4},{1,5},{2,6},{3,7},{4,0},{5,1},{6,2},{7,3},{8,12},{9,13},{10,... | collective-permute-start | bytes 1572872 | tf_op jit(solution)/shard_map/ppermute | solution.py:691
  15.0 15.8 %collective-permute-start.7 = (s32[2,8,8192]{2,1,0:T(8,128)S(1)}, s32[2,8,8192]{2,1,0:T(8,128)S(1)}, u32[]{:S(2)}, u32[]{:S(2)}) collective-permute-start(s32[2,8,8192]{2,1,0:T(8,128)S(1)} %get-tuple-element.65), channel_id=1, source_target_pairs={{0,2},{1,3},{2,0},{3,1},{4,6},{5,7},{6,4},{7,5},{8,10},{9,11},{10,... | collective-permute-start | bytes 1572872 | tf_op jit(solution)/shard_map/ppermute | solution.py:691
  20.9 13.3 %collective-permute-start.6 = (s32[2,8,8192]{2,1,0:T(8,128)S(1)}, s32[2,8,8192]{2,1,0:T(8,128)S(1)}, u32[]{:S(2)}, u32[]{:S(2)}) collective-permute-start(s32[2,8,8192]{2,1,0:T(8,128)S(1)} %get-tuple-element.64), channel_id=1, source_target_pairs={{8,16},{16,8},{9,17},{17,9},{10,18},{18,10},{11,19},{19,11},{12,20... | collective-permute-start | bytes 1572872 | tf_op jit(solution)/shard_map/ppermute | solution.py:706
  23.6 19.5 %collective-permute-start.9 = (s32[2,8,8192]{2,1,0:T(8,128)S(1)}, s32[2,8,8192]{2,1,0:T(8,128)S(1)}, u32[]{:S(2)}, u32[]{:S(2)}) collective-permute-start(s32[2,8,8192]{2,1,0:T(8,128)S(1)} %get-tuple-element.71.own), channel_id=1, source_target_pairs={{0,8},{24,16},{1,9},{25,17},{2,10},{26,18},{3,11},{27,19},{4,12},{... | collective-permute-start | bytes 1572872 | tf_op jit(solution)/shard_map/ppermute | solution.py:700
  32.9 21.5 %collective-permute-start.22 = (s32[2,8,8192]{2,1,0:T(8,128)S(1)}, s32[2,8,8192]{2,1,0:T(8,128)S(1)}, u32[]{:S(2)}, u32[]{:S(2)}) collective-permute-start(s32[2,8,8192]{2,1,0:T(8,128)S(1)} %get-tuple-element.95.own), channel_id=1, source_target_pairs={{0,8},{24,16},{1,9},{25,17},{2,10},{26,18},{3,11},{27,19},{4,12},{... | collective-permute-start | bytes 1572872 | tf_op jit(solution)/shard_map/ppermute | solution.py:700
  36.4 26.9 %collective-permute-start.17 = (s32[2,8,8192]{2,1,0:T(8,128)S(1)}, s32[2,8,8192]{2,1,0:T(8,128)S(1)}, u32[]{:S(2)}, u32[]{:S(2)}) collective-permute-start(s32[2,8,8192]{2,1,0:T(8,128)S(1)} %get-tuple-element.85), channel_id=1, source_target_pairs={{0,8},{24,16},{8,0},{16,24},{1,9},{25,17},{9,1},{17,25},{2,10},{26... | collective-permute-start | bytes 1572872 | tf_op jit(solution)/shard_map/ppermute | solution.py:700
  40.3 25.5 %collective-permute-start = (s32[2,8,8192]{2,1,0:T(8,128)S(1)}, s32[2,8,8192]{2,1,0:T(8,128)S(1)}, u32[]{:S(2)}, u32[]{:S(2)}) collective-permute-start(s32[2,8,8192]{2,1,0:T(8,128)S(1)} %get-tuple-element.55), channel_id=1, source_target_pairs={{0,3},{1,2},{2,1},{3,0},{4,7},{5,6},{6,5},{7,4},{8,11},{9,10},{10,... | collective-permute-start | bytes 1572872 | tf_op jit(solution)/shard_map/ppermute | solution.py:691
  44.9 21.6 %collective-permute-start.10 = (s32[2,8,8192]{2,1,0:T(8,128)S(1)}, s32[2,8,8192]{2,1,0:T(8,128)S(1)}, u32[]{:S(2)}, u32[]{:S(2)}) collective-permute-start(s32[2,8,8192]{2,1,0:T(8,128)S(1)} %get-tuple-element.73), channel_id=1, source_target_pairs={{8,16},{16,8},{9,17},{17,9},{10,18},{18,10},{11,19},{19,11},{12,20... | collective-permute-start | bytes 1572872 | tf_op jit(solution)/shard_map/ppermute | solution.py:706
  45.6 29.3 %collective-permute-start.1 = (s32[2,8,8192]{2,1,0:T(8,128)S(1)}, s32[2,8,8192]{2,1,0:T(8,128)S(1)}, u32[]{:S(2)}, u32[]{:S(2)}) collective-permute-start(s32[2,8,8192]{2,1,0:T(8,128)S(1)} %get-tuple-element.56), channel_id=1, source_target_pairs={{0,5},{1,4},{2,7},{3,6},{4,1},{5,0},{6,3},{7,2},{8,13},{9,12},{10,... | collective-permute-start | bytes 1572872 | tf_op jit(solution)/shard_map/ppermute | solution.py:691
  54.4 29.6 %collective-permute-start.2 = (s32[2,8,8192]{2,1,0:T(8,128)S(1)}, s32[2,8,8192]{2,1,0:T(8,128)S(1)}, u32[]{:S(2)}, u32[]{:S(2)}) collective-permute-start(s32[2,8,8192]{2,1,0:T(8,128)S(1)} %get-tuple-element.57), channel_id=1, source_target_pairs={{0,6},{1,7},{2,4},{3,5},{4,2},{5,3},{6,0},{7,1},{8,14},{9,15},{10,... | collective-permute-start | bytes 1572872 | tf_op jit(solution)/shard_map/ppermute | solution.py:691
  63.3 11.6 %collective-permute-start.23 = (s32[2,8,8192]{2,1,0:T(8,128)S(1)}, s32[2,8,8192]{2,1,0:T(8,128)S(1)}, u32[]{:S(2)}, u32[]{:S(2)}) collective-permute-start(s32[2,8,8192]{2,1,0:T(8,128)S(1)} %get-tuple-element.97), channel_id=1, source_target_pairs={{8,16},{16,8},{9,17},{17,9},{10,18},{18,10},{11,19},{19,11},{12,20... | collective-permute-start | bytes 1572872 | tf_op jit(solution)/shard_map/ppermute | solution.py:706
  65.8 18.1 %collective-permute-start.18 = (s32[2,8,8192]{2,1,0:T(8,128)S(1)}, s32[2,8,8192]{2,1,0:T(8,128)S(1)}, u32[]{:S(2)}, u32[]{:S(2)}) collective-permute-start(s32[2,8,8192]{2,1,0:T(8,128)S(1)} %get-tuple-element.87), channel_id=1, source_target_pairs={{8,16},{16,8},{9,17},{17,9},{10,18},{18,10},{11,19},{19,11},{12,20... | collective-permute-start | bytes 1572872 | tf_op jit(solution)/shard_map/ppermute | solution.py:706
  67.9 24.1 %collective-permute-start.11 = (s32[2,8,8192]{2,1,0:T(8,128)S(1)}, s32[2,8,8192]{2,1,0:T(8,128)S(1)}, u32[]{:S(2)}, u32[]{:S(2)}) collective-permute-start(s32[2,8,8192]{2,1,0:T(8,128)S(1)} %get-tuple-element.75), channel_id=1, source_target_pairs={{0,8},{24,16},{8,0},{16,24},{1,9},{25,17},{9,1},{17,25},{2,10},{26... | collective-permute-start | bytes 1572872 | tf_op jit(solution)/shard_map/ppermute | solution.py:700
  76.4 22.6 %collective-permute-start.24 = (s32[2,8,8192]{2,1,0:T(8,128)S(1)}, s32[2,8,8192]{2,1,0:T(8,128)S(1)}, u32[]{:S(2)}, u32[]{:S(2)}) collective-permute-start(s32[2,8,8192]{2,1,0:T(8,128)S(1)} %get-tuple-element.99), channel_id=1, source_target_pairs={{0,8},{24,16},{8,0},{16,24},{1,9},{25,17},{9,1},{17,25},{2,10},{26... | collective-permute-start | bytes 1572872 | tf_op jit(solution)/shard_map/ppermute | solution.py:700
  85.3 21.4 %collective-permute-start.19 = (s32[2,8,8192]{2,1,0:T(8,128)S(1)}, s32[2,8,8192]{2,1,0:T(8,128)S(1)}, u32[]{:S(2)}, u32[]{:S(2)}) collective-permute-start(s32[2,8,8192]{2,1,0:T(8,128)S(1)} %get-tuple-element.89), channel_id=1, source_target_pairs={{0,8},{24,16},{8,0},{16,24},{1,9},{25,17},{9,1},{17,25},{2,10},{26... | collective-permute-start | bytes 1572872 | tf_op jit(solution)/shard_map/ppermute | solution.py:700
  92.0 17.3 %collective-permute-start.3 = (s32[2,8,8192]{2,1,0:T(8,128)S(1)}, s32[2,8,8192]{2,1,0:T(8,128)S(1)}, u32[]{:S(2)}, u32[]{:S(2)}) collective-permute-start(s32[2,8,8192]{2,1,0:T(8,128)S(1)} %get-tuple-element.58), channel_id=1, source_target_pairs={{0,7},{1,6},{2,5},{3,4},{4,3},{5,2},{6,1},{7,0},{8,15},{9,14},{10,... | collective-permute-start | bytes 1572872 | tf_op jit(solution)/shard_map/ppermute | solution.py:691
  93.8 15.5 %collective-permute-start.12 = (s32[2,8,8192]{2,1,0:T(8,128)S(1)}, s32[2,8,8192]{2,1,0:T(8,128)S(1)}, u32[]{:S(2)}, u32[]{:S(2)}) collective-permute-start(s32[2,8,8192]{2,1,0:T(8,128)S(1)} %get-tuple-element.77), channel_id=1, source_target_pairs={{8,16},{16,8},{9,17},{17,9},{10,18},{18,10},{11,19},{19,11},{12,20... | collective-permute-start | bytes 1572872 | tf_op jit(solution)/shard_map/ppermute | solution.py:706
  100.8 13.4 %collective-permute-start.25 = (s32[2,8,8192]{2,1,0:T(8,128)S(1)}, s32[2,8,8192]{2,1,0:T(8,128)S(1)}, u32[]{:S(2)}, u32[]{:S(2)}) collective-permute-start(s32[2,8,8192]{2,1,0:T(8,128)S(1)} %get-tuple-element.104), channel_id=1, source_target_pairs={{8,16},{16,8},{9,17},{17,9},{10,18},{18,10},{11,19},{19,11},{12,20... | collective-permute-start | bytes 1572872 | tf_op jit(solution)/shard_map/ppermute | solution.py:706
  108.6 7.0 %collective-permute-start.20 = (s32[2,8,8192]{2,1,0:T(8,128)S(1)}, s32[2,8,8192]{2,1,0:T(8,128)S(1)}, u32[]{:S(2)}, u32[]{:S(2)}) collective-permute-start(s32[2,8,8192]{2,1,0:T(8,128)S(1)} %get-tuple-element.91), channel_id=1, source_target_pairs={{8,16},{16,8},{9,17},{17,9},{10,18},{18,10},{11,19},{19,11},{12,20... | collective-permute-start | bytes 1572872 | tf_op jit(solution)/shard_map/ppermute | solution.py:706
  110.7 15.2 %collective-permute-start.13 = (s32[2,8,8192]{2,1,0:T(8,128)S(1)}, s32[2,8,8192]{2,1,0:T(8,128)S(1)}, u32[]{:S(2)}, u32[]{:S(2)}) collective-permute-start(s32[2,8,8192]{2,1,0:T(8,128)S(1)} %get-tuple-element.79), channel_id=1, source_target_pairs={{0,8},{24,16},{8,0},{16,24},{1,9},{25,17},{9,1},{17,25},{2,10},{26... | collective-permute-start | bytes 1572872 | tf_op jit(solution)/shard_map/ppermute | solution.py:700
  114.3 19.5 %collective-permute-start.26 = (s32[1,8,8192]{2,1,0:T(8,128)S(1)}, s32[1,8,8192]{2,1,0:T(8,128)S(1)}, u32[]{:S(2)}, u32[]{:S(2)}) collective-permute-start(s32[1,8,8192]{2,1,0:T(8,128)S(1)} %forward.3), channel_id=1, source_target_pairs={{8,0},{16,24},{9,1},{17,25},{10,2},{18,26},{11,3},{19,27},{12,4},{... | collective-permute-start | bytes 786440 | tf_op jit(solution)/shard_map/ppermute | solution.py:711
  115.8 23.6 %collective-permute-start.21 = (s32[1,8,8192]{2,1,0:T(8,128)S(1)}, s32[1,8,8192]{2,1,0:T(8,128)S(1)}, u32[]{:S(2)}, u32[]{:S(2)}) collective-permute-start(s32[1,8,8192]{2,1,0:T(8,128)S(1)} %forward.2), channel_id=1, source_target_pairs={{8,0},{16,24},{9,1},{17,25},{10,2},{18,26},{11,3},{19,27},{12,4},{... | collective-permute-start | bytes 786440 | tf_op jit(solution)/shard_map/ppermute | solution.py:711
  127.7 13.2 %collective-permute-start.14 = (s32[1,8,8192]{2,1,0:T(8,128)S(1)}, s32[1,8,8192]{2,1,0:T(8,128)S(1)}, u32[]{:S(2)}, u32[]{:S(2)}) collective-permute-start(s32[1,8,8192]{2,1,0:T(8,128)S(1)} %get-tuple-element.81), channel_id=1, source_target_pairs={{8,16},{16,8},{9,17},{17,9},{10,18},{18,10},{11,19},{19,11},{12,20... | collective-permute-start | bytes 786440 | tf_op jit(solution)/shard_map/ppermute | solution.py:706
  128.4 17.5 %collective-permute-start.15 = (s32[1,8,8192]{2,1,0:T(8,128)S(1)}, s32[1,8,8192]{2,1,0:T(8,128)S(1)}, u32[]{:S(2)}, u32[]{:S(2)}) collective-permute-start(s32[1,8,8192]{2,1,0:T(8,128)S(1)} %get-tuple-element.82), channel_id=1, source_target_pairs={{8,0},{16,24},{9,1},{17,25},{10,2},{18,26},{11,3},{19,27},{12,4},{... | collective-permute-start | bytes 786440 | tf_op jit(solution)/shard_map/ppermute | solution.py:711
  129.7 20.9 %collective-permute-start.16 = (s32[1,8,8192]{2,1,0:T(8,128)S(1)}, s32[1,8,8192]{2,1,0:T(8,128)S(1)}, u32[]{:S(2)}, u32[]{:S(2)}) collective-permute-start(s32[1,8,8192]{2,1,0:T(8,128)S(1)} %get-tuple-element.83), channel_id=1, source_target_pairs={{8,24},{16,0},{9,25},{17,1},{10,26},{18,2},{11,27},{19,3},{12,28},... | collective-permute-start | bytes 786440 | tf_op jit(solution)/shard_map/ppermute | solution.py:713

commit v4 on v3

v4 whole, which is shorter than its diff:
```python
import functools

import jax
import jax.numpy as jnp
from jax import lax
from jax.experimental import pallas as pl
from jax.experimental.pallas import tpu as pltpu
from jax.sharding import PartitionSpec as P

LANES = 128
MIB = 1024 * 1024
HERE = pl.BlockSpec(memory_space=pltpu.VMEM)
FAR = pl.BlockSpec(memory_space=pl.ANY)
SCALARS = pl.BlockSpec(memory_space=pltpu.SMEM)


def log2(number):
    assert number & (number - 1) == 0
    return number.bit_length() - 1


def pack_pair(first, second):
    return first | lax.shift_left(second, 16)


def halves(word):
    return word & 0xFFFF, lax.shift_right_logical(word, 16)


def centred(amount, modulus, inverse):
    return amount - jnp.round(amount * inverse) * modulus


def residue(amount, modulus, inverse):
    remain = centred(amount, modulus, inverse)
    return jnp.where(remain < 0, remain + modulus, remain)


def join_residues(first, second, modulus):
    total = first + second
    less = total - modulus
    return jnp.where(less < 0, total, less)


def spread(column, width):
    return jnp.concatenate([column] * (width // LANES), axis=1)


def params(limit):
    return pltpu.CompilerParams(vmem_limit_bytes=limit * MIB)


def cost(elements, ops, moved):
    return pl.CostEstimate(flops=elements * ops, bytes_accessed=moved, transcendentals=0)


def loop(count, body):
    lax.fori_loop(0, count, lambda step, carry: (body(step), carry)[1], 0)


def span_of(step, tile):
    return pl.ds(pl.multiple_of(step * tile, tile), tile)


def constants(limit):
    return lambda number: jnp.full(limit, number, jnp.int32).astype(jnp.float32)


def product(left, right):
    return jnp.dot(left, right, preferred_element_type=jnp.float32)


def bytes_of(table):
    parts = (table & 0xFF, lax.shift_right_logical(table, 8))
    return [part.astype(jnp.float32).astype(jnp.bfloat16) for part in parts]


def level_rows(place, levels, block, source_count):
    lane = lax.broadcasted_iota(jnp.int32, (block, source_count), 1)
    rank = lax.broadcasted_iota(jnp.int32, (block, source_count), 0)
    level_rank = jnp.zeros((block, source_count), jnp.int32)
    for n in range(block):
        level_rank = jnp.where(rank == n, levels[place[1] * block + n] - 1, level_rank)
    return lane, level_rank, jnp.where(lane == level_rank, 1.0, 0.0).astype(jnp.bfloat16)


def build_columns(place, levels, moduli, inverse, columns):
    group = place[0]
    limbs, block = columns.shape[1], columns.shape[2]
    lane, level_rank, onehot = level_rows(place, levels, block, inverse.shape[0])
    inverse_low, inverse_high = (product(onehot, part) for part in bytes_of(inverse[...]))
    inverse_rows = jnp.where(lane <= level_rank, inverse_low + 256.0 * inverse_high, 0.0)
    live_rows = jnp.where(lane <= level_rank, 1.0, 0.0)
    shape = (block, LANES)
    fill = constants(shape)
    for limb in range(limbs):
        index = group * limbs + limb
        here = lane == index
        picked = jnp.sum(jnp.where(here, inverse_rows, 0.0), axis=1, keepdims=True)
        picked = jnp.broadcast_to(picked, shape)
        live = jnp.broadcast_to(jnp.sum(jnp.where(here, live_rows, 0.0), axis=1, keepdims=True), shape)
        high = jnp.floor((picked + 128.0) * (1.0 / 256.0))
        modulus = fill(moduli[index])
        columns[0, limb] = high
        columns[1, limb] = picked - 256.0 * high
        columns[2, limb] = live / modulus
        columns[3, limb] = modulus
        columns[4, limb] = 1.0 / modulus


def build_weights(place, levels, moduli, cross, limbs, targets, weights):
    group = place[0]
    total, block = targets.shape[1:3]
    source_count = cross.shape[0]
    quarter = total // 4
    fill = constants((block, LANES))
    onehot = level_rows(place, levels, block, source_count)[2]
    left = group < 2
    inner = (group == 1) | (group == 2)
    order = (jnp.where(left, 2, 1), jnp.where(left, 3, 0), group ^ 1, group)
    rows = []
    for target in range(total):
        index = order[target // quarter] * quarter + target % quarter
        rows += [product(onehot, part) for part in bytes_of(cross[:, index, :])]
    width = weights.shape[1]
    entry = lax.broadcasted_iota(jnp.int32, (source_count, width), 0)
    column = lax.broadcasted_iota(jnp.int32, (source_count, width), 1)
    received = lax.shift_right_logical(column, log2(2 * block * limbs))
    limb = lax.shift_right_logical(column, log2(2 * block)) & (limbs - 1)
    limb = limb + jnp.where(received == 0, group * limbs, (group ^ 1) * limbs)
    choose = jnp.where(entry == limb, 1.0, 0.0).astype(jnp.bfloat16)
    chosen = product(jnp.concatenate(rows, axis=0).astype(jnp.bfloat16), choose)
    column = lax.broadcasted_iota(jnp.int32, (block, width), 1)
    same = (column & (block - 1)) == lax.broadcasted_iota(jnp.int32, (block, width), 0)
    upper = (lax.shift_right_logical(column, log2(block)) & 1) == 1
    from_outer = lax.shift_right_logical(column, log2(2 * block * limbs)) == 1
    results = []
    for target in range(total):
        index = order[target // quarter] * quarter + target % quarter
        modulus = fill(moduli[source_count + index])
        inverse_modulus = 1.0 / modulus
        targets[0, target] = modulus
        targets[1, target] = inverse_modulus
        modulus, inverse_modulus = spread(modulus, width), spread(inverse_modulus, width)
        first = 2 * target * block
        value = chosen[first : first + block] + 256.0 * chosen[first + block : first + 2 * block]
        value = jnp.where(upper, residue(256.0 * value, modulus, inverse_modulus), value)
        use = jnp.where(inner, 1, 0) if target // quarter != 2 else 0
        value = jnp.where(same & ((from_outer == False) | (use > 0)), value, 0.0)
        high_byte = jnp.floor(value * (1.0 / 256.0))
        results += [value - 256.0 * high_byte, high_byte]
    weights[...] = jnp.concatenate(results, axis=0).astype(jnp.bfloat16)


def scale_tile(values, columns, scaled, read, write):
    width = write.size
    for word in range(scaled.shape[0]):
        if values.dtype == jnp.int32:
            pair = halves(values[word, :, read])
        else:
            pair = (values[2 * word, :, read], values[2 * word + 1, :, read])
        results = []
        for side, value in enumerate(pair):
            value = value.astype(jnp.float32)
            high, low, _, modulus, inverse = (spread(columns[kind, 2 * word + side], width) for kind in range(5))
            upper = centred(value * high, modulus, inverse)
            results.append(residue(256.0 * upper + value * low, modulus, inverse).astype(jnp.int32))
        scaled[word, :, write] = pack_pair(*results)


def first_kernel(place, *rest):
    tables, residues, scaled, landing, columns = rest[:3], *rest[3:7]
    copies, (sems, table_sems) = rest[7:-2], rest[-2:]
    block, width = landing.shape[1:]
    tile = width // sems.shape[0]

    def load(step):
        return pltpu.make_async_copy(
            residues.at[:, pl.ds(pl.multiple_of(place[1] * block, block), block), span_of(step, tile)],
            landing.at[:, :, span_of(step, tile)],
            sems.at[step],
        )

    @pl.when((place[0] != 1) & (place[0] != 2))
    def _():
        steps = width // tile
        fetches = [pltpu.make_async_copy(a, b, table_sems.at[i]) for i, (a, b) in enumerate(zip(tables, copies))]
        for fetch in fetches:
            fetch.start()
        loop(steps, lambda step: load(step).start())
        for fetch in fetches:
            fetch.wait()
        build_columns(place, *copies, columns)

        def body(step):
            load(step).wait()
            span = span_of(step, tile)
            scale_tile(landing, columns, scaled, span, span)

        loop(steps, body)


def tile_of(width, most=1024):
    return next(tile for tile in range(min(width, most), 0, -LANES) if width % tile == 0)


def first(place, levels, moduli, inverse_table, residues, block, length):
    limbs = residues.shape[0]
    steps = length // tile_of(length)
    return pl.pallas_call(
        first_kernel,
        in_specs=[SCALARS] + [FAR] * 4,
        out_specs=HERE,
        out_shape=pltpu.VMEM((limbs // 2, block, length), jnp.int32),
        scratch_shapes=[
            pltpu.VMEM((limbs, block, length), jnp.float32),
            pltpu.VMEM((5, limbs, block, LANES), jnp.float32),
            pltpu.SMEM(levels.shape, jnp.int32),
            pltpu.SMEM(moduli.shape, jnp.int32),
            pltpu.VMEM(inverse_table.shape, jnp.int32),
            pltpu.SemaphoreType.DMA((steps,)),
            pltpu.SemaphoreType.DMA((3,)),
        ],
        compiler_params=params(8),
        cost_estimate=cost(limbs * block * length, 60, 10 * limbs * block * length),
        name="first",
    )(place, *(far(x) for x in (levels, moduli, inverse_table, residues)))


def far(array):
    return pltpu.with_memory_space_constraint(array, pltpu.HBM)


def pack_kernel(offsets, tables, place, residues, *rest):
    if tables:
        arrays, rest = rest[:4], rest[4:]
        columns, targets, weights, scaled, *rest = rest
        *rest, level_copy, moduli_copy, inverse_copy, cross_copy, table_sems = rest
        copies = (level_copy, moduli_copy, inverse_copy, cross_copy)
    *outs, landing, sems = rest
    _, limbs, block, width = landing.shape
    tile = tile_of(width)

    def load(turn):
        peer = place[1] ^ offsets[turn]
        return pltpu.make_async_copy(
            residues.at[:, pl.ds(pl.multiple_of(peer * block, block), block), :], landing.at[turn], sems.at[turn]
        )

    if tables:
        fetches = [pltpu.make_async_copy(a, b, table_sems.at[i]) for i, (a, b) in enumerate(zip(arrays, copies))]
        for fetch in fetches:
            fetch.start()
    for turn in range(len(offsets)):
        load(turn).start()
    if tables:
        for fetch in fetches:
            fetch.wait()
        build_columns(place, level_copy, moduli_copy, inverse_copy, columns)
        build_weights(place, level_copy, moduli_copy, cross_copy, limbs, targets, weights)
    for turn, out in enumerate(outs):
        load(turn).wait()

        def body(step):
            span = span_of(step, tile)
            for word in range(limbs // 2):
                one = landing[turn, 2 * word, :, span].astype(jnp.int32)
                two = landing[turn, 2 * word + 1, :, span].astype(jnp.int32)
                out[word, :, span] = pack_pair(one, two)
            if offsets[turn] == 0:
                scale_tile(landing.at[turn], columns, scaled, span, span)

        loop(width // tile, body)


def pack_blocks(place, residues, offsets, block, tables=()):
    limbs, _, width = residues.shape
    blocks = len(offsets)
    words = pltpu.VMEM((limbs // 2, block, width), jnp.int32)
    shapes, scratch = [], []
    if tables:
        levels, moduli, inverse_table, cross = tables
        total = cross.shape[1]
        shapes = [
            pltpu.VMEM((5, limbs, block, LANES), jnp.float32),
            pltpu.VMEM((2, total, block, LANES), jnp.float32),
            pltpu.VMEM((2 * total * block, 4 * limbs * block), jnp.bfloat16),
            words,
        ]
        scratch = [
            pltpu.SMEM(levels.shape, jnp.int32),
            pltpu.SMEM(moduli.shape, jnp.int32),
            pltpu.VMEM(inverse_table.shape, jnp.int32),
            pltpu.VMEM(cross.shape, jnp.int32),
            pltpu.SemaphoreType.DMA((4,)),
        ]
    results = pl.pallas_call(
        functools.partial(pack_kernel, offsets, bool(tables)),
        in_specs=[SCALARS] + [FAR] * (1 + len(tables)),
        out_specs=[HERE] * (len(shapes) + blocks),
        out_shape=shapes + [words] * blocks,
        scratch_shapes=[
            pltpu.VMEM((blocks, limbs, block, width), jnp.float32),
            pltpu.SemaphoreType.DMA((blocks,)),
        ]
        + scratch,
        compiler_params=params(10),
        cost_estimate=cost(blocks * limbs * block * width, 16, 6 * blocks * limbs * block * width),
        name="pack",
    )(place, *(far(x) for x in (residues, *tables)))
    return results[: len(shapes)], dict(zip(offsets, results[len(shapes) :]))


def scale_kernel(chunk, relay, place, columns, targets, *rest):
    offsets, low, high = chunk
    values, rest = rest[: len(offsets)], rest[len(offsets) :]
    if relay:
        outer, arrived, scaled, send = rest
    else:
        (scaled,) = rest
    length = high - low
    tile = tile_of(length)
    inner = (place[0] == 1) | (place[0] == 2)
    for turn in range(len(offsets)):

        def body(step):
            write = pl.ds(pl.multiple_of(turn * length + step * tile, tile), tile)
            read = pl.ds(pl.multiple_of(low + step * tile, tile), tile)
            scale_tile(values[turn], columns, scaled, read, write)
            if relay:
                for word in range(send.shape[0]):
                    words = scaled[word, :, write]
                    if word < outer.shape[0]:
                        words = jnp.where(inner, relay_word(targets, outer, arrived, word, write), words)
                    send[word, :, write] = words

        loop(length // tile, body)


def scale_chunk(place, columns, targets, values, chunk, relay=None):
    words, block, _ = values[0].shape
    parts = len(values)
    length = parts * (chunk[2] - chunk[1])
    operands = [place, columns, targets, *values, *(relay or ())]
    count = 2 if relay else 1
    results = pl.pallas_call(
        functools.partial(scale_kernel, chunk, relay is not None),
        in_specs=[SCALARS] + [HERE] * (len(operands) - 1),
        out_specs=[HERE] * count,
        out_shape=[pltpu.VMEM((words, block, length), jnp.int32)] * count,
        compiler_params=params(4),
        cost_estimate=cost(2 * words * block * length, 40, 16 * words * block * length),
        name="scale",
    )(*operands)
    return results[0], results[-1]


def spread_kernel(pieces, place, columns, *rest):
    values = rest[: len(pieces)]
    source, stage, sems = rest[-3:]
    tile = stage.shape[3]
    stores = []
    for turn, (offset, low, high, width) in enumerate(pieces):
        steps = (high - low) // tile
        base = sum((p[2] - p[1]) // tile for p in pieces[:turn])

        def store(step, base=base, offset=offset, low=low, width=width):
            return pltpu.make_async_copy(
                stage.at[base + step],
                source.at[:, :, pl.ds(pl.multiple_of((place[1] ^ offset) * width + low + step * tile, tile), tile)],
                sems.at[base + step],
            )

        def body(step):
            read = pl.ds(pl.multiple_of(low + step * tile, tile), tile)
            for word in range(values[turn].shape[0]):
                for side, value in enumerate(halves(values[turn][word, :, read])):
                    limb = 2 * word + side
                    stage[base + step, limb] = value.astype(jnp.float32) * spread(columns[2, limb], tile)
            store(step).start()

        loop(steps, body)
        stores.append((steps, store))
    for steps, store in stores:
        loop(steps, lambda step: store(step).wait())


def spread_blocks(place, columns, values, offsets, shape, buffer):
    words, block, width = values[0].shape
    tile = tile_of(width)
    pieces = tuple((offset, 0, width, width) for offset in offsets)
    slots = len(pieces) * (width // tile)
    operands = [place, columns, *values]
    in_specs = [SCALARS] + [HERE] * (len(operands) - 1)
    aliases = {}
    if buffer is not None:
        aliases[len(operands)] = 0
        operands.append(buffer)
        in_specs.append(FAR)
    return pl.pallas_call(
        functools.partial(spread_kernel, pieces),
        in_specs=in_specs,
        out_specs=FAR,
        out_shape=jax.ShapeDtypeStruct(shape, jnp.float32),
        scratch_shapes=[
            pltpu.VMEM((slots, 2 * words, block, tile), jnp.float32),
            pltpu.SemaphoreType.DMA((slots,)),
        ],
        input_output_aliases=aliases,
        compiler_params=params(10),
        cost_estimate=cost(slots * 2 * words * block * tile, 20, 6 * slots * 2 * words * block * tile),
        name="spread",
    )(*operands)


def mix_kernel(first_target, targets, weights, own, received, *outs):
    block = own.shape[1]
    tile = tile_of(own.shape[2], 2048)
    count = 2 * sum(out.shape[0] for out in outs)
    rows = pl.ds(2 * first_target * block, 2 * count * block)

    def body(step):
        span = span_of(step, tile)
        digits = []
        for words in (own, received):
            for word in range(words.shape[0]):
                value = words[word, :, span]
                for byte in range(4):
                    part = lax.shift_right_logical(value, 8 * byte) if byte else value
                    if byte < 3:
                        part = part & 0xFF
                    digits.append(part.astype(jnp.float32))
        stacked = jnp.concatenate(digits, axis=0).astype(jnp.bfloat16)
        sums = product(weights[rows, :], stacked)
        reduced = []
        for target in range(count):
            modulus = spread(targets[0, first_target + target], tile)
            inverse = spread(targets[1, first_target + target], tile)
            low = sums[2 * target * block : (2 * target + 1) * block]
            high = sums[(2 * target + 1) * block : (2 * target + 2) * block]
            upper = centred(high, modulus, inverse)
            reduced.append(residue(256.0 * upper + low, modulus, inverse).astype(jnp.int32))
        words = [pack_pair(reduced[t], reduced[t + 1]) for t in range(0, count, 2)]
        position = 0
        for out in outs:
            for word in range(out.shape[0]):
                out[word, :, span] = words[position]
                position += 1

    loop(own.shape[2] // tile, body)


def mix_chunk(own, received, weights, targets, near):
    words, block, length = own.shape
    total = targets.shape[1]
    counts = (total // 8, total // 8) if near else (total // 4,)
    return pl.pallas_call(
        functools.partial(mix_kernel, total // 2 if near else 0),
        in_specs=[HERE] * 4,
        out_specs=[HERE] * len(counts),
        out_shape=[pltpu.VMEM((count, block, length), jnp.int32) for count in counts],
        compiler_params=params(8),
        cost_estimate=cost(total * block * length, 20, 4 * (2 * words + 2) * block * length),
        name="near" if near else "far",
    )(targets, weights, own, received)


def relay_word(targets, outer, arrived, word, span):
    words = outer.shape[0]
    results = []
    for side, (a, b) in enumerate(zip(halves(outer[word, :, span]), halves(arrived[words + word, :, span]))):
        modulus = spread(targets[0, 4 * words + 2 * word + side].astype(jnp.int32), span.size)
        results.append(join_residues(a, b, modulus))
    return pack_pair(*results)


def forward_kernel(targets, outer, arrived, out):
    tile = tile_of(out.shape[2])

    def body(step):
        span = span_of(step, tile)
        for word in range(out.shape[0]):
            out[word, :, span] = relay_word(targets, outer, arrived, word, span)

    loop(out.shape[2] // tile, body)


def forward_chunk(outer, arrived, targets):
    words, block, length = outer.shape
    return pl.pallas_call(
        forward_kernel,
        in_specs=[HERE] * 3,
        out_specs=HERE,
        out_shape=pltpu.VMEM(outer.shape, jnp.int32),
        compiler_params=params(4),
        cost_estimate=cost(words * block * length, 40, 12 * words * block * length),
        name="forward",
    )(targets, outer, arrived)


def finish_kernel(chunks, full, place, targets, *rest):
    out, stage, sems = rest[-3:]
    tile = stage.shape[3]
    inner = (place[0] == 1) | (place[0] == 2)
    stores = []
    slot = 0
    for turn, (offsets, low, high) in enumerate(chunks):
        mine, arrived, relayed = rest[3 * turn : 3 * turn + 3]
        first_target = 6 * mine.shape[0]
        steps = (high - low) // tile
        for part, offset in enumerate(offsets):

            def store(step, offset=offset, low=low, base=slot):
                start = (place[1] ^ offset) * full + low
                return pltpu.make_async_copy(
                    stage.at[base + step],
                    out.at[:, :, pl.ds(pl.multiple_of(start + step * tile, tile), tile)],
                    sems.at[base + step],
                )

            def body(step):
                span = pl.ds(pl.multiple_of(part * (high - low) + step * tile, tile), tile)
                for word in range(mine.shape[0]):
                    other = jnp.where(inner, arrived[word, :, span], relayed[word, :, span])
                    parts = [halves(mine[word, :, span]), halves(other)]
                    for side, (a, b) in enumerate(zip(*parts)):
                        target = first_target + 2 * word + side
                        modulus = spread(targets[0, target].astype(jnp.int32), tile)
                        total = join_residues(a, b, modulus).astype(jnp.float32)
                        stage[slot + step, 2 * word + side] = total * spread(targets[1, target], tile)
                store(step).start()

            loop(steps, body)
            stores.append((steps, store))
            slot += steps
    for steps, store in stores:
        loop(steps, lambda step: store(step).wait())


def finish_chunks(place, targets, triples, chunks, shape, full, buffer):
    words, block, _ = triples[0][0].shape
    tile = min(tile_of(high - low) for _, low, high in chunks)
    slots = sum(len(offsets) * (high - low) // tile for offsets, low, high in chunks)
    operands = [place, targets, *(array for triple in triples for array in triple)]
    in_specs = [SCALARS] + [HERE] * (len(operands) - 1)
    aliases = {}
    if buffer is not None:
        aliases[len(operands)] = 0
        operands.append(buffer)
        in_specs.append(FAR)
    return pl.pallas_call(
        functools.partial(finish_kernel, chunks, full),
        in_specs=in_specs,
        out_specs=FAR,
        out_shape=jax.ShapeDtypeStruct(shape, jnp.float32),
        scratch_shapes=[
            pltpu.VMEM((slots, 2 * words, block, tile), jnp.float32),
            pltpu.SemaphoreType.DMA((slots,)),
        ],
        input_output_aliases=aliases,
        compiler_params=params(8),
        cost_estimate=cost(2 * words * block * slots * tile, 20, 10 * 2 * words * block * slots * tile),
        name="finish",
    )(*operands)


def chunk_plan(count, width):
    if count == 8:
        order = [(offset,) for offset in (0, 1, 2, 4, 3, 5, 6, 7)]
    else:
        unit = max(1, count // 8)
        edges = sorted({0, 1} | set(range(unit, count + 1, unit)))
        order = [tuple(range(start, end)) for start, end in zip(edges, edges[1:])]
    cut = 5 * width // 8
    plan = [(offsets, 0, width) for offsets in order]
    if cut % LANES == 0:
        plan[-1:] = [(order[-1], 0, cut), (order[-1], cut, width)]
    return plan


LAG = 3


def length_of(chunk):
    return len(chunk[0]) * (chunk[2] - chunk[1])


def riders(plan):
    return {
        step: step - LAG
        for step in range(LAG, len(plan))
        if length_of(plan[step]) == length_of(plan[step - LAG])
    }


def name_of(kind, numbers):
    return kind + "_".join(map(str, numbers))


def peers_of(chunks):
    return list(dict.fromkeys(offset for chunk in chunks for offset in chunk[0] if offset))


def timeline(plan):
    steps = len(plan)
    alone = [step for step in range(steps) if step not in riders(plan).values()]
    soon, later = peers_of(plan[:4]), peers_of(plan[4:])
    later = [offset for offset in later if offset not in soon]
    middle = [offset for offset in peers_of(plan[:6]) if offset not in soon]
    blocks = [0] + peers_of(plan)
    quarter = -(-len(blocks) // 4)
    groups = [blocks[start : start + quarter] for start in range(0, len(blocks), quarter)]
    fill = {3: [name_of("spread", groups[0])], 4: [name_of("spread", groups[1])]}
    fill |= {5: [name_of("finish", [0, 1])], 6: [name_of("spread", groups[2])], 7: [name_of("finish", [2, 3])]}
    events = ["first", "a0", "packa"] + [f"p{offset}" for offset in soon] + ["packb"]
    events += [f"p{offset}" for offset in middle] + ["scale1", "a1"]
    for step in range(steps):
        events += [f"far{step}", f"b{step}", f"near{step}"]
        if step == 0:
            events += [f"p{offset}" for offset in later if offset not in middle]
        if step == steps - 1:
            events += [name_of("spread", group) for group in groups[3:]]
        if step + 2 < steps:
            events += [f"scale{step + 2}", f"a{step + 2}"]
        if step - 1 in alone:
            events += [f"forward{step - 1}", f"c{step - 1}"]
        events += fill.get(step, [])
    last = steps - 1
    events += [name_of("finish", range(4, last - 1)), f"forward{last}", f"c{last}"]
    events += [name_of("finish", [last - 1, last])]
    return events


def per_device(residues, levels, moduli, inverse_table, cross_table):
    target_count = cross_table.shape[2]
    limbs, _, width = residues.shape
    count = lax.axis_size("coef")
    assert lax.axis_size("limb") == 4
    block = residues.shape[1] // count
    place = jnp.stack([lax.axis_index("limb"), lax.axis_index("coef")]).astype(jnp.int32)
    cross = jnp.transpose(cross_table, (0, 2, 1))
    plan = chunk_plan(count, width)
    steps = len(plan)
    ride = riders(plan)

    scaled, send, received, far_sums, near_sums, crossed, relayed = ([None] * steps for _ in range(7))
    arrived = {}
    source, result = None, None
    source_shape = (limbs, block, width * count)
    shape = (target_count // 4, block, width * count)
    soon = tuple(peers_of(plan[:4]))
    for event in timeline(plan):
        kind = event.rstrip("0123456789_")
        numbers = [int(number) for number in event[len(kind) :].split("_") if number]
        step = numbers[0] if numbers else 0
        if kind == "first":
            send[0] = first(place, levels, moduli, inverse_table, residues, block, plan[0][2])
        elif kind == "packa":
            packed = pack_blocks(place, residues, soon, block)[1]
        elif kind == "packb":
            others = tuple(offset for offset in range(count) if offset not in soon)
            tables = (levels, moduli, inverse_table, cross)
            (columns, targets, weights, scaled[0]), more = pack_blocks(place, residues, others, block, tables)
            packed |= more
            arrived[0] = packed[0]
        elif kind == "p":
            arrived[step] = lax.ppermute(packed[step], "coef", [(i, i ^ step) for i in range(count)])
        elif kind == "scale":
            values = [arrived[offset] for offset in plan[step][0]]
            relay = (near_sums[ride[step]][0], crossed[ride[step]]) if step in ride else None
            scaled[step], send[step] = scale_chunk(place, columns, targets, values, plan[step], relay)
        elif kind == "a":
            pairs = [(0, 1), (3, 2)] + ([(1, 0), (2, 3)] if step in ride else [])
            received[step] = lax.ppermute(send[step], "limb", pairs)
            if step in ride:
                relayed[ride[step]] = received[step]
        elif kind == "far":
            (far_sums[step],) = mix_chunk(scaled[step], received[step], weights, targets, False)
        elif kind == "near":
            near_sums[step] = mix_chunk(scaled[step], received[step], weights, targets, True)
        elif kind == "b":
            crossed[step] = lax.ppermute(far_sums[step], "limb", [(1, 2), (2, 1)])
        elif kind == "forward":
            relayed[step] = forward_chunk(near_sums[step][0], crossed[step], targets)
        elif kind == "c":
            relayed[step] = lax.ppermute(relayed[step], "limb", [(1, 0), (2, 3)])
        elif kind == "spread":
            values = [arrived[offset] for offset in numbers]
            source = spread_blocks(place, columns, values, numbers, source_shape, source)
        else:
            triples = [(near_sums[i][1], crossed[i], relayed[i]) for i in numbers]
            chunks = tuple(plan[i] for i in numbers)
            result = finish_chunks(place, targets, triples, chunks, shape, width, result)
    return (source, result)


def solution(mesh):
    placed = (P("limb", None, "coef"), P(), P(), P(), P())

    return jax.shard_map(
        per_device,
        mesh=mesh,
        in_specs=placed,
        out_specs=(P("limb", "coef", None), P("limb", "coef", None)),
        check_vma=False,
    )
```

time: 153 us -> 156 us (1.020)
  Pallas kernels: 42.7 us -> 55.9 us
  waiting for transfers between devices: 49.7 us -> 42.1 us
  starting transfers between devices: 58.5 us -> 55 us
    pallas_call x21 -> x37, Pallas kernels: 42.4 us -> 55.2 us  [the longest x18 20.7 us: mix_chunk(): pl.pallas_call(functools.partial(mix_kernel, total // 2 if near else 0),...]
    ppermute x12 -> x14, waiting for transfers between devices: 12.4 us -> 3.01 us  [the longest x5 2.99 us: per_device(): relayed[step] = lax.ppermute(relayed[step], 'limb', [(1, 0), (2, 3)])]
    ppermute x8 -> x9, starting transfers between devices: 42.2 us -> 36.6 us  [per_device(): received[step] = lax.ppermute(send[step], 'limb', pairs)]
    ppermute x7, waiting for transfers between devices: 0.02 us -> 2.36 us  [per_device(): lax.ppermute(packed[step], 'coef', [(i, i ^ step) for i in range(count)])]
    ppermute x12 -> x14, starting transfers between devices: 10.7 us -> 12.7 us  [the longest x5 6.46 us: per_device(): relayed[step] = lax.ppermute(relayed[step], 'limb', [(1, 0), (2, 3)])]
    ppermute x8 -> x9, waiting for transfers between devices: 37.3 us -> 36.7 us  [per_device(): received[step] = lax.ppermute(send[step], 'limb', pairs)]
  transfers between devices with their start and end apart: 27 -> 30, of which waited for: 10 -> 11; matrix products, arithmetic and copies ran while one was open for 0% -> 0% of each run, Pallas kernels for 26% -> 34%
where the time goes in v4:
time: 156 us; the launch traced here: 154 us
  Pallas kernels  55.9 us (36%)
  starting transfers between devices  55 us (35%)
  waiting for transfers between devices  42.1 us (27%)
    ppermute x9, waiting for transfers between devices, per_device(): received[step] = lax.ppermute(send[step], 'limb', pairs)  36.7 us
    ppermute x9, starting transfers between devices, per_device(): received[step] = lax.ppermute(send[step], 'limb', pairs)  36.6 us
    pallas_call x18, Pallas kernels, mix_chunk(): pl.pallas_call(functools.partial(mix_kernel, total // 2 if near else 0),...  20.7 us
    pallas_call x8, Pallas kernels, scale_chunk(): pl.pallas_call(functools.partial(scale_kernel, chunk, relay is not None),...  10.1 us
    pallas_call x4, Pallas kernels, spread_blocks(): pl.pallas_call(functools.partial(spread_kernel, pieces), in_specs=in_spec...  7.99 us
    pallas_call x2, Pallas kernels, pack_blocks(): pl.pallas_call(functools.partial(pack_kernel, offsets, bool(tables)), in_...  7.17 us
    pallas_call x4, Pallas kernels, finish_chunks(): pl.pallas_call(functools.partial(finish_kernel, chunks, full), in_specs=i...  6.96 us
    ppermute x5, starting transfers between devices, per_device(): relayed[step] = lax.ppermute(relayed[step], 'limb', [(1, 0), (2, 3)])  6.46 us
  transfers between devices with their start and end apart: 30, of which 11 were waited for; matrix products, arithmetic and copies ran while one was open for 0% of the time, Pallas kernels for 34%

profile of v4, /device:TPU:0, one launch (start us, length us, event | category | flops | bytes accessed | tf_op | source)
XLA Modules:
  0.0 154.4 jit_solution(13218341553807577681)
XLA Ops:
  0.7 2.3 %first.1 = s32[2,8,8192]{2,1,0:T(8,128)S(1)} custom-call(s32[2]{0:T(128)S(1)} %pad_add_fusion.place, s32[64]{0:T(128)} %rest_0_.3, s32[24]{0:T(128)} %rest_1_.3, s32[16,16]{1,0:T(8,128)} %rest_2_.3, f32[4,64,8192]{2,1,0:T(8,128)} %rest_3_.1), custom_call_target="tpu_custom_call" | custom-call | flops 15728640 | bytes 2621440 | tf_op jit(solution)/shard_map/first/pallas_call | solution.py:210
  3.0 3.4 %collective-permute-start.23 = (s32[2,8,8192]{2,1,0:T(8,128)S(1)}, s32[2,8,8192]{2,1,0:T(8,128)S(1)}, u32[]{:S(2)}, u32[]{:S(2)}) collective-permute-start(s32[2,8,8192]{2,1,0:T(8,128)S(1)} %first.1), channel_id=1, source_target_pairs={{0,8},{24,16},{1,9},{25,17},{2,10},{26,18},{3,11},{27,19},{4,12},{... | collective-permute-start | bytes 1572872 | tf_op jit(solution)/shard_map/ppermute | solution.py:674
  6.4 2.6 %pack.3 = (s32[2,8,8192]{2,1,0:T(8,128)S(1)}, s32[2,8,8192]{2,1,0:T(8,128)S(1)}, s32[2,8,8192]{2,1,0:T(8,128)S(1)}) custom-call(s32[2]{0:T(128)S(1)} %pad_add_fusion.place, f32[4,64,8192]{2,1,0:T(8,128)} %rest_3_.1), custom_call_target="tpu_custom_call" | custom-call | flops 12582912 | bytes 4718592 | tf_op jit(solution)/shard_map/pack/pallas_call | solution.py:297
  9.0 1.6 %collective-permute-start.4 = (s32[2,8,8192]{2,1,0:T(8,128)S(1)}, s32[2,8,8192]{2,1,0:T(8,128)S(1)}, u32[]{:S(2)}, u32[]{:S(2)}) collective-permute-start(s32[2,8,8192]{2,1,0:T(8,128)S(1)} %get-tuple-element.45), channel_id=1, source_target_pairs={{0,2},{1,3},{2,0},{3,1},{4,6},{5,7},{6,4},{7,5},{8,10},{9,11},{10,... | collective-permute-start | bytes 1572872 | tf_op jit(solution)/shard_map/ppermute | solution.py:667
  10.6 1.5 collective-permute-start.5
  12.1 4.6 %pack.2 = (f32[5,4,8,128]{3,2,1,0:T(8,128)S(1)}, f32[2,8,8,128]{3,2,1,0:T(8,128)S(1)}, bf16[128,128]{1,0:T(8,128)(2,1)S(1)}, s32[2,8,8192]{2,1,0:T(8,128)S(1)}, ...) custom-call(s32[2]{0:T(128)S(1)} %pad_add_fusion.place, ...), custom_call_target="tpu_custom_call" | custom-call | flops 20971520 | bytes 7864320 | tf_op jit(solution)/shard_map/pack/pallas_call | solution.py:297
  16.7 0.8 collective-permute-done.23.received
  17.5 1.3 far.15
  19.5 1.3 scale.10.own
  20.8 8.1 %collective-permute-start.13 = (s32[2,8,8192]{2,1,0:T(8,128)S(1)}, s32[2,8,8192]{2,1,0:T(8,128)S(1)}, u32[]{:S(2)}, u32[]{:S(2)}) collective-permute-start(s32[2,8,8192]{2,1,0:T(8,128)S(1)} %scale.10.own), channel_id=1, source_target_pairs={{0,8},{24,16},{1,9},{25,17},{2,10},{26,18},{3,11},{27,19},{4,12},{... | collective-permute-start | bytes 1572872 | tf_op jit(solution)/shard_map/ppermute | solution.py:674
  28.9 1.3 scale.12.own
  30.2 1.3 collective-permute-start.18
  31.5 1.3 near.15
  32.8 1.4 scale.14
  34.2 4.2 %collective-permute-start.25 = (s32[2,8,8192]{2,1,0:T(8,128)S(1)}, s32[2,8,8192]{2,1,0:T(8,128)S(1)}, u32[]{:S(2)}, u32[]{:S(2)}) collective-permute-start(s32[2,8,8192]{2,1,0:T(8,128)S(1)} %get-tuple-element.68), channel_id=1, source_target_pairs={{0,8},{24,16},{8,0},{16,24},{1,9},{25,17},{9,1},{17,25},{2,10},{26... | collective-permute-start | bytes 1572872 | tf_op jit(solution)/shard_map/ppermute | solution.py:674
  38.4 2.7 %collective-permute-done.13.received = s32[2,8,8192]{2,1,0:T(8,128)S(1)} collective-permute-done((s32[2,8,8192]{2,1,0:T(8,128)S(1)}, s32[2,8,8192]{2,1,0:T(8,128)S(1)}, u32[]{:S(2)}, u32[]{:S(2)}) %collective-permute-start.13) | collective-permute-done | bytes 524320 | tf_op jit(solution)/shard_map/ppermute | solution.py:674
  41.1 1.3 far.11
  43.2 9.2 %collective-permute-done.18.received = s32[2,8,8192]{2,1,0:T(8,128)S(1)} collective-permute-done((s32[2,8,8192]{2,1,0:T(8,128)S(1)}, s32[2,8,8192]{2,1,0:T(8,128)S(1)}, u32[]{:S(2)}, u32[]{:S(2)}) %collective-permute-start.18) | collective-permute-done | bytes 524320 | tf_op jit(solution)/shard_map/ppermute | solution.py:674
  52.3 1.3 far.13
  53.6 0.7 collective-permute-start.19
  54.3 7.3 %collective-permute-done.25.received.rest_2_ = s32[2,8,8192]{2,1,0:T(8,128)S(1)} collective-permute-done((s32[2,8,8192]{2,1,0:T(8,128)S(1)}, s32[2,8,8192]{2,1,0:T(8,128)S(1)}, u32[]{:S(2)}, u32[]{:S(2)}) %collective-permute-start.25) | collective-permute-done | bytes 524320 | tf_op jit(solution)/shard_map/ppermute | solution.py:674
  61.6 2.4 %collective-permute-start = (s32[2,8,8192]{2,1,0:T(8,128)S(1)}, s32[2,8,8192]{2,1,0:T(8,128)S(1)}, u32[]{:S(2)}, u32[]{:S(2)}) collective-permute-start(s32[2,8,8192]{2,1,0:T(8,128)S(1)} %get-tuple-element.41), channel_id=1, source_target_pairs={{0,6},{1,7},{2,4},{3,5},{4,2},{5,3},{6,0},{7,1},{8,14},{9,15},{10,... | collective-permute-start | bytes 1572872 | tf_op jit(solution)/shard_map/ppermute | solution.py:667
  64.0 1.3 far.16
  66.1 1.3 near.11
  67.4 1.3 near.13
  68.6 1.4 scale.11
  70.1 4.1 %collective-permute-start.15 = (s32[2,8,8192]{2,1,0:T(8,128)S(1)}, s32[2,8,8192]{2,1,0:T(8,128)S(1)}, u32[]{:S(2)}, u32[]{:S(2)}) collective-permute-start(s32[2,8,8192]{2,1,0:T(8,128)S(1)} %get-tuple-element.57), channel_id=1, source_target_pairs={{0,8},{24,16},{8,0},{16,24},{1,9},{25,17},{9,1},{17,25},{2,10},{26... | collective-permute-start | bytes 1572872 | tf_op jit(solution)/shard_map/ppermute | solution.py:674
  74.1 1.4 scale.13
  75.6 1.3 near.16
  77.3 1.4 scale.15
  78.7 4.1 %collective-permute-start.27 = (s32[2,8,8192]{2,1,0:T(8,128)S(1)}, s32[2,8,8192]{2,1,0:T(8,128)S(1)}, u32[]{:S(2)}, u32[]{:S(2)}) collective-permute-start(s32[2,8,8192]{2,1,0:T(8,128)S(1)} %get-tuple-element.71), channel_id=1, source_target_pairs={{0,8},{24,16},{8,0},{16,24},{1,9},{25,17},{9,1},{17,25},{2,10},{26... | collective-permute-start | bytes 1572872 | tf_op jit(solution)/shard_map/ppermute | solution.py:674
  82.8 1.9 %collective-permute-done.1.rest_1_.rest_0_ = s32[2,8,8192]{2,1,0:T(8,128)S(1)} collective-permute-done((s32[2,8,8192]{2,1,0:T(8,128)S(1)}, s32[2,8,8192]{2,1,0:T(8,128)S(1)}, u32[]{:S(2)}, u32[]{:S(2)}) %collective-permute-start.1) | collective-permute-done | bytes 524320 | tf_op jit(solution)/shard_map/ppermute | solution.py:667
  84.8 1.0 scale.8.own
  85.8 4.4 %collective-permute-start.7 = (s32[2,8,5120]{2,1,0:T(8,128)S(1)}, s32[2,8,5120]{2,1,0:T(8,128)S(1)}, u32[]{:S(2)}, u32[]{:S(2)}) collective-permute-start(s32[2,8,5120]{2,1,0:T(8,128)S(1)} %scale.8.own), channel_id=1, source_target_pairs={{0,8},{24,16},{1,9},{25,17},{2,10},{26,18},{3,11},{27,19},{4,12},{... | collective-permute-start | bytes 983048 | tf_op jit(solution)/shard_map/ppermute | solution.py:674
  90.2 1.3 far.12
  91.5 0.7 collective-permute-start.16
  92.2 6.0 %collective-permute-done.20.received.rest_2_ = s32[2,8,8192]{2,1,0:T(8,128)S(1)} collective-permute-done((s32[2,8,8192]{2,1,0:T(8,128)S(1)}, s32[2,8,8192]{2,1,0:T(8,128)S(1)}, u32[]{:S(2)}, u32[]{:S(2)}) %collective-permute-start.20) | collective-permute-done | bytes 524320 | tf_op jit(solution)/shard_map/ppermute | solution.py:674
  98.1 1.3 far.14
  100.1 9.2 %collective-permute-done.27.received.rest_5_ = s32[2,8,8192]{2,1,0:T(8,128)S(1)} collective-permute-done((s32[2,8,8192]{2,1,0:T(8,128)S(1)}, s32[2,8,8192]{2,1,0:T(8,128)S(1)}, u32[]{:S(2)}, u32[]{:S(2)}) %collective-permute-start.27) | collective-permute-done | bytes 524320 | tf_op jit(solution)/shard_map/ppermute | solution.py:674
  109.2 1.3 far.17
  110.5 0.7 collective-permute-start.28
  111.2 0.8 scale.9.own
  112.0 7.0 %collective-permute-start.10 = (s32[2,8,3072]{2,1,0:T(8,128)S(1)}, s32[2,8,3072]{2,1,0:T(8,128)S(1)}, u32[]{:S(2)}, u32[]{:S(2)}) collective-permute-start(s32[2,8,3072]{2,1,0:T(8,128)S(1)} %scale.9.own), channel_id=1, source_target_pairs={{0,8},{24,16},{1,9},{25,17},{2,10},{26,18},{3,11},{27,19},{4,12},{... | collective-permute-start | bytes 589832 | tf_op jit(solution)/shard_map/ppermute | solution.py:674
  119.1 1.0 far.9
  120.8 1.6 %collective-permute-done.10.received = s32[2,8,3072]{2,1,0:T(8,128)S(1)} collective-permute-done((s32[2,8,3072]{2,1,0:T(8,128)S(1)}, s32[2,8,3072]{2,1,0:T(8,128)S(1)}, u32[]{:S(2)}, u32[]{:S(2)}) %collective-permute-start.10) | collective-permute-done | bytes 196640 | tf_op jit(solution)/shard_map/ppermute | solution.py:674
  123.6 1.3 near.12
  124.9 1.3 near.14
  126.4 1.3 collective-permute-start.17
  127.9 1.3 collective-permute-start.22
  129.2 1.3 near.17
  130.6 1.3 collective-permute-start.29
  131.9 1.0 near.9
  133.1 1.3 collective-permute-start.9
  135.0 1.3 collective-permute-start.12
  136.3 2.0 %spread.4.rest_2_ = f32[4,8,65536]{2,1,0:T(8,128)} custom-call(s32[2]{0:T(128)S(1)} %pad_add_fusion.place, f32[5,4,8,128]{3,2,1,0:T(8,128)S(1)} %get-tuple-element.40.columns, s32[2,8,8192]{2,1,0:T(8,128)S(1)} %get-tuple-element.47.rest_0_, s32[2,8,8192]{2,1,0:T(8,128)S(1)} %collective-permute-done.6.rest_1_.rest_0_), custom_call_target="tpu_custom_call" | custom-call | flops 10485760 | bytes 3145728 | tf_op jit(solution)/shard_map/spread/pallas_call | solution.py:400
  138.3 2.0 %spread.5.rest_2_ = f32[4,8,65536]{2,1,0:T(8,128)} custom-call(s32[2]{0:T(128)S(1)} %pad_add_fusion.place, f32[5,4,8,128]{3,2,1,0:T(8,128)S(1)} %get-tuple-element.40.columns, s32[2,8,8192]{2,1,0:T(8,128)S(1)} %collective-permute-done.4.rest_0_, s32[2,8,8192]{2,1,0:T(8,128)S(1)} %collective-permute-done.5.rest_1_.rest_0_, ...), custom_call_target="tpu_custom_call", output_to_operand_aliasing={{}: (4, {})} | custom-call | flops 10485760 | bytes 3145728 | tf_op jit(solution)/shard_map/spread/pallas_call | solution.py:400
  140.4 2.0 %spread.6.rest_2_ = f32[4,8,65536]{2,1,0:T(8,128)} custom-call(s32[2]{0:T(128)S(1)} %pad_add_fusion.place, f32[5,4,8,128]{3,2,1,0:T(8,128)S(1)} %get-tuple-element.40.columns, s32[2,8,8192]{2,1,0:T(8,128)S(1)} %collective-permute-done.2.rest_0_, s32[2,8,8192]{2,1,0:T(8,128)S(1)} %collective-permute-done.3.rest_1_.rest_0_, ...), custom_call_target="tpu_custom_call", output_to_operand_aliasing={{}: (4, {})} | custom-call | flops 10485760 | bytes 3145728 | tf_op jit(solution)/shard_map/spread/pallas_call | solution.py:400
  142.4 2.0 %spread.7 = f32[4,8,65536]{2,1,0:T(8,128)} custom-call(s32[2]{0:T(128)S(1)} %pad_add_fusion.place, f32[5,4,8,128]{3,2,1,0:T(8,128)S(1)} %get-tuple-element.40.columns, s32[2,8,8192]{2,1,0:T(8,128)S(1)} %collective-permute-done.rest_0_, s32[2,8,8192]{2,1,0:T(8,128)S(1)} %collective-permute-done.1.rest_1_.rest_0_, ...), custom_call_target="tpu_custom_call", output_to_operand_aliasing={{}: (4, {})} | custom-call | flops 10485760 | bytes 3145728 | tf_op jit(solution)/shard_map/spread/pallas_call | solution.py:400
  144.4 1.7 %finish.4.rest_6_ = f32[2,8,65536]{2,1,0:T(8,128)} custom-call(s32[2]{0:T(128)S(1)} %pad_add_fusion.place, f32[2,8,8,128]{3,2,1,0:T(8,128)S(1)} %get-tuple-element.49.targets, s32[1,8,8192]{2,1,0:T(8,128)S(1)} %get-tuple-element.76.rest_0_, s32[2,8,8192]{2,1,0:T(8,128)S(1)} %collective-permute-done.24.rest_2_.rest_1_, ...), custom_call_target="tpu_custom_call" | custom-call | flops 5242880 | bytes 2621440 | tf_op jit(solution)/shard_map/finish/pallas_call | solution.py:551
  146.1 1.7 %finish.5.rest_9_ = f32[2,8,65536]{2,1,0:T(8,128)} custom-call(s32[2]{0:T(128)S(1)} %pad_add_fusion.place, f32[2,8,8,128]{3,2,1,0:T(8,128)S(1)} %get-tuple-element.49.targets, s32[1,8,8192]{2,1,0:T(8,128)S(1)} %get-tuple-element.74.rest_0_, s32[2,8,8192]{2,1,0:T(8,128)S(1)} %collective-permute-done.19.rest_2_.rest_1_, ...), custom_call_target="tpu_custom_call", output_to_operand_aliasing={{}: (8, {})} | custom-call | flops 5242880 | bytes 2621440 | tf_op jit(solution)/shard_map/finish/pallas_call | solution.py:551
  147.9 2.2 %collective-permute-done.29.rest_8_ = s32[1,8,8192]{2,1,0:T(8,128)S(1)} collective-permute-done((s32[1,8,8192]{2,1,0:T(8,128)S(1)}, s32[1,8,8192]{2,1,0:T(8,128)S(1)}, u32[]{:S(2)}, u32[]{:S(2)}) %collective-permute-start.29) | collective-permute-done | bytes 262176 | tf_op jit(solution)/shard_map/ppermute | solution.py:686
  150.0 2.0 %finish.6.rest_6_ = f32[2,8,65536]{2,1,0:T(8,128)} custom-call(s32[2]{0:T(128)S(1)} %pad_add_fusion.place, f32[2,8,8,128]{3,2,1,0:T(8,128)S(1)} %get-tuple-element.49.targets, s32[1,8,8192]{2,1,0:T(8,128)S(1)} %get-tuple-element.58.rest_0_, s32[2,8,8192]{2,1,0:T(8,128)S(1)} %collective-permute-done.16.arrived.rest_1_, ...), custom_call_target="tpu_custom_call", output_to_operand_aliasing={{}: (11, {})} | custom-call | flops 7864320 | bytes 3932160 | tf_op jit(solution)/shard_map/finish/pallas_call | solution.py:551
  152.1 0.8 collective-permute-done.12.rest_5_
  152.9 1.5 finish.7
  (39 shorter events, 6.8 us)
Async XLA Ops:
  3.0 14.5 %collective-permute-start.23 = (s32[2,8,8192]{2,1,0:T(8,128)S(1)}, s32[2,8,8192]{2,1,0:T(8,128)S(1)}, u32[]{:S(2)}, u32[]{:S(2)}) collective-permute-start(s32[2,8,8192]{2,1,0:T(8,128)S(1)} %first.1), channel_id=1, source_target_pairs={{0,8},{24,16},{1,9},{25,17},{2,10},{26,18},{3,11},{27,19},{4,12},{... | collective-permute-start | bytes 1572872 | tf_op jit(solution)/shard_map/ppermute | solution.py:674
  8.9 10.5 %collective-permute-start.6 = (s32[2,8,8192]{2,1,0:T(8,128)S(1)}, s32[2,8,8192]{2,1,0:T(8,128)S(1)}, u32[]{:S(2)}, u32[]{:S(2)}) collective-permute-start(s32[2,8,8192]{2,1,0:T(8,128)S(1)} %get-tuple-element.48), channel_id=1, source_target_pairs={{0,1},{1,0},{2,3},{3,2},{4,5},{5,4},{6,7},{7,6},{8,9},{9,8},{10,11... | collective-permute-start | bytes 1572872 | tf_op jit(solution)/shard_map/ppermute | solution.py:667
  9.0 19.8 %collective-permute-start.4 = (s32[2,8,8192]{2,1,0:T(8,128)S(1)}, s32[2,8,8192]{2,1,0:T(8,128)S(1)}, u32[]{:S(2)}, u32[]{:S(2)}) collective-permute-start(s32[2,8,8192]{2,1,0:T(8,128)S(1)} %get-tuple-element.45), channel_id=1, source_target_pairs={{0,2},{1,3},{2,0},{3,1},{4,6},{5,7},{6,4},{7,5},{8,10},{9,11},{10,... | collective-permute-start | bytes 1572872 | tf_op jit(solution)/shard_map/ppermute | solution.py:667
  10.6 22.2 %collective-permute-start.5 = (s32[2,8,8192]{2,1,0:T(8,128)S(1)}, s32[2,8,8192]{2,1,0:T(8,128)S(1)}, u32[]{:S(2)}, u32[]{:S(2)}) collective-permute-start(s32[2,8,8192]{2,1,0:T(8,128)S(1)} %get-tuple-element.46), channel_id=1, source_target_pairs={{0,4},{1,5},{2,6},{3,7},{4,0},{5,1},{6,2},{7,3},{8,12},{9,13},{10,... | collective-permute-start | bytes 1572872 | tf_op jit(solution)/shard_map/ppermute | solution.py:667
  18.8 14.0 %collective-permute-start.24 = (s32[2,8,8192]{2,1,0:T(8,128)S(1)}, s32[2,8,8192]{2,1,0:T(8,128)S(1)}, u32[]{:S(2)}, u32[]{:S(2)}) collective-permute-start(s32[2,8,8192]{2,1,0:T(8,128)S(1)} %far.15), channel_id=1, source_target_pairs={{8,16},{16,8},{9,17},{17,9},{10,18},{18,10},{11,19},{19,11},{12,20... | collective-permute-start | bytes 1572872 | tf_op jit(solution)/shard_map/ppermute | solution.py:682
  20.8 20.3 %collective-permute-start.13 = (s32[2,8,8192]{2,1,0:T(8,128)S(1)}, s32[2,8,8192]{2,1,0:T(8,128)S(1)}, u32[]{:S(2)}, u32[]{:S(2)}) collective-permute-start(s32[2,8,8192]{2,1,0:T(8,128)S(1)} %scale.10.own), channel_id=1, source_target_pairs={{0,8},{24,16},{1,9},{25,17},{2,10},{26,18},{3,11},{27,19},{4,12},{... | collective-permute-start | bytes 1572872 | tf_op jit(solution)/shard_map/ppermute | solution.py:674
  30.2 22.2 %collective-permute-start.18 = (s32[2,8,8192]{2,1,0:T(8,128)S(1)}, s32[2,8,8192]{2,1,0:T(8,128)S(1)}, u32[]{:S(2)}, u32[]{:S(2)}) collective-permute-start(s32[2,8,8192]{2,1,0:T(8,128)S(1)} %scale.12.own), channel_id=1, source_target_pairs={{0,8},{24,16},{1,9},{25,17},{2,10},{26,18},{3,11},{27,19},{4,12},{... | collective-permute-start | bytes 1572872 | tf_op jit(solution)/shard_map/ppermute | solution.py:674
  34.2 27.4 %collective-permute-start.25 = (s32[2,8,8192]{2,1,0:T(8,128)S(1)}, s32[2,8,8192]{2,1,0:T(8,128)S(1)}, u32[]{:S(2)}, u32[]{:S(2)}) collective-permute-start(s32[2,8,8192]{2,1,0:T(8,128)S(1)} %get-tuple-element.68), channel_id=1, source_target_pairs={{0,8},{24,16},{8,0},{16,24},{1,9},{25,17},{9,1},{17,25},{2,10},{26... | collective-permute-start | bytes 1572872 | tf_op jit(solution)/shard_map/ppermute | solution.py:674
  38.4 26.9 %collective-permute-start.2 = (s32[2,8,8192]{2,1,0:T(8,128)S(1)}, s32[2,8,8192]{2,1,0:T(8,128)S(1)}, u32[]{:S(2)}, u32[]{:S(2)}) collective-permute-start(s32[2,8,8192]{2,1,0:T(8,128)S(1)} %get-tuple-element.43), channel_id=1, source_target_pairs={{0,3},{1,2},{2,1},{3,0},{4,7},{5,6},{6,5},{7,4},{8,11},{9,10},{10,... | collective-permute-start | bytes 1572872 | tf_op jit(solution)/shard_map/ppermute | solution.py:667
  42.4 23.6 %collective-permute-start.14 = (s32[2,8,8192]{2,1,0:T(8,128)S(1)}, s32[2,8,8192]{2,1,0:T(8,128)S(1)}, u32[]{:S(2)}, u32[]{:S(2)}) collective-permute-start(s32[2,8,8192]{2,1,0:T(8,128)S(1)} %far.11), channel_id=1, source_target_pairs={{8,16},{16,8},{9,17},{17,9},{10,18},{18,10},{11,19},{19,11},{12,20... | collective-permute-start | bytes 1572872 | tf_op jit(solution)/shard_map/ppermute | solution.py:682
  43.1 27.0 %collective-permute-start.3 = (s32[2,8,8192]{2,1,0:T(8,128)S(1)}, s32[2,8,8192]{2,1,0:T(8,128)S(1)}, u32[]{:S(2)}, u32[]{:S(2)}) collective-permute-start(s32[2,8,8192]{2,1,0:T(8,128)S(1)} %get-tuple-element.44), channel_id=1, source_target_pairs={{0,5},{1,4},{2,7},{3,6},{4,1},{5,0},{6,3},{7,2},{8,13},{9,12},{10,... | collective-permute-start | bytes 1572872 | tf_op jit(solution)/shard_map/ppermute | solution.py:667
  53.6 20.5 %collective-permute-start.19 = (s32[2,8,8192]{2,1,0:T(8,128)S(1)}, s32[2,8,8192]{2,1,0:T(8,128)S(1)}, u32[]{:S(2)}, u32[]{:S(2)}) collective-permute-start(s32[2,8,8192]{2,1,0:T(8,128)S(1)} %far.13), channel_id=1, source_target_pairs={{8,16},{16,8},{9,17},{17,9},{10,18},{18,10},{11,19},{19,11},{12,20... | collective-permute-start | bytes 1572872 | tf_op jit(solution)/shard_map/ppermute | solution.py:682
  61.6 15.7 %collective-permute-start = (s32[2,8,8192]{2,1,0:T(8,128)S(1)}, s32[2,8,8192]{2,1,0:T(8,128)S(1)}, u32[]{:S(2)}, u32[]{:S(2)}) collective-permute-start(s32[2,8,8192]{2,1,0:T(8,128)S(1)} %get-tuple-element.41), channel_id=1, source_target_pairs={{0,6},{1,7},{2,4},{3,5},{4,2},{5,3},{6,0},{7,1},{8,14},{9,15},{10,... | collective-permute-start | bytes 1572872 | tf_op jit(solution)/shard_map/ppermute | solution.py:667
  65.3 12.0 %collective-permute-start.26 = (s32[2,8,8192]{2,1,0:T(8,128)S(1)}, s32[2,8,8192]{2,1,0:T(8,128)S(1)}, u32[]{:S(2)}, u32[]{:S(2)}) collective-permute-start(s32[2,8,8192]{2,1,0:T(8,128)S(1)} %far.16), channel_id=1, source_target_pairs={{8,16},{16,8},{9,17},{17,9},{10,18},{18,10},{11,19},{19,11},{12,20... | collective-permute-start | bytes 1572872 | tf_op jit(solution)/shard_map/ppermute | solution.py:682
  66.0 18.7 %collective-permute-start.1 = (s32[2,8,8192]{2,1,0:T(8,128)S(1)}, s32[2,8,8192]{2,1,0:T(8,128)S(1)}, u32[]{:S(2)}, u32[]{:S(2)}) collective-permute-start(s32[2,8,8192]{2,1,0:T(8,128)S(1)} %get-tuple-element.42), channel_id=1, source_target_pairs={{0,7},{1,6},{2,5},{3,4},{4,3},{5,2},{6,1},{7,0},{8,15},{9,14},{10,... | collective-permute-start | bytes 1572872 | tf_op jit(solution)/shard_map/ppermute | solution.py:667
  70.1 20.1 %collective-permute-start.15 = (s32[2,8,8192]{2,1,0:T(8,128)S(1)}, s32[2,8,8192]{2,1,0:T(8,128)S(1)}, u32[]{:S(2)}, u32[]{:S(2)}) collective-permute-start(s32[2,8,8192]{2,1,0:T(8,128)S(1)} %get-tuple-element.57), channel_id=1, source_target_pairs={{0,8},{24,16},{8,0},{16,24},{1,9},{25,17},{9,1},{17,25},{2,10},{26... | collective-permute-start | bytes 1572872 | tf_op jit(solution)/shard_map/ppermute | solution.py:674
  75.5 22.6 %collective-permute-start.20 = (s32[2,8,8192]{2,1,0:T(8,128)S(1)}, s32[2,8,8192]{2,1,0:T(8,128)S(1)}, u32[]{:S(2)}, u32[]{:S(2)}) collective-permute-start(s32[2,8,8192]{2,1,0:T(8,128)S(1)} %get-tuple-element.62), channel_id=1, source_target_pairs={{0,8},{24,16},{8,0},{16,24},{1,9},{25,17},{9,1},{17,25},{2,10},{26... | collective-permute-start | bytes 1572872 | tf_op jit(solution)/shard_map/ppermute | solution.py:674
  78.7 30.5 %collective-permute-start.27 = (s32[2,8,8192]{2,1,0:T(8,128)S(1)}, s32[2,8,8192]{2,1,0:T(8,128)S(1)}, u32[]{:S(2)}, u32[]{:S(2)}) collective-permute-start(s32[2,8,8192]{2,1,0:T(8,128)S(1)} %get-tuple-element.71), channel_id=1, source_target_pairs={{0,8},{24,16},{8,0},{16,24},{1,9},{25,17},{9,1},{17,25},{2,10},{26... | collective-permute-start | bytes 1572872 | tf_op jit(solution)/shard_map/ppermute | solution.py:674
  85.8 33.3 %collective-permute-start.7 = (s32[2,8,5120]{2,1,0:T(8,128)S(1)}, s32[2,8,5120]{2,1,0:T(8,128)S(1)}, u32[]{:S(2)}, u32[]{:S(2)}) collective-permute-start(s32[2,8,5120]{2,1,0:T(8,128)S(1)} %scale.8.own), channel_id=1, source_target_pairs={{0,8},{24,16},{1,9},{25,17},{2,10},{26,18},{3,11},{27,19},{4,12},{... | collective-permute-start | bytes 983048 | tf_op jit(solution)/shard_map/ppermute | solution.py:674
  91.5 34.7 %collective-permute-start.16 = (s32[2,8,8192]{2,1,0:T(8,128)S(1)}, s32[2,8,8192]{2,1,0:T(8,128)S(1)}, u32[]{:S(2)}, u32[]{:S(2)}) collective-permute-start(s32[2,8,8192]{2,1,0:T(8,128)S(1)} %far.12), channel_id=1, source_target_pairs={{8,16},{16,8},{9,17},{17,9},{10,18},{18,10},{11,19},{19,11},{12,20... | collective-permute-start | bytes 1572872 | tf_op jit(solution)/shard_map/ppermute | solution.py:682
  99.4 28.3 %collective-permute-start.21 = (s32[2,8,8192]{2,1,0:T(8,128)S(1)}, s32[2,8,8192]{2,1,0:T(8,128)S(1)}, u32[]{:S(2)}, u32[]{:S(2)}) collective-permute-start(s32[2,8,8192]{2,1,0:T(8,128)S(1)} %far.14), channel_id=1, source_target_pairs={{8,16},{16,8},{9,17},{17,9},{10,18},{18,10},{11,19},{19,11},{12,20... | collective-permute-start | bytes 1572872 | tf_op jit(solution)/shard_map/ppermute | solution.py:682
  110.5 19.9 %collective-permute-start.28 = (s32[2,8,8192]{2,1,0:T(8,128)S(1)}, s32[2,8,8192]{2,1,0:T(8,128)S(1)}, u32[]{:S(2)}, u32[]{:S(2)}) collective-permute-start(s32[2,8,8192]{2,1,0:T(8,128)S(1)} %far.17), channel_id=1, source_target_pairs={{8,16},{16,8},{9,17},{17,9},{10,18},{18,10},{11,19},{19,11},{12,20... | collective-permute-start | bytes 1572872 | tf_op jit(solution)/shard_map/ppermute | solution.py:682
  112.0 10.4 %collective-permute-start.10 = (s32[2,8,3072]{2,1,0:T(8,128)S(1)}, s32[2,8,3072]{2,1,0:T(8,128)S(1)}, u32[]{:S(2)}, u32[]{:S(2)}) collective-permute-start(s32[2,8,3072]{2,1,0:T(8,128)S(1)} %scale.9.own), channel_id=1, source_target_pairs={{0,8},{24,16},{1,9},{25,17},{2,10},{26,18},{3,11},{27,19},{4,12},{... | collective-permute-start | bytes 589832 | tf_op jit(solution)/shard_map/ppermute | solution.py:674
  120.1 12.9 %collective-permute-start.8 = (s32[2,8,5120]{2,1,0:T(8,128)S(1)}, s32[2,8,5120]{2,1,0:T(8,128)S(1)}, u32[]{:S(2)}, u32[]{:S(2)}) collective-permute-start(s32[2,8,5120]{2,1,0:T(8,128)S(1)} %far.9), channel_id=1, source_target_pairs={{8,16},{16,8},{9,17},{17,9},{10,18},{18,10},{11,19},{19,11},{12,20... | collective-permute-start | bytes 983048 | tf_op jit(solution)/shard_map/ppermute | solution.py:682
  122.9 12.0 %collective-permute-start.11 = (s32[2,8,3072]{2,1,0:T(8,128)S(1)}, s32[2,8,3072]{2,1,0:T(8,128)S(1)}, u32[]{:S(2)}, u32[]{:S(2)}) collective-permute-start(s32[2,8,3072]{2,1,0:T(8,128)S(1)} %far.10), channel_id=1, source_target_pairs={{8,16},{16,8},{9,17},{17,9},{10,18},{18,10},{11,19},{19,11},{12,20... | collective-permute-start | bytes 589832 | tf_op jit(solution)/shard_map/ppermute | solution.py:682
  126.4 21.5 %collective-permute-start.17 = (s32[1,8,8192]{2,1,0:T(8,128)S(1)}, s32[1,8,8192]{2,1,0:T(8,128)S(1)}, u32[]{:S(2)}, u32[]{:S(2)}) collective-permute-start(s32[1,8,8192]{2,1,0:T(8,128)S(1)} %forward.7), channel_id=1, source_target_pairs={{8,0},{16,24},{9,1},{17,25},{10,2},{18,26},{11,3},{19,27},{12,4},{... | collective-permute-start | bytes 786440 | tf_op jit(solution)/shard_map/ppermute | solution.py:686
  127.9 20.0 %collective-permute-start.22 = (s32[1,8,8192]{2,1,0:T(8,128)S(1)}, s32[1,8,8192]{2,1,0:T(8,128)S(1)}, u32[]{:S(2)}, u32[]{:S(2)}) collective-permute-start(s32[1,8,8192]{2,1,0:T(8,128)S(1)} %forward.8), channel_id=1, source_target_pairs={{8,0},{16,24},{9,1},{17,25},{10,2},{18,26},{11,3},{19,27},{12,4},{... | collective-permute-start | bytes 786440 | tf_op jit(solution)/shard_map/ppermute | solution.py:686
  130.6 19.4 %collective-permute-start.29 = (s32[1,8,8192]{2,1,0:T(8,128)S(1)}, s32[1,8,8192]{2,1,0:T(8,128)S(1)}, u32[]{:S(2)}, u32[]{:S(2)}) collective-permute-start(s32[1,8,8192]{2,1,0:T(8,128)S(1)} %forward.9), channel_id=1, source_target_pairs={{8,0},{16,24},{9,1},{17,25},{10,2},{18,26},{11,3},{19,27},{12,4},{... | collective-permute-start | bytes 786440 | tf_op jit(solution)/shard_map/ppermute | solution.py:686
  133.1 19.8 %collective-permute-start.9 = (s32[1,8,5120]{2,1,0:T(8,128)S(1)}, s32[1,8,5120]{2,1,0:T(8,128)S(1)}, u32[]{:S(2)}, u32[]{:S(2)}) collective-permute-start(s32[1,8,5120]{2,1,0:T(8,128)S(1)} %forward.5), channel_id=1, source_target_pairs={{8,0},{16,24},{9,1},{17,25},{10,2},{18,26},{11,3},{19,27},{12,4},{... | collective-permute-start | bytes 491528 | tf_op jit(solution)/shard_map/ppermute | solution.py:686
  135.0 17.9 %collective-permute-start.12 = (s32[1,8,3072]{2,1,0:T(8,128)S(1)}, s32[1,8,3072]{2,1,0:T(8,128)S(1)}, u32[]{:S(2)}, u32[]{:S(2)}) collective-permute-start(s32[1,8,3072]{2,1,0:T(8,128)S(1)} %forward.6), channel_id=1, source_target_pairs={{8,0},{16,24},{9,1},{17,25},{10,2},{18,26},{11,3},{19,27},{12,4},{... | collective-permute-start | bytes 294920 | tf_op jit(solution)/shard_map/ppermute | solution.py:686
